TPU v7x, 8 devices: a whole 2x2x1 slice. The times are simulated.
8 devices in a mesh: dp: 1 (over z), tp: 2 (over y), pp: 4 (over x, core).
Axes of the slice: x: 2, y: 2, z: 1, core: 2. Of those that a mesh axis runs over, the one named last changes fastest.
Arguments:
- x_in: bfloat16 [2, 12, 256, 1536], P(None, 'dp')
- dy_out: bfloat16 [2, 12, 256, 1536], P(None, 'dp')
- w_qkv: bfloat16 [4, 3, 1536, 16, 96], P('pp', None, None, 'tp')
- b_qkv: bfloat16 [4, 3, 16, 96], P('pp', None, 'tp')
- w_out: bfloat16 [4, 16, 96, 1536], P('pp', 'tp')
- b_out: bfloat16 [4, 1536], P('pp')
- ln_par: bfloat16 [4, 4, 1536], P('pp')
- w_fc1: bfloat16 [4, 1536, 6144], P('pp', None, 'tp')
- b_fc1: bfloat16 [4, 6144], P('pp', 'tp')
- w_fc2: bfloat16 [4, 6144, 1536], P('pp', 'tp')
- b_fc2: bfloat16 [4, 1536], P('pp')
Outputs:
- output 1: bfloat16 [4, 2, 12, 256, 1536], P('pp', None, 'dp')
- output 2: bfloat16 [4, 2, 12, 256, 1536], P('pp', None, 'dp')
- output 3: float32 [4, 3, 1536, 16, 96], P(('dp', 'pp'), None, None, 'tp')
- output 4: float32 [4, 3, 16, 96], P(('dp', 'pp'), None, 'tp')
- output 5: float32 [4, 16, 96, 1536], P(('dp', 'pp'), 'tp')
- output 6: float32 [4, 1536], P(('dp', 'pp'))
- output 7: float32 [4, 4, 1536], P(('dp', 'pp'))
- output 8: float32 [4, 1536, 6144], P(('dp', 'pp'), None, 'tp')
- output 9: float32 [4, 6144], P(('dp', 'pp'), 'tp')
- output 10: float32 [4, 6144, 1536], P(('dp', 'pp'), 'tp')
- output 11: float32 [4, 1536], P(('dp', 'pp'))
All inputs are finite; a program needn't handle non-finite values.
Results may differ from a plain program's by a relative error of at most 0.02.
Values are sent between devices in bfloat16 or wider.
A program may use at most 1 GiB of HBM per device.

v0:
```python
import jax
import jax.numpy as jnp
from jax import lax
from jax.sharding import PartitionSpec as P

LN_EPS = 1e-5


def layer_norm(x_act, ln_gain, ln_shift):
    x_wide = x_act.astype(jnp.float32)
    row_mean = jnp.mean(x_wide, axis=-1, keepdims=True)
    centered = x_wide - row_mean
    row_var = jnp.mean(centered * centered, axis=-1, keepdims=True)
    normed = centered * lax.rsqrt(row_var + LN_EPS)
    return (normed * ln_gain + ln_shift).astype(jnp.bfloat16)


def causal_attention(q_heads, k_heads, v_heads):
    head_dim = q_heads.shape[-1]
    seq_len = q_heads.shape[1]
    scores = jnp.einsum("bqhe,bkhe->bhqk", q_heads, k_heads, preferred_element_type=jnp.float32) * (head_dim ** -0.5)
    row_pos = lax.broadcasted_iota(jnp.int32, (seq_len, seq_len), 0)
    col_pos = lax.broadcasted_iota(jnp.int32, (seq_len, seq_len), 1)
    scores = jnp.where(row_pos >= col_pos, scores, -1e30)
    attn_probs = jax.nn.softmax(scores, axis=-1).astype(jnp.bfloat16)
    attn_mix = jnp.einsum("bhqk,bkhe->bqhe", attn_probs, v_heads, preferred_element_type=jnp.float32)
    return attn_mix.astype(jnp.bfloat16)


def gelu_tanh(pre_act):
    return jax.nn.gelu(pre_act, approximate=True)


def layer_forward(x_act, layer_w):
    w_qkv, b_qkv, w_out, b_out, ln_par, w_fc1, b_fc1, w_fc2, b_fc2 = layer_w
    ln_wide = ln_par.astype(jnp.float32)
    h_one = layer_norm(x_act, ln_wide[0], ln_wide[1])
    qkv_all = (jnp.einsum("bsd,cdhe->bsche", h_one, w_qkv, preferred_element_type=jnp.float32) + b_qkv.astype(jnp.float32)).astype(jnp.bfloat16)
    attn_mix = causal_attention(qkv_all[:, :, 0], qkv_all[:, :, 1], qkv_all[:, :, 2])
    attn_part = jnp.einsum("bshe,hed->bsd", attn_mix, w_out, preferred_element_type=jnp.float32).astype(jnp.bfloat16)
    attn_sum = lax.psum(attn_part, "tp")
    x_mid = (x_act.astype(jnp.float32) + attn_sum.astype(jnp.float32) + b_out.astype(jnp.float32)).astype(jnp.bfloat16)
    h_two = layer_norm(x_mid, ln_wide[2], ln_wide[3])
    pre_act = jnp.einsum("bsd,df->bsf", h_two, w_fc1, preferred_element_type=jnp.float32) + b_fc1.astype(jnp.float32)
    gelu_out = gelu_tanh(pre_act).astype(jnp.bfloat16)
    mlp_part = jnp.einsum("bsf,fd->bsd", gelu_out, w_fc2, preferred_element_type=jnp.float32).astype(jnp.bfloat16)
    mlp_sum = lax.psum(mlp_part, "tp")
    y_act = (x_mid.astype(jnp.float32) + mlp_sum.astype(jnp.float32) + b_fc2.astype(jnp.float32)).astype(jnp.bfloat16)
    return y_act, qkv_all, x_mid, pre_act


def layer_backward(grad_out, x_act, qkv_all, x_mid, pre_act, layer_w):
    w_qkv = layer_w[0]
    w_out = layer_w[2]
    ln_wide = layer_w[4].astype(jnp.float32)
    w_fc1 = layer_w[5]
    w_fc2 = layer_w[7]
    grad_wide = grad_out.astype(jnp.float32)
    g_b_fc2 = jnp.sum(grad_wide, axis=(0, 1))
    gelu_wide, gelu_pull = jax.vjp(gelu_tanh, pre_act)
    gelu_out = gelu_wide.astype(jnp.bfloat16)
    g_w_fc2 = jnp.einsum("bsf,bsd->fd", gelu_out, grad_out, preferred_element_type=jnp.float32)
    g_gelu = jnp.einsum("bsd,fd->bsf", grad_out, w_fc2, preferred_element_type=jnp.float32).astype(jnp.bfloat16)
    g_pre = gelu_pull(g_gelu.astype(jnp.float32))[0]
    g_b_fc1 = jnp.sum(g_pre, axis=(0, 1))
    g_pre_half = g_pre.astype(jnp.bfloat16)
    h_two, ln_two_pull = jax.vjp(layer_norm, x_mid, ln_wide[2], ln_wide[3])
    g_w_fc1 = jnp.einsum("bsd,bsf->df", h_two, g_pre_half, preferred_element_type=jnp.float32)
    g_h_two = lax.psum(jnp.einsum("bsf,df->bsd", g_pre_half, w_fc1, preferred_element_type=jnp.float32).astype(jnp.bfloat16), "tp")
    g_mid_ln, g_gain_two, g_shift_two = ln_two_pull(g_h_two)
    g_mid_wide = grad_wide + g_mid_ln.astype(jnp.float32)
    g_mid = g_mid_wide.astype(jnp.bfloat16)
    g_b_out = jnp.sum(g_mid_wide, axis=(0, 1))
    attn_mix, attn_pull = jax.vjp(causal_attention, qkv_all[:, :, 0], qkv_all[:, :, 1], qkv_all[:, :, 2])
    g_w_out = jnp.einsum("bshe,bsd->hed", attn_mix, g_mid, preferred_element_type=jnp.float32)
    g_mix = jnp.einsum("bsd,hed->bshe", g_mid, w_out, preferred_element_type=jnp.float32).astype(jnp.bfloat16)
    g_query, g_key, g_value = attn_pull(g_mix)
    g_qkv = jnp.stack([g_query, g_key, g_value], axis=2)
    g_b_qkv = jnp.sum(g_qkv.astype(jnp.float32), axis=(0, 1))
    h_one, ln_one_pull = jax.vjp(layer_norm, x_act, ln_wide[0], ln_wide[1])
    g_w_qkv = jnp.einsum("bsd,bsche->cdhe", h_one, g_qkv, preferred_element_type=jnp.float32)
    g_h_one = lax.psum(jnp.einsum("bsche,cdhe->bsd", g_qkv, w_qkv, preferred_element_type=jnp.float32).astype(jnp.bfloat16), "tp")
    g_in_ln, g_gain_one, g_shift_one = ln_one_pull(g_h_one)
    grad_in = (g_mid_wide + g_in_ln.astype(jnp.float32)).astype(jnp.bfloat16)
    g_ln = jnp.stack([g_gain_one, g_shift_one, g_gain_two, g_shift_two])
    return grad_in, (g_w_qkv, g_b_qkv, g_w_out, g_b_out, g_ln, g_w_fc1, g_b_fc1, g_w_fc2, g_b_fc2)


def solution(mesh):
    stages = mesh.shape["pp"]
    tp_size = mesh.shape["tp"]
    fwd_pairs = [(src_idx, src_idx + 1) for src_idx in range(stages - 1)]
    back_pairs = [(src_idx + 1, src_idx) for src_idx in range(stages - 1)]

    def pass_on(boundary, stage_pairs):
        seq_part = boundary.shape[1] // tp_size
        own_part = lax.dynamic_slice_in_dim(boundary, lax.axis_index("tp") * seq_part, seq_part, axis=1)
        moved_part = lax.ppermute(own_part, "pp", stage_pairs)
        return lax.all_gather(moved_part, "tp", axis=1, tiled=True)

    def stage_program(x_in, dy_out, w_qkv, b_qkv, w_out, b_out, ln_par, w_fc1, b_fc1, w_fc2, b_fc2):
        layer_w = (w_qkv[0], b_qkv[0], w_out[0], b_out[0], ln_par[0], w_fc1[0], b_fc1[0], w_fc2[0], b_fc2[0])
        micro_count, batch_rows, seq_len, d_model = x_in.shape
        local_heads = w_qkv.shape[3]
        head_dim = w_qkv.shape[4]
        ff_local = w_fc1.shape[2]
        stage_idx = lax.axis_index("pp")
        last_stage = stages - 1
        step_count = micro_count + stages - 1
        act_shape = (batch_rows, seq_len, d_model)
        buf_len = micro_count + 1

        def fwd_step(fwd_carry, step_idx):
            received, x_buf, qkv_buf, mid_buf, pre_buf, out_buf = fwd_carry
            micro_idx = step_idx - stage_idx
            is_valid = (micro_idx >= 0) & (micro_idx < micro_count)
            read_idx = jnp.clip(micro_idx, 0, micro_count - 1)
            write_idx = jnp.where(is_valid, micro_idx, micro_count)
            x_first = lax.dynamic_index_in_dim(x_in, read_idx, 0, keepdims=False)
            x_act = jnp.where(stage_idx == 0, x_first, received)
            y_act, qkv_all, x_mid, pre_act = layer_forward(x_act, layer_w)
            x_buf = lax.dynamic_update_index_in_dim(x_buf, x_act, write_idx, 0)
            qkv_buf = lax.dynamic_update_index_in_dim(qkv_buf, qkv_all, write_idx, 0)
            mid_buf = lax.dynamic_update_index_in_dim(mid_buf, x_mid, write_idx, 0)
            pre_buf = lax.dynamic_update_index_in_dim(pre_buf, pre_act, write_idx, 0)
            out_buf = lax.dynamic_update_index_in_dim(out_buf, y_act, write_idx, 0)
            received = pass_on(y_act, fwd_pairs)
            return (received, x_buf, qkv_buf, mid_buf, pre_buf, out_buf), None

        fwd_init = (jnp.zeros(act_shape, jnp.bfloat16),
                    jnp.zeros((buf_len,) + act_shape, jnp.bfloat16),
                    jnp.zeros((buf_len, batch_rows, seq_len, 3, local_heads, head_dim), jnp.bfloat16),
                    jnp.zeros((buf_len,) + act_shape, jnp.bfloat16),
                    jnp.zeros((buf_len, batch_rows, seq_len, ff_local), jnp.float32),
                    jnp.zeros((buf_len,) + act_shape, jnp.bfloat16))
        fwd_final, _ = lax.scan(fwd_step, fwd_init, jnp.arange(step_count))
        _, x_buf, qkv_buf, mid_buf, pre_buf, out_buf = fwd_final

        def bwd_step(bwd_carry, step_idx):
            received, grad_acc, grad_buf = bwd_carry
            micro_idx = micro_count + last_stage - 1 - stage_idx - step_idx
            is_valid = (micro_idx >= 0) & (micro_idx < micro_count)
            read_idx = jnp.clip(micro_idx, 0, micro_count - 1)
            write_idx = jnp.where(is_valid, micro_idx, micro_count)
            dy_last = lax.dynamic_index_in_dim(dy_out, read_idx, 0, keepdims=False)
            grad_out = jnp.where(stage_idx == last_stage, dy_last, received)
            grad_out = jnp.where(is_valid, grad_out, jnp.zeros_like(grad_out))
            x_act = lax.dynamic_index_in_dim(x_buf, read_idx, 0, keepdims=False)
            qkv_all = lax.dynamic_index_in_dim(qkv_buf, read_idx, 0, keepdims=False)
            x_mid = lax.dynamic_index_in_dim(mid_buf, read_idx, 0, keepdims=False)
            pre_act = lax.dynamic_index_in_dim(pre_buf, read_idx, 0, keepdims=False)
            grad_in, layer_grads = layer_backward(grad_out, x_act, qkv_all, x_mid, pre_act, layer_w)
            grad_acc = tuple(acc_item + new_item for acc_item, new_item in zip(grad_acc, layer_grads))
            grad_buf = lax.dynamic_update_index_in_dim(grad_buf, grad_in, write_idx, 0)
            received = pass_on(grad_in, back_pairs)
            return (received, grad_acc, grad_buf), None

        grad_init = tuple(jnp.zeros(w_item.shape, jnp.float32) for w_item in layer_w)
        bwd_init = (jnp.zeros(act_shape, jnp.bfloat16), grad_init, jnp.zeros((buf_len,) + act_shape, jnp.bfloat16))
        bwd_final, _ = lax.scan(bwd_step, bwd_init, jnp.arange(step_count))
        _, grad_sum, grad_buf = bwd_final
        return (out_buf[:micro_count][None], grad_buf[:micro_count][None]) + tuple(g_item[None] for g_item in grad_sum)

    act_spec = P(None, "dp", None, None)
    arg_specs = (act_spec, act_spec,
                 P("pp", None, None, "tp", None), P("pp", None, "tp", None), P("pp", "tp", None, None),
                 P("pp", None), P("pp", None, None), P("pp", None, "tp"), P("pp", "tp"),
                 P("pp", "tp", None), P("pp", None))
    stage_spec = P("pp", None, "dp", None, None)
    grad_axes = ("dp", "pp")
    result_specs = (stage_spec, stage_spec,
                    P(grad_axes, None, None, "tp", None), P(grad_axes, None, "tp", None), P(grad_axes, "tp", None, None),
                    P(grad_axes, None), P(grad_axes, None, None), P(grad_axes, None, "tp"), P(grad_axes, "tp"),
                    P(grad_axes, "tp", None), P(grad_axes, None))
    return jax.shard_map(stage_program, mesh=mesh, in_specs=arg_specs, out_specs=result_specs, check_vma=False)
```

profile of v0, /device:TPU:0, one launch (start us, length us, event | category | flops | bytes accessed | tf_op | source)
XLA Modules:
  0.0 8815.9 jit_solution(3209535024797656508)
XLA Ops:
  91.6 4156.8 %while.54 = (s32[]{:T(128)}, bf16[12,256,1536]{2,1,0:T(8,128)(2,1)}, bf16[3,12,256,1536]{3,2,1,0:T(8,128)(2,1)}, bf16[3,12,256,3,8,96]{2,5,4,3,1,0:T(8,128)(2,1)...) while((s32[]{:T(128)}, ...), condition=%wide.region_9.10_spmd, body=%wide.region_0.9_spmd.sunk | while | flops 89743777792 | bytes 743302912 | solution.py:136
  207.3 219.6 %all-reduce.5.cloned.1.call-done = bf16[12,256,1536]{2,1,0:T(8,128)(2,1)} async-done(((bf16[12,256,1536]{2,1,0:T(8,128)(2,1)}), bf16[12,256,1536]{2,1,0:T(8,128)(2,1)}) %all-reduce.5.cloned.1.call-update) | async-done | bytes 9437200 | tf_op jit(solution)/shard_map/while/body/eval_jaxpr/psum | solution.py:41
  527.1 215.0 %all-reduce.7.cloned.1.call-done = bf16[12,256,1536]{2,1,0:T(8,128)(2,1)} async-done(((bf16[12,256,1536]{2,1,0:T(8,128)(2,1)}), bf16[12,256,1536]{2,1,0:T(8,128)(2,1)}) %all-reduce.7.cloned.1.call-update) | async-done | bytes 9437200 | tf_op jit(solution)/shard_map/while/body/eval_jaxpr/psum | solution.py:47
  762.9 162.2 %all-gather.3.cloned.1.call-done = bf16[12,256,1536]{2,1,0:T(8,128)(2,1)} async-done(((bf16[12,128,1536]{2,1,0:T(8,128)(2,1)}), bf16[12,256,1536]{2,1,0:T(8,128)(2,1)}) %all-gather.3.cloned.1.call-update) | async-done | bytes 9437200 | tf_op jit(solution)/shard_map/while/body/eval_jaxpr/all_gather | solution.py:99
  1040.4 216.8 %all-reduce.5.cloned.1.call-done = bf16[12,256,1536]{2,1,0:T(8,128)(2,1)} async-done(((bf16[12,256,1536]{2,1,0:T(8,128)(2,1)}), bf16[12,256,1536]{2,1,0:T(8,128)(2,1)}) %all-reduce.5.cloned.1.call-update) | async-done | bytes 9437200 | tf_op jit(solution)/shard_map/while/body/eval_jaxpr/psum | solution.py:41
  1357.7 214.9 %all-reduce.7.cloned.1.call-done = bf16[12,256,1536]{2,1,0:T(8,128)(2,1)} async-done(((bf16[12,256,1536]{2,1,0:T(8,128)(2,1)}), bf16[12,256,1536]{2,1,0:T(8,128)(2,1)}) %all-reduce.7.cloned.1.call-update) | async-done | bytes 9437200 | tf_op jit(solution)/shard_map/while/body/eval_jaxpr/psum | solution.py:47
  1593.4 162.3 %all-gather.3.cloned.1.call-done = bf16[12,256,1536]{2,1,0:T(8,128)(2,1)} async-done(((bf16[12,128,1536]{2,1,0:T(8,128)(2,1)}), bf16[12,256,1536]{2,1,0:T(8,128)(2,1)}) %all-gather.3.cloned.1.call-update) | async-done | bytes 9437200 | tf_op jit(solution)/shard_map/while/body/eval_jaxpr/all_gather | solution.py:99
  1870.7 217.0 %all-reduce.5.cloned.1.call-done = bf16[12,256,1536]{2,1,0:T(8,128)(2,1)} async-done(((bf16[12,256,1536]{2,1,0:T(8,128)(2,1)}), bf16[12,256,1536]{2,1,0:T(8,128)(2,1)}) %all-reduce.5.cloned.1.call-update) | async-done | bytes 9437200 | tf_op jit(solution)/shard_map/while/body/eval_jaxpr/psum | solution.py:41
  2188.2 214.7 %all-reduce.7.cloned.1.call-done = bf16[12,256,1536]{2,1,0:T(8,128)(2,1)} async-done(((bf16[12,256,1536]{2,1,0:T(8,128)(2,1)}), bf16[12,256,1536]{2,1,0:T(8,128)(2,1)}) %all-reduce.7.cloned.1.call-update) | async-done | bytes 9437200 | tf_op jit(solution)/shard_map/while/body/eval_jaxpr/psum | solution.py:47
  2423.6 162.2 %all-gather.3.cloned.1.call-done = bf16[12,256,1536]{2,1,0:T(8,128)(2,1)} async-done(((bf16[12,128,1536]{2,1,0:T(8,128)(2,1)}), bf16[12,256,1536]{2,1,0:T(8,128)(2,1)}) %all-gather.3.cloned.1.call-update) | async-done | bytes 9437200 | tf_op jit(solution)/shard_map/while/body/eval_jaxpr/all_gather | solution.py:99
  2701.2 216.9 %all-reduce.5.cloned.1.call-done = bf16[12,256,1536]{2,1,0:T(8,128)(2,1)} async-done(((bf16[12,256,1536]{2,1,0:T(8,128)(2,1)}), bf16[12,256,1536]{2,1,0:T(8,128)(2,1)}) %all-reduce.5.cloned.1.call-update) | async-done | bytes 9437200 | tf_op jit(solution)/shard_map/while/body/eval_jaxpr/psum | solution.py:41
  3018.3 214.8 %all-reduce.7.cloned.1.call-done = bf16[12,256,1536]{2,1,0:T(8,128)(2,1)} async-done(((bf16[12,256,1536]{2,1,0:T(8,128)(2,1)}), bf16[12,256,1536]{2,1,0:T(8,128)(2,1)}) %all-reduce.7.cloned.1.call-update) | async-done | bytes 9437200 | tf_op jit(solution)/shard_map/while/body/eval_jaxpr/psum | solution.py:47
  3253.9 162.2 %all-gather.3.cloned.1.call-done = bf16[12,256,1536]{2,1,0:T(8,128)(2,1)} async-done(((bf16[12,128,1536]{2,1,0:T(8,128)(2,1)}), bf16[12,256,1536]{2,1,0:T(8,128)(2,1)}) %all-gather.3.cloned.1.call-update) | async-done | bytes 9437200 | tf_op jit(solution)/shard_map/while/body/eval_jaxpr/all_gather | solution.py:99
  3531.4 216.9 %all-reduce.5.cloned.1.call-done = bf16[12,256,1536]{2,1,0:T(8,128)(2,1)} async-done(((bf16[12,256,1536]{2,1,0:T(8,128)(2,1)}), bf16[12,256,1536]{2,1,0:T(8,128)(2,1)}) %all-reduce.5.cloned.1.call-update) | async-done | bytes 9437200 | tf_op jit(solution)/shard_map/while/body/eval_jaxpr/psum | solution.py:41
  3848.6 214.9 %all-reduce.7.cloned.1.call-done = bf16[12,256,1536]{2,1,0:T(8,128)(2,1)} async-done(((bf16[12,256,1536]{2,1,0:T(8,128)(2,1)}), bf16[12,256,1536]{2,1,0:T(8,128)(2,1)}) %all-reduce.7.cloned.1.call-update) | async-done | bytes 9437200 | tf_op jit(solution)/shard_map/while/body/eval_jaxpr/psum | solution.py:47
  4084.2 162.2 %all-gather.3.cloned.1.call-done = bf16[12,256,1536]{2,1,0:T(8,128)(2,1)} async-done(((bf16[12,128,1536]{2,1,0:T(8,128)(2,1)}), bf16[12,256,1536]{2,1,0:T(8,128)(2,1)}) %all-gather.3.cloned.1.call-update) | async-done | bytes 9437200 | tf_op jit(solution)/shard_map/while/body/eval_jaxpr/all_gather | solution.py:99
  4262.7 4519.2 %while.55 = (s32[]{:T(128)}, bf16[12,256,1536]{2,1,0:T(8,128)(2,1)}, f32[3,1536,8,96]{1,3,2,0:T(8,128)}, f32[3,8,96]{2,1,0:T(8,128)}, f32[8,96,1536]{2,1,0:T(8,1...) while((s32[]{:T(128)}, ...), condition=%wide.region_32.33_spmd.clone, body=%wide.region_10.32_spmd.clone.sunk | while | flops 182236135424 | bytes 1371787904 | solution.py:160
  4438.0 150.9 %all-reduce.9.cloned.1.call-done = bf16[12,256,1536]{2,1,0:T(8,128)(2,1)} async-done(((bf16[12,256,1536]{2,1,0:T(8,128)(2,1)}), bf16[12,256,1536]{2,1,0:T(8,128)(2,1)}) %all-reduce.9.cloned.1.call-update) | async-done | bytes 9437200 | tf_op jit(solution)/shard_map/while/body/eval_jaxpr/psum | solution.py:69
  4793.2 160.5 %all-reduce.11.cloned.1.call-done = bf16[12,256,1536]{2,1,0:T(8,128)(2,1)} async-done(((bf16[12,256,1536]{2,1,0:T(8,128)(2,1)}), bf16[12,256,1536]{2,1,0:T(8,128)(2,1)}) %all-reduce.11.cloned.1.call-update) | async-done | bytes 9437200 | tf_op jit(solution)/shard_map/while/body/eval_jaxpr/psum | solution.py:82
  5090.2 75.8 all-gather.5.cloned.1.call-done
  5341.3 151.1 %all-reduce.9.cloned.1.call-done = bf16[12,256,1536]{2,1,0:T(8,128)(2,1)} async-done(((bf16[12,256,1536]{2,1,0:T(8,128)(2,1)}), bf16[12,256,1536]{2,1,0:T(8,128)(2,1)}) %all-reduce.9.cloned.1.call-update) | async-done | bytes 9437200 | tf_op jit(solution)/shard_map/while/body/eval_jaxpr/psum | solution.py:69
  5698.0 159.3 %all-reduce.11.cloned.1.call-done = bf16[12,256,1536]{2,1,0:T(8,128)(2,1)} async-done(((bf16[12,256,1536]{2,1,0:T(8,128)(2,1)}), bf16[12,256,1536]{2,1,0:T(8,128)(2,1)}) %all-reduce.11.cloned.1.call-update) | async-done | bytes 9437200 | tf_op jit(solution)/shard_map/while/body/eval_jaxpr/psum | solution.py:82
  5998.0 72.0 all-gather.5.cloned.1.call-done
  6245.3 150.9 %all-reduce.9.cloned.1.call-done = bf16[12,256,1536]{2,1,0:T(8,128)(2,1)} async-done(((bf16[12,256,1536]{2,1,0:T(8,128)(2,1)}), bf16[12,256,1536]{2,1,0:T(8,128)(2,1)}) %all-reduce.9.cloned.1.call-update) | async-done | bytes 9437200 | tf_op jit(solution)/shard_map/while/body/eval_jaxpr/psum | solution.py:69
  6601.8 159.1 %all-reduce.11.cloned.1.call-done = bf16[12,256,1536]{2,1,0:T(8,128)(2,1)} async-done(((bf16[12,256,1536]{2,1,0:T(8,128)(2,1)}), bf16[12,256,1536]{2,1,0:T(8,128)(2,1)}) %all-reduce.11.cloned.1.call-update) | async-done | bytes 9437200 | tf_op jit(solution)/shard_map/while/body/eval_jaxpr/psum | solution.py:82
  6901.4 72.0 all-gather.5.cloned.1.call-done
  7148.5 151.1 %all-reduce.9.cloned.1.call-done = bf16[12,256,1536]{2,1,0:T(8,128)(2,1)} async-done(((bf16[12,256,1536]{2,1,0:T(8,128)(2,1)}), bf16[12,256,1536]{2,1,0:T(8,128)(2,1)}) %all-reduce.9.cloned.1.call-update) | async-done | bytes 9437200 | tf_op jit(solution)/shard_map/while/body/eval_jaxpr/psum | solution.py:69
  7505.3 159.3 %all-reduce.11.cloned.1.call-done = bf16[12,256,1536]{2,1,0:T(8,128)(2,1)} async-done(((bf16[12,256,1536]{2,1,0:T(8,128)(2,1)}), bf16[12,256,1536]{2,1,0:T(8,128)(2,1)}) %all-reduce.11.cloned.1.call-update) | async-done | bytes 9437200 | tf_op jit(solution)/shard_map/while/body/eval_jaxpr/psum | solution.py:82
  7805.2 72.0 all-gather.5.cloned.1.call-done
  8052.6 150.8 %all-reduce.9.cloned.1.call-done = bf16[12,256,1536]{2,1,0:T(8,128)(2,1)} async-done(((bf16[12,256,1536]{2,1,0:T(8,128)(2,1)}), bf16[12,256,1536]{2,1,0:T(8,128)(2,1)}) %all-reduce.9.cloned.1.call-update) | async-done | bytes 9437200 | tf_op jit(solution)/shard_map/while/body/eval_jaxpr/psum | solution.py:69
  8409.1 159.1 %all-reduce.11.cloned.1.call-done = bf16[12,256,1536]{2,1,0:T(8,128)(2,1)} async-done(((bf16[12,256,1536]{2,1,0:T(8,128)(2,1)}), bf16[12,256,1536]{2,1,0:T(8,128)(2,1)}) %all-reduce.11.cloned.1.call-update) | async-done | bytes 9437200 | tf_op jit(solution)/shard_map/while/body/eval_jaxpr/psum | solution.py:82
  8708.6 72.0 all-gather.5.cloned.1.call-done
  (1035 shorter events, 3894.8 us)
Async XLA Ops:
  92.1 334.9 %all-reduce.5.cloned.1.call-start = ((), (), s32[]{:S(2)}) async-start(), calls=%async_computation | async-start | bytes 18874368 | tf_op jit(solution)/shard_map/while/body/eval_jaxpr/psum | solution.py:41
  207.2 534.9 %all-reduce.7.cloned.1.call-start = ((), (), s32[]{:S(2)}) async-start(), calls=%async_computation.1 | async-start | bytes 18874368 | tf_op jit(solution)/shard_map/while/body/eval_jaxpr/psum | solution.py:47
  527.0 398.1 %all-gather.3.cloned.1.call-start = ((), (), s32[]{:S(2)}) async-start(), calls=%async_computation.2 | async-start | bytes 14155776 | tf_op jit(solution)/shard_map/while/body/eval_jaxpr/all_gather | solution.py:99
  925.6 331.6 %all-reduce.5.cloned.1.call-start = ((), (), s32[]{:S(2)}) async-start(), calls=%async_computation | async-start | bytes 18874368 | tf_op jit(solution)/shard_map/while/body/eval_jaxpr/psum | solution.py:41
  1040.4 532.3 %all-reduce.7.cloned.1.call-start = ((), (), s32[]{:S(2)}) async-start(), calls=%async_computation.1 | async-start | bytes 18874368 | tf_op jit(solution)/shard_map/while/body/eval_jaxpr/psum | solution.py:47
  1357.6 398.0 %all-gather.3.cloned.1.call-start = ((), (), s32[]{:S(2)}) async-start(), calls=%async_computation.2 | async-start | bytes 14155776 | tf_op jit(solution)/shard_map/while/body/eval_jaxpr/all_gather | solution.py:99
  1755.9 331.8 %all-reduce.5.cloned.1.call-start = ((), (), s32[]{:S(2)}) async-start(), calls=%async_computation | async-start | bytes 18874368 | tf_op jit(solution)/shard_map/while/body/eval_jaxpr/psum | solution.py:41
  1870.6 532.3 %all-reduce.7.cloned.1.call-start = ((), (), s32[]{:S(2)}) async-start(), calls=%async_computation.1 | async-start | bytes 18874368 | tf_op jit(solution)/shard_map/while/body/eval_jaxpr/psum | solution.py:47
  2188.1 397.8 %all-gather.3.cloned.1.call-start = ((), (), s32[]{:S(2)}) async-start(), calls=%async_computation.2 | async-start | bytes 14155776 | tf_op jit(solution)/shard_map/while/body/eval_jaxpr/all_gather | solution.py:99
  2586.1 331.9 %all-reduce.5.cloned.1.call-start = ((), (), s32[]{:S(2)}) async-start(), calls=%async_computation | async-start | bytes 18874368 | tf_op jit(solution)/shard_map/while/body/eval_jaxpr/psum | solution.py:41
  2701.1 532.0 %all-reduce.7.cloned.1.call-start = ((), (), s32[]{:S(2)}) async-start(), calls=%async_computation.1 | async-start | bytes 18874368 | tf_op jit(solution)/shard_map/while/body/eval_jaxpr/psum | solution.py:47
  3018.3 397.8 %all-gather.3.cloned.1.call-start = ((), (), s32[]{:S(2)}) async-start(), calls=%async_computation.2 | async-start | bytes 14155776 | tf_op jit(solution)/shard_map/while/body/eval_jaxpr/all_gather | solution.py:99
  3416.4 331.8 %all-reduce.5.cloned.1.call-start = ((), (), s32[]{:S(2)}) async-start(), calls=%async_computation | async-start | bytes 18874368 | tf_op jit(solution)/shard_map/while/body/eval_jaxpr/psum | solution.py:41
  3531.3 532.2 %all-reduce.7.cloned.1.call-start = ((), (), s32[]{:S(2)}) async-start(), calls=%async_computation.1 | async-start | bytes 18874368 | tf_op jit(solution)/shard_map/while/body/eval_jaxpr/psum | solution.py:47
  3848.5 398.0 %all-gather.3.cloned.1.call-start = ((), (), s32[]{:S(2)}) async-start(), calls=%async_computation.2 | async-start | bytes 14155776 | tf_op jit(solution)/shard_map/while/body/eval_jaxpr/all_gather | solution.py:99
  4262.9 325.9 %all-reduce.9.cloned.1.call-start = ((), (), s32[]{:S(2)}) async-start(), calls=%async_computation.3 | async-start | bytes 18874368 | tf_op jit(solution)/shard_map/while/body/eval_jaxpr/psum | solution.py:69
  4373.9 579.7 %all-reduce.11.cloned.1.call-start = ((), (), s32[]{:S(2)}) async-start(), calls=%async_computation.4 | async-start | bytes 18874368 | tf_op jit(solution)/shard_map/while/body/eval_jaxpr/psum | solution.py:82
  4738.7 427.3 %all-gather.5.cloned.1.call-start = ((), (), s32[]{:S(2)}) async-start(), calls=%async_computation.5 | async-start | bytes 14155776 | tf_op jit(solution)/shard_map/while/body/eval_jaxpr/all_gather | solution.py:99
  5166.4 325.9 %all-reduce.9.cloned.1.call-start = ((), (), s32[]{:S(2)}) async-start(), calls=%async_computation.3 | async-start | bytes 18874368 | tf_op jit(solution)/shard_map/while/body/eval_jaxpr/psum | solution.py:69
  5277.4 579.9 %all-reduce.11.cloned.1.call-start = ((), (), s32[]{:S(2)}) async-start(), calls=%async_computation.4 | async-start | bytes 18874368 | tf_op jit(solution)/shard_map/while/body/eval_jaxpr/psum | solution.py:82
  5642.4 427.6 %all-gather.5.cloned.1.call-start = ((), (), s32[]{:S(2)}) async-start(), calls=%async_computation.5 | async-start | bytes 14155776 | tf_op jit(solution)/shard_map/while/body/eval_jaxpr/all_gather | solution.py:99
  5900.1 44.0 collective-permute-start.1
  6070.2 326.0 %all-reduce.9.cloned.1.call-start = ((), (), s32[]{:S(2)}) async-start(), calls=%async_computation.3 | async-start | bytes 18874368 | tf_op jit(solution)/shard_map/while/body/eval_jaxpr/psum | solution.py:69
  6181.2 579.7 %all-reduce.11.cloned.1.call-start = ((), (), s32[]{:S(2)}) async-start(), calls=%async_computation.4 | async-start | bytes 18874368 | tf_op jit(solution)/shard_map/while/body/eval_jaxpr/psum | solution.py:82
  6546.0 427.3 %all-gather.5.cloned.1.call-start = ((), (), s32[]{:S(2)}) async-start(), calls=%async_computation.5 | async-start | bytes 14155776 | tf_op jit(solution)/shard_map/while/body/eval_jaxpr/all_gather | solution.py:99
  6803.5 44.1 collective-permute-start.1
  6973.7 325.9 %all-reduce.9.cloned.1.call-start = ((), (), s32[]{:S(2)}) async-start(), calls=%async_computation.3 | async-start | bytes 18874368 | tf_op jit(solution)/shard_map/while/body/eval_jaxpr/psum | solution.py:69
  7084.7 579.9 %all-reduce.11.cloned.1.call-start = ((), (), s32[]{:S(2)}) async-start(), calls=%async_computation.4 | async-start | bytes 18874368 | tf_op jit(solution)/shard_map/while/body/eval_jaxpr/psum | solution.py:82
  7449.7 427.6 %all-gather.5.cloned.1.call-start = ((), (), s32[]{:S(2)}) async-start(), calls=%async_computation.5 | async-start | bytes 14155776 | tf_op jit(solution)/shard_map/while/body/eval_jaxpr/all_gather | solution.py:99
  7877.4 326.0 %all-reduce.9.cloned.1.call-start = ((), (), s32[]{:S(2)}) async-start(), calls=%async_computation.3 | async-start | bytes 18874368 | tf_op jit(solution)/shard_map/while/body/eval_jaxpr/psum | solution.py:69
  7988.5 579.7 %all-reduce.11.cloned.1.call-start = ((), (), s32[]{:S(2)}) async-start(), calls=%async_computation.4 | async-start | bytes 18874368 | tf_op jit(solution)/shard_map/while/body/eval_jaxpr/psum | solution.py:82
  8353.3 427.3 %all-gather.5.cloned.1.call-start = ((), (), s32[]{:S(2)}) async-start(), calls=%async_computation.5 | async-start | bytes 14155776 | tf_op jit(solution)/shard_map/while/body/eval_jaxpr/all_gather | solution.py:99
  (278 other events, 17651.7 us)
Sparse Core Ops, SparseCore 0:
  207.3 219.5 all-reduce.4
  527.1 214.8 all-reduce.6
  763.0 162.0 all-gather.2
  1040.5 216.7 all-reduce.4
  1357.8 214.8 all-reduce.6
  1593.5 162.1 all-gather.2
  1870.7 216.9 all-reduce.4
  2188.2 214.6 all-reduce.6
  2423.7 162.0 all-gather.2
  2701.2 216.8 all-reduce.4
  3018.4 214.6 all-reduce.6
  3254.0 162.0 all-gather.2
  3531.4 216.8 all-reduce.4
  3848.6 214.7 all-reduce.6
  4084.3 162.0 all-gather.2
  4374.0 214.7 all-reduce.8
  4738.8 214.7 all-reduce.10
  5039.0 127.0 all-gather.4
  5277.5 214.7 all-reduce.8
  5642.5 214.7 all-reduce.10
  5944.3 125.6 all-gather.4
  6181.4 214.7 all-reduce.8
  6546.2 214.7 all-reduce.10
  6847.7 125.5 all-gather.4
  7084.8 214.7 all-reduce.8
  7449.8 214.7 all-reduce.10
  7751.6 125.6 all-gather.4
  7988.6 214.7 all-reduce.8
  8353.4 214.7 all-reduce.10
  8654.9 125.6 all-gather.4
where the time goes:
time: 8820 us
  waiting for transfers between devices  4920 us (56%)
  matrix products  2530 us (29%)
  other arithmetic  1080 us (12%)
  local copies, waits for them, and re-layouts  230 us (3%)
    all_gather x10, waiting for transfers between devices, pass_on(): return lax.all_gather(moved_part, 'tp', axis=1, tiled=True)  1180 us
    psum x5, waiting for transfers between devices, layer_forward(): attn_sum = lax.psum(attn_part, 'tp')  1090 us
    psum x5, waiting for transfers between devices, layer_forward(): mlp_sum = lax.psum(mlp_part, 'tp')  1070 us
    psum x5, waiting for transfers between devices, layer_backward(): lax.psum(jnp.einsum('bsche,cdhe->bsd', g_qkv, w_qkv, preferred_element_ty...  797 us
    psum x5, waiting for transfers between devices, layer_backward(): lax.psum(jnp.einsum('bsf,df->bsd', g_pre_half, w_fc1, preferred_element_t...  755 us
    dot_general x20, matrix products, causal_attention(): jnp.einsum('bqhe,bkhe->bhqk', q_heads, k_heads, preferred_element_type=jn...  335 us
    sub x10, other arithmetic, causal_attention(): attn_probs = jax.nn.softmax(scores, axis=-1).astype(jnp.bfloat16)  319 us
    dot_general x5, matrix products, layer_backward(): jnp.einsum('bsd,fd->bsf', grad_out, w_fc2, preferred_element_type=jnp.flo...  312 us
  transfers between devices with their start and end apart: 40, of which 35 were waited for; matrix products, arithmetic and copies ran while one was open for 12% of the time, Pallas kernels for 0%

commit v1 on v0

v1 whole, which is shorter than its diff:
```python
import functools

import jax
import jax.numpy as jnp
from jax import lax
from jax.experimental import pallas as pl
from jax.experimental.pallas import tpu as pltpu
from jax.sharding import PartitionSpec as P

LN_EPS = 1e-5
F32 = jnp.float32
BF16 = jnp.bfloat16
MESH = pl.DeviceIdType.MESH
NEG = -1e30
ROW_CHUNK = 32
GELU_C = 0.7978845608028654
GELU_K = 0.044715

WINDOWS = ((0, 128, 0), (0, 256, 96), (128, 256, 64), (256, 128, 32))


def dot_nn(lhs, rhs):
    return lax.dot_general(lhs, rhs, (((1,), (0,)), ((), ())), preferred_element_type=F32)


def dot_nt(lhs, rhs):
    return lax.dot_general(lhs, rhs, (((1,), (1,)), ((), ())), preferred_element_type=F32)


def dot_tn(lhs, rhs):
    return lax.dot_general(lhs, rhs, (((0,), (0,)), ((), ())), preferred_element_type=F32)


def head_only(window, offset, width):
    lane = lax.broadcasted_iota(jnp.int32, window.shape, 1)
    return jnp.where((lane >= offset) & (lane < offset + width), window, jnp.zeros_like(window))


def join_heads(parts, width):
    lane = lax.broadcasted_iota(jnp.int32, (parts[0].shape[0], 128), 1)
    first = jnp.where(lane < width, parts[0], parts[1][:, :128])
    second = jnp.where(lane < 2 * width - 128, parts[1][:, 128:], parts[2][:, :128])
    third = jnp.where(lane < 3 * width - 256, parts[2][:, 128:], parts[3])
    return first, second, third


def norm_stats(x_wide):
    centered = x_wide - jnp.mean(x_wide, axis=-1, keepdims=True)
    inv_std = lax.rsqrt(jnp.mean(centered * centered, axis=-1, keepdims=True) + LN_EPS)
    return centered * inv_std, inv_std


def fold_rows(block):
    rows, cols = block.shape
    return jnp.sum(block.reshape(rows // 8, 8, cols), axis=0)


def neighbour_barrier(stage, tp_peer, stages):
    barrier = pltpu.get_barrier_semaphore()
    pl.semaphore_signal(barrier, inc=1, device_id={"tp": tp_peer}, device_id_type=MESH)
    pl.semaphore_signal(barrier, inc=1, device_id={"pp": lax.rem(stage + 1, stages)}, device_id_type=MESH)
    pl.semaphore_signal(barrier, inc=1, device_id={"pp": lax.rem(stage + stages - 1, stages)}, device_id_type=MESH)
    pl.semaphore_wait(barrier, 3)


def fwd_kernel(subs, stages, width, tile,
               x_in, wq_h, wo_h, w1_h, w2_h, bq, bo, ln, b1, b2,
               x_all, qkv_all, o_all, mid_all, h1_all, h2_all, u_all, a_all, y_all, part_all,
               wq, wo, w1, w2, xb, h1b, qkvb, ob, midb, h2b, ub, ab, partb, rb, yb,
               w_sem, in_sem, out_sem, mid_sem, y_sem, part_send, part_recv, y_send, x_recv):
    stage = lax.axis_index("pp")
    tp_me = lax.axis_index("tp")
    tp_peer = 1 - tp_me
    last_stage = stages - 1
    rows, d_model = xb.shape
    half = d_model // 2
    ff = ub.shape[1]
    scale = width ** -0.5

    loads = [pltpu.make_async_copy(src, dst, w_sem.at[i]) for i, (src, dst) in enumerate(((wq_h, wq), (wo_h, wo), (w1_h, w1), (w2_h, w2)))]
    for load in loads:
        load.start()
    neighbour_barrier(stage, tp_peer, stages)

    def outs(m):
        return (pltpu.make_async_copy(h1b, h1_all.at[m], out_sem.at[0]),
                pltpu.make_async_copy(qkvb, qkv_all.at[m], out_sem.at[1]),
                pltpu.make_async_copy(ob.at[:, pl.ds(pl.multiple_of(tp_me * half, 128), half)], o_all.at[m], out_sem.at[2]),
                pltpu.make_async_copy(h2b, h2_all.at[m], out_sem.at[3]),
                pltpu.make_async_copy(ub, u_all.at[m], out_sem.at[4]),
                pltpu.make_async_copy(ab, a_all.at[m], out_sem.at[5]),
                pltpu.make_async_copy(xb, x_all.at[m], out_sem.at[6]))

    def mid_out(m):
        slot = lax.rem(m, 2)
        return pltpu.make_async_copy(midb.at[slot], mid_all.at[m], mid_sem.at[slot])

    def y_out(m):
        slot = lax.rem(m, 2)
        return pltpu.make_async_copy(yb.at[slot], y_all.at[m], y_sem.at[slot])

    def part_copy(m):
        slot = lax.rem(m, 2)
        return pltpu.make_async_remote_copy(src_ref=partb.at[slot], dst_ref=part_all.at[m], send_sem=part_send.at[slot], recv_sem=part_recv.at[m],
                                            device_id={"tp": tp_peer}, device_id_type=MESH)

    def next_copy(m):
        slot = lax.rem(m, 2)
        return pltpu.make_async_remote_copy(src_ref=yb.at[slot], dst_ref=x_all.at[m], send_sem=y_send.at[slot], recv_sem=x_recv.at[m],
                                            device_id={"pp": jnp.minimum(stage + 1, last_stage)}, device_id_type=MESH)

    def layer_norm(src, dst, gain, shift):
        for r in range(0, rows, ROW_CHUNK):
            normed, _ = norm_stats(src[r:r + ROW_CHUNK, :].astype(F32))
            dst[r:r + ROW_CHUNK, :] = (normed * gain + shift).astype(BF16)

    def attend(group, carry):
        base = pl.multiple_of((group // 2) * (3 * half) + lax.rem(group, 2) * (4 * width), 128)
        out_base = pl.multiple_of(group * (4 * width), 128)
        for blk in range(rows // 128):
            r0, keys = blk * 128, (blk + 1) * 128
            row = lax.broadcasted_iota(jnp.int32, (128, keys), 0) + r0
            col = lax.broadcasted_iota(jnp.int32, (128, keys), 1)
            parts = []
            for start, size, offset in WINDOWS:
                query = head_only(qkvb[r0:r0 + 128, pl.ds(base + start, size)], offset, width)
                key = qkvb[0:keys, pl.ds(base + half + start, size)]
                value = qkvb[0:keys, pl.ds(base + 2 * half + start, size)]
                score = jnp.where(row >= col, dot_nt(query, key) * scale, NEG)
                weight = jnp.exp(score - jnp.max(score, axis=1, keepdims=True))
                prob = (weight * (1.0 / jnp.sum(weight, axis=1, keepdims=True))).astype(BF16)
                parts.append(dot_nn(prob, value))
            for i, piece in enumerate(join_heads(parts, width)):
                ob[r0:r0 + 128, pl.ds(out_base + i * 128, 128)] = piece.astype(BF16)
        return carry

    def finish(m):
        slot = lax.rem(m, 2)
        part_copy(m).wait_recv()
        load = pltpu.make_async_copy(part_all.at[m], rb, in_sem)
        load.start()

        @pl.when(m >= 2)
        def _():
            y_out(m - 2).wait()

            @pl.when(stage < last_stage)
            def _():
                next_copy(m - 2).wait_send()

        load.wait()
        for r in range(0, rows, ROW_CHUNK):
            both = partb[slot, r:r + ROW_CHUNK, :].astype(F32) + rb[r:r + ROW_CHUNK, :].astype(F32)
            yb[slot, r:r + ROW_CHUNK, :] = (midb[slot, r:r + ROW_CHUNK, :].astype(F32) + both + b2[...]).astype(BF16)

        @pl.when(stage < last_stage)
        def _():
            next_copy(m).start()

        y_out(m).start()
        part_copy(m).wait_send()

    def one_sub(m, carry):
        slot = lax.rem(m, 2)
        prev = jnp.maximum(m - 1, 0)
        h1_o, qkv_o, o_o, h2_o, u_o, a_o, x_o = outs(m)
        h1_p, qkv_p, o_p, h2_p, u_p, a_p, x_p = outs(prev)

        @pl.when(stage == 0)
        def _():
            @pl.when(m > 0)
            def _():
                x_p.wait()

            load = pltpu.make_async_copy(x_in.at[m], xb, in_sem)
            load.start()
            load.wait()
            x_o.start()

        @pl.when(stage > 0)
        def _():
            next_copy(m).wait_recv()
            load = pltpu.make_async_copy(x_all.at[m], xb, in_sem)
            load.start()
            load.wait()

        @pl.when(m > 0)
        def _():
            h1_p.wait()
            qkv_p.wait()
            o_p.wait()
            h2_p.wait()

        layer_norm(xb, h1b, ln[0:1, :], ln[1:2, :])
        h1_o.start()

        @pl.when(m == 0)
        def _():
            loads[0].wait()

        for n in range(0, 3 * d_model, tile):
            qkvb[:, n:n + tile] = (dot_nn(h1b[...], wq[:, n:n + tile]) + bq[:, n:n + tile]).astype(BF16)
        qkv_o.start()
        lax.fori_loop(0, d_model // (4 * width), attend, 0)
        o_o.start()

        @pl.when(m == 0)
        def _():
            for load in loads[1:]:
                load.wait()

        @pl.when(m >= 2)
        def _():
            mid_out(m - 2).wait()

        for n in range(0, d_model, tile):
            midb[slot, :, n:n + tile] = (xb[:, n:n + tile].astype(F32) + dot_nn(ob[...], wo[:, n:n + tile]) + bo[:, n:n + tile]).astype(BF16)
        mid_out(m).start()
        layer_norm(midb.at[slot], h2b, ln[2:3, :], ln[3:4, :])
        h2_o.start()

        @pl.when(m > 0)
        def _():
            u_p.wait()
            a_p.wait()

        for n in range(0, ff, tile):
            pre = dot_nn(h2b[...], w1[:, n:n + tile]) + b1[:, n:n + tile]
            ub[:, n:n + tile] = pre
            cdf = 0.5 * (1.0 + jnp.tanh(GELU_C * (pre + GELU_K * (pre * pre * pre))))
            ab[:, n:n + tile] = (pre * cdf).astype(BF16)
        u_o.start()
        a_o.start()
        for n in range(0, d_model, tile):
            partb[slot, :, n:n + tile] = dot_nn(ab[...], w2[:, n:n + tile]).astype(BF16)
        part_copy(m).start()

        @pl.when(m > 0)
        def _():
            finish(m - 1)

        return carry

    lax.fori_loop(0, subs, one_sub, 0)
    finish(subs - 1)
    h1_o, qkv_o, o_o, h2_o, u_o, a_o, x_o = outs(subs - 1)
    for copy in (h1_o, qkv_o, o_o, h2_o, u_o, a_o):
        copy.wait()

    @pl.when(stage == 0)
    def _():
        x_o.wait()

    for m in (subs - 2, subs - 1):
        mid_out(m).wait()
        y_out(m).wait()

        @pl.when(stage < last_stage)
        def _():
            next_copy(m).wait_send()


def bwd_kernel(subs, stages, width, tile,
               dy_in, x_all, mid_all, u_all, qkv_all, w2t_h, w1t_h, wot_h, wqt_h, ln,
               dy_all, dpre_all, gmid_all, dqkv_all, gin_all, part_all, db1, db2, dbo, dbq, dln,
               w2t, w1t, wot, wqt, dyb, ub, dpb, partb, rb, midb, xb, gmb, qkvb, gib,
               w_sem, in_sem, pre_sem, out_sem, dy_sem, gi_sem, part_send, part_recv, gi_send, dy_recv):
    stage = lax.axis_index("pp")
    tp_me = lax.axis_index("tp")
    tp_peer = 1 - tp_me
    last_stage = stages - 1
    rows, d_model = xb.shape
    half = d_model // 2
    ff = ub.shape[1]
    scale = width ** -0.5

    loads = [pltpu.make_async_copy(src, dst, w_sem.at[i]) for i, (src, dst) in enumerate(((w2t_h, w2t), (w1t_h, w1t), (wot_h, wot), (wqt_h, wqt)))]
    for load in loads:
        load.start()

    def fetch(m):
        return (pltpu.make_async_copy(u_all.at[m], ub, pre_sem.at[0]),
                pltpu.make_async_copy(mid_all.at[m], midb, pre_sem.at[1]),
                pltpu.make_async_copy(qkv_all.at[m], qkvb, pre_sem.at[2]),
                pltpu.make_async_copy(x_all.at[m], xb, pre_sem.at[3]))

    for copy in fetch(0):
        copy.start()
    for acc in (db1, db2, dbo, dbq, dln):
        acc[...] = jnp.zeros_like(acc)
    neighbour_barrier(stage, tp_peer, stages)

    def outs(m):
        return (pltpu.make_async_copy(dpb, dpre_all.at[m], out_sem.at[0]),
                pltpu.make_async_copy(gmb, gmid_all.at[m], out_sem.at[1]),
                pltpu.make_async_copy(qkvb.at[:, pl.ds(pl.multiple_of(tp_me * (3 * half), 128), 3 * half)], dqkv_all.at[m], out_sem.at[2]))

    def dy_out(m):
        slot = lax.rem(m, 2)
        return pltpu.make_async_copy(dyb.at[slot], dy_all.at[m], dy_sem.at[slot])

    def gi_out(m):
        slot = lax.rem(m, 2)
        return pltpu.make_async_copy(gib.at[slot], gin_all.at[m], gi_sem.at[slot])

    def part_copy(m):
        slot = lax.rem(m, 2)
        return pltpu.make_async_remote_copy(src_ref=partb.at[slot], dst_ref=part_all.at[m], send_sem=part_send.at[slot], recv_sem=part_recv.at[m],
                                            device_id={"tp": tp_peer}, device_id_type=MESH)

    def prev_copy(m):
        slot = lax.rem(m, 2)
        return pltpu.make_async_remote_copy(src_ref=gib.at[slot], dst_ref=dy_all.at[m], send_sem=gi_send.at[slot], recv_sem=dy_recv.at[m],
                                            device_id={"pp": jnp.maximum(stage - 1, 0)}, device_id_type=MESH)

    def norm_grad(x_rows, grad, gain, which):
        normed, inv_std = norm_stats(x_rows)
        dln[which] += fold_rows(grad * normed)
        dln[which + 1] += fold_rows(grad)
        scaled = grad * gain
        mean_scaled = jnp.mean(scaled, axis=-1, keepdims=True)
        mean_proj = jnp.mean(scaled * normed, axis=-1, keepdims=True)
        return inv_std * (scaled - mean_scaled - normed * mean_proj)

    def mlp_part(m):
        slot = lax.rem(m, 2)
        u_f = fetch(m)[0]

        @pl.when(stage == last_stage)
        def _():
            @pl.when(m >= 2)
            def _():
                dy_out(m - 2).wait()

            load = pltpu.make_async_copy(dy_in.at[m], dyb.at[slot], in_sem)
            load.start()
            load.wait()
            dy_out(m).start()

        @pl.when(stage < last_stage)
        def _():
            prev_copy(m).wait_recv()
            load = pltpu.make_async_copy(dy_all.at[m], dyb.at[slot], in_sem)
            load.start()
            load.wait()

        @pl.when(m == 0)
        def _():
            loads[0].wait()
            loads[1].wait()

        @pl.when(m > 0)
        def _():
            outs(m - 1)[0].wait()

        u_f.wait()
        for r in range(0, rows, ROW_CHUNK):
            db2[...] += fold_rows(dyb[slot, r:r + ROW_CHUNK, :].astype(F32))
        for n in range(0, ff, tile):
            grad = dot_nn(dyb[slot], w2t[:, n:n + tile]).astype(BF16).astype(F32)
            pre = ub[:, n:n + tile]
            square = pre * pre
            bend = jnp.tanh(GELU_C * (pre + GELU_K * (square * pre)))
            slope = 0.5 * (1.0 + bend) + (0.5 * GELU_C) * pre * (1.0 - bend * bend) * (1.0 + (3.0 * GELU_K) * square)
            grad = grad * slope
            db1[:, n:n + tile] += fold_rows(grad)
            dpb[:, n:n + tile] = grad.astype(BF16)
        outs(m)[0].start()

        @pl.when(m + 1 < subs)
        def _():
            fetch(m + 1)[0].start()

        for n in range(0, d_model, tile):
            partb[slot, :, n:n + tile] = dot_nn(dpb[...], w1t[:, n:n + tile]).astype(BF16)
        part_copy(m).start()

    def attend_grad(group, carry):
        base = pl.multiple_of((group // 2) * (3 * half) + lax.rem(group, 2) * (4 * width), 128)
        do_base = pl.multiple_of(group * (4 * width), 128)
        key_rows = rows
        d_query = [[], []]
        d_key, d_value = [], []
        for start, size, offset in WINDOWS:
            dk_sum = dv_sum = None
            for blk in range(rows // 128):
                r0, keys = blk * 128, (blk + 1) * 128
                query = qkvb[r0:r0 + 128, pl.ds(base + start, size)]
                d_out = rb[r0:r0 + 128, pl.ds(do_base + start, size)]
                key = qkvb[0:keys, pl.ds(base + half + start, size)]
                value = qkvb[0:keys, pl.ds(base + 2 * half + start, size)]
                krow = lax.broadcasted_iota(jnp.int32, (keys, 128), 0)
                qcol = lax.broadcasted_iota(jnp.int32, (keys, 128), 1) + r0
                score = jnp.where(qcol >= krow, dot_nt(key, head_only(query, offset, width)) * scale, NEG)
                weight = jnp.exp(score - jnp.max(score, axis=0, keepdims=True))
                prob = weight * (1.0 / jnp.sum(weight, axis=0, keepdims=True))
                d_prob = dot_nt(value, head_only(d_out, offset, width))
                d_score = prob * (d_prob - jnp.sum(prob * d_prob, axis=0, keepdims=True))
                d_score = d_score.astype(BF16)
                d_query[blk].append(dot_tn(d_score, key) * scale)
                dk_new = dot_nn(d_score, query) * scale
                dv_new = dot_nn(prob.astype(BF16), d_out)
                if keys < key_rows:
                    rest = jnp.zeros((key_rows - keys, size), F32)
                    dk_new = jnp.concatenate([dk_new, rest], axis=0)
                    dv_new = jnp.concatenate([dv_new, rest], axis=0)
                dk_sum = dk_new if dk_sum is None else dk_sum + dk_new
                dv_sum = dv_new if dv_sum is None else dv_sum + dv_new
            d_key.append(dk_sum)
            d_value.append(dv_sum)
        for blk in range(rows // 128):
            for i, piece in enumerate(join_heads(d_query[blk], width)):
                piece = piece.astype(BF16)
                lanes = pl.ds(base + i * 128, 128)
                qkvb[blk * 128:(blk + 1) * 128, lanes] = piece
                dbq[:, lanes] += fold_rows(piece.astype(F32))
        for c, parts in ((1, d_key), (2, d_value)):
            for i, piece in enumerate(join_heads(parts, width)):
                piece = piece.astype(BF16)
                lanes = pl.ds(base + c * half + i * 128, 128)
                qkvb[:, lanes] = piece
                dbq[:, lanes] += fold_rows(piece.astype(F32))
        return carry

    def attn_part(m):
        slot = lax.rem(m, 2)
        _, mid_f, qkv_f, x_f = fetch(m)
        _, gm_o, dq_o = outs(m)
        part_copy(m).wait_recv()
        load = pltpu.make_async_copy(part_all.at[m], rb, in_sem)
        load.start()
        mid_f.wait()

        @pl.when(m > 0)
        def _():
            outs(m - 1)[1].wait()

        @pl.when(m == 0)
        def _():
            loads[2].wait()
            loads[3].wait()

        load.wait()
        for r in range(0, rows, ROW_CHUNK):
            rr = slice(r, r + ROW_CHUNK)
            grad = (partb[slot, rr, :].astype(F32) + rb[rr, :].astype(F32)).astype(BF16).astype(F32)
            total = dyb[slot, rr, :].astype(F32) + norm_grad(midb[rr, :].astype(F32), grad, ln[2:3, :], 2)
            gmb[rr, :] = total.astype(BF16)
            dbo[...] += fold_rows(total)
        gm_o.start()

        @pl.when(m + 1 < subs)
        def _():
            fetch(m + 1)[1].start()

        for n in range(0, d_model, tile):
            rb[:, n:n + tile] = dot_nn(gmb[...], wot[:, n:n + tile]).astype(BF16)
        qkv_f.wait()
        lax.fori_loop(0, d_model // (4 * width), attend_grad, 0)
        dq_o.start()
        part_copy(m).wait_send()
        for n in range(0, d_model, tile):
            rb[:, n:n + tile] = dot_nn(qkvb[...], wqt[:, n:n + tile]).astype(BF16)
        x_f.wait()

        @pl.when(m >= 2)
        def _():
            gi_out(m - 2).wait()

            @pl.when(stage > 0)
            def _():
                prev_copy(m - 2).wait_send()

        for r in range(0, rows, ROW_CHUNK):
            rr = slice(r, r + ROW_CHUNK)
            total = gmb[rr, :].astype(F32) + norm_grad(xb[rr, :].astype(F32), rb[rr, :].astype(F32), ln[0:1, :], 0)
            gib[slot, rr, :] = total.astype(BF16)

        @pl.when(stage > 0)
        def _():
            prev_copy(m).start()

        gi_out(m).start()
        dq_o.wait()

        @pl.when(m + 1 < subs)
        def _():
            fetch(m + 1)[2].start()
            fetch(m + 1)[3].start()

    def one_sub(m, carry):
        mlp_part(m)

        @pl.when(m > 0)
        def _():
            attn_part(m - 1)

        return carry

    lax.fori_loop(0, subs, one_sub, 0)
    attn_part(subs - 1)
    for copy in outs(subs - 1)[:2]:
        copy.wait()
    for m in (subs - 2, subs - 1):
        gi_out(m).wait()

        @pl.when(stage > 0)
        def _():
            prev_copy(m).wait_send()

        @pl.when(stage == last_stage)
        def _():
            dy_out(m).wait()


ANY = pl.BlockSpec(memory_space=pl.ANY)
VMEM = pl.BlockSpec(memory_space=pltpu.VMEM)
DMA = pltpu.SemaphoreType.DMA
VMEM_LIMIT = 67043328


def fwd_call(stages, width, tile, x_in, wq, wo, w1, w2, bq, bo, ln, b1, b2):
    subs, rows, d_model = x_in.shape
    ff = w1.shape[1]
    half = d_model // 2

    def hbm(cols, dtype=BF16):
        return jax.ShapeDtypeStruct((subs, rows, cols), dtype)

    def buf(cols, dtype=BF16):
        return pltpu.VMEM((rows, cols), dtype)

    def two(cols):
        return pltpu.VMEM((2, rows, cols), BF16)

    weights = 2 * (4 * d_model * d_model + 2 * d_model * ff)
    return pl.pallas_call(
        functools.partial(fwd_kernel, subs, stages, width, tile),
        name="fwd_stage",
        out_shape=(hbm(d_model), hbm(3 * d_model), hbm(half), hbm(d_model), hbm(d_model), hbm(d_model), hbm(ff, F32), hbm(ff), hbm(d_model), hbm(d_model)),
        in_specs=[ANY] * 5 + [VMEM] * 5,
        out_specs=[ANY] * 10,
        scratch_shapes=[
            pltpu.VMEM(wq.shape, BF16), pltpu.VMEM(wo.shape, BF16), pltpu.VMEM(w1.shape, BF16), pltpu.VMEM(w2.shape, BF16),
            buf(d_model), buf(d_model), buf(3 * d_model), buf(d_model), two(d_model), buf(d_model), buf(ff, F32), buf(ff), two(d_model), buf(d_model), two(d_model),
            DMA((4,)), DMA, DMA((7,)), DMA((2,)), DMA((2,)), DMA((2,)), DMA((subs,)), DMA((2,)), DMA((subs,)),
        ],
        cost_estimate=pl.CostEstimate(flops=subs * rows * weights, bytes_accessed=weights + subs * rows * d_model * 30, transcendentals=subs * rows * (ff + rows * 16)),
        compiler_params=pltpu.CompilerParams(collective_id=0, has_side_effects=True, vmem_limit_bytes=VMEM_LIMIT),
    )(x_in, wq, wo, w1, w2, bq, bo, ln, b1, b2)


def bwd_call(stages, width, tile, dy_in, x_all, mid_all, u_all, qkv_all, w2t, w1t, wot, wqt, ln):
    subs, rows, d_model = dy_in.shape
    ff = u_all.shape[2]
    half = d_model // 2

    def hbm(cols, dtype=BF16):
        return jax.ShapeDtypeStruct((subs, rows, cols), dtype)

    def buf(cols, dtype=BF16):
        return pltpu.VMEM((rows, cols), dtype)

    def two(cols):
        return pltpu.VMEM((2, rows, cols), BF16)

    def acc(*shape):
        return jax.ShapeDtypeStruct(shape, F32)

    weights = 2 * (4 * d_model * d_model + 2 * d_model * ff)
    return pl.pallas_call(
        functools.partial(bwd_kernel, subs, stages, width, tile),
        name="bwd_stage",
        out_shape=(hbm(d_model), hbm(ff), hbm(d_model), hbm(3 * half), hbm(d_model), hbm(d_model),
                   acc(8, ff), acc(8, d_model), acc(8, d_model), acc(8, 3 * d_model), acc(4, 8, d_model)),
        in_specs=[ANY] * 9 + [VMEM],
        out_specs=[ANY] * 6 + [VMEM] * 5,
        scratch_shapes=[
            pltpu.VMEM(w2t.shape, BF16), pltpu.VMEM(w1t.shape, BF16), pltpu.VMEM(wot.shape, BF16), pltpu.VMEM(wqt.shape, BF16),
            two(d_model), buf(ff, F32), buf(ff), two(d_model), buf(d_model), buf(d_model), buf(d_model), buf(d_model), buf(3 * d_model), two(d_model),
            DMA((4,)), DMA, DMA((4,)), DMA((3,)), DMA((2,)), DMA((2,)), DMA((2,)), DMA((subs,)), DMA((2,)), DMA((subs,)),
        ],
        cost_estimate=pl.CostEstimate(flops=subs * rows * weights, bytes_accessed=weights + subs * rows * d_model * 30, transcendentals=subs * rows * (ff + rows * 16)),
        compiler_params=pltpu.CompilerParams(collective_id=1, has_side_effects=True, vmem_limit_bytes=VMEM_LIMIT),
    )(dy_in, x_all, mid_all, u_all, qkv_all, w2t, w1t, wot, wqt, ln)


def solution(mesh):
    stages = mesh.shape["pp"]
    swap = [(0, 1), (1, 0)]

    def stage_program(x_in, dy_out, w_qkv, b_qkv, w_out, b_out, ln_par, w_fc1, b_fc1, w_fc2, b_fc2):
        micro, batch, rows, d_model = x_in.shape
        heads, width = w_qkv.shape[3:]
        half = heads * width
        subs = micro * batch
        tile = half
        tp_me = lax.axis_index("tp")

        def both_halves(own, axis):
            other = lax.ppermute(own, "tp", swap)
            first = jnp.where(tp_me == 0, own, other)
            second = jnp.where(tp_me == 0, other, own)
            return jnp.concatenate([first, second], axis=axis)

        wq_own = jnp.transpose(w_qkv[0].reshape(3, d_model, half), (1, 0, 2)).reshape(d_model, 3 * half)
        wq = both_halves(wq_own, 1)
        wo = both_halves(w_out[0].reshape(half, d_model), 0)
        bq = both_halves(b_qkv[0].reshape(1, 3 * half), 1).astype(F32)
        w1, w2 = w_fc1[0], w_fc2[0]
        ln = ln_par[0].astype(F32)
        x_all, qkv_all, o_all, mid_all, h1_all, h2_all, u_all, a_all, y_all, _ = fwd_call(
            stages, width, tile, x_in.reshape(subs, rows, d_model), wq, wo, w1, w2, bq, b_out.astype(F32), ln, b_fc1.astype(F32), b_fc2.astype(F32))
        dy_all, dpre_all, gmid_all, dqkv_all, gin_all, _, db1, db2, dbo, dbq, dln = bwd_call(
            stages, width, tile, dy_out.reshape(subs, rows, d_model), x_all, mid_all, u_all, qkv_all, w2.T, w1.T, wo.T, wq.T, ln)

        def weight_grad(left, right):
            return lax.dot_general(left.reshape(subs * rows, -1), right.reshape(subs * rows, -1), (((0,), (0,)), ((), ())), preferred_element_type=F32)

        g_w_fc2 = weight_grad(a_all, dy_all)
        g_w_fc1 = weight_grad(h2_all, dpre_all)
        g_w_out = weight_grad(o_all, gmid_all).reshape(heads, width, d_model)
        g_w_qkv = jnp.transpose(weight_grad(h1_all, dqkv_all).reshape(d_model, 3, heads, width), (1, 0, 2, 3))
        g_b_qkv = lax.dynamic_slice_in_dim(jnp.sum(dbq, axis=0), tp_me * (3 * half), 3 * half).reshape(3, heads, width)
        act = (1, micro, batch, rows, d_model)
        return (y_all.reshape(act), gin_all.reshape(act), g_w_qkv[None], g_b_qkv[None], g_w_out[None], jnp.sum(dbo, axis=0)[None],
                jnp.sum(dln, axis=1)[None], g_w_fc1[None], jnp.sum(db1, axis=0)[None], g_w_fc2[None], jnp.sum(db2, axis=0)[None])

    act_spec = P(None, "dp", None, None)
    arg_specs = (act_spec, act_spec,
                 P("pp", None, None, "tp", None), P("pp", None, "tp", None), P("pp", "tp", None, None),
                 P("pp", None), P("pp", None, None), P("pp", None, "tp"), P("pp", "tp"),
                 P("pp", "tp", None), P("pp", None))
    stage_spec = P("pp", None, "dp", None, None)
    grad_axes = ("dp", "pp")
    result_specs = (stage_spec, stage_spec,
                    P(grad_axes, None, None, "tp", None), P(grad_axes, None, "tp", None), P(grad_axes, "tp", None, None),
                    P(grad_axes, None), P(grad_axes, None, None), P(grad_axes, None, "tp"), P(grad_axes, "tp"),
                    P(grad_axes, "tp", None), P(grad_axes, None))
    return jax.shard_map(stage_program, mesh=mesh, in_specs=arg_specs, out_specs=result_specs, check_vma=False)
```

time: 8820 us -> 2200 us (0.25)
  waiting for transfers between devices: 4920 us -> 167 us
  matrix products: 2530 us -> 216 us
  Pallas kernels: 0 us -> 1640 us
  other arithmetic: 1080 us -> 37.8 us
  local copies, waits for them, and re-layouts: 230 us -> 131 us
    psum x20 -> x0, waiting for transfers between devices: 3710 us -> none  [the longest x5 1090 us: layer_forward(): attn_sum = lax.psum(attn_part, 'tp')]
    dot_general x90 -> x4, matrix products: 2530 us -> 216 us  [weight_grad(): lax.dot_general(left.reshape(subs * rows, -1), right.reshape(subs * rows,...]
    pallas_call x0 -> x2, Pallas kernels: none -> 1640 us  [the longest x1 1040 us: bwd_call(): pl.pallas_call(functools.partial(bwd_kernel, subs, stages, width, tile),...]
    all_gather x10 -> x0, waiting for transfers between devices: 1180 us -> none  [pass_on(): return lax.all_gather(moved_part, 'tp', axis=1, tiled=True)]
    reduce_sum x60 -> x5, other arithmetic: 438 us -> 1.37 us  [the longest x1 0.67 us: stage_program(): jnp.sum(dln, axis=1)[None]]
    sub x10 -> x0, other arithmetic: 319 us -> none  [causal_attention(): attn_probs = jax.nn.softmax(scores, axis=-1).astype(jnp.bfloat16)]
    dynamic_update_slice x20 -> x0, other arithmetic: 232 us -> none  [the longest x5 76 us: bwd_step(): grad_buf = lax.dynamic_update_index_in_dim(grad_buf, grad_in, write_idx, 0)]
    ppermute x10 -> x3, waiting for transfers between devices: 26.9 us -> 167 us  [both_halves(): other = lax.ppermute(own, 'tp', swap)]
  transfers between devices with their start and end apart: 40 -> 3, of which waited for: 35 -> 1; matrix products, arithmetic and copies ran while one was open for 12% -> 2% of each run, Pallas kernels for 0% -> 0%
where the time goes in v1:
time: 2200 us; the launch traced here: 2190 us
  Pallas kernels  1640 us (75%)
  matrix products  216 us (10%)
  waiting for transfers between devices  167 us (8%)
  local copies, waits for them, and re-layouts  131 us (6%)
  other arithmetic  37.8 us (2%)
    pallas_call x1, Pallas kernels, bwd_call(): pl.pallas_call(functools.partial(bwd_kernel, subs, stages, width, tile),...  1040 us
    pallas_call x1, Pallas kernels, fwd_call(): pl.pallas_call(functools.partial(fwd_kernel, subs, stages, width, tile),...  599 us
    dot_general x4, matrix products, weight_grad(): lax.dot_general(left.reshape(subs * rows, -1), right.reshape(subs * rows,...  216 us
    ppermute x3, waiting for transfers between devices, both_halves(): other = lax.ppermute(own, 'tp', swap)  167 us
    unnamed x16, local copies, waits for them, and re-layouts  51.1 us
    dot_general x2, local copies, waits for them, and re-layouts, weight_grad(): lax.dot_general(left.reshape(subs * rows, -1), right.reshape(subs * rows,...  49.4 us
  transfers between devices with their start and end apart: 3, of which 1 were waited for; matrix products, arithmetic and copies ran while one was open for 2% of the time, Pallas kernels for 0%

profile of v1, /device:TPU:0, one launch (start us, length us, event | category | flops | bytes accessed | tf_op | source)
XLA Modules:
  0.0 2193.5 jit_solution(1722497176243265529)
XLA Ops:
  0.6 3.4 collective-permute-start
  4.0 2.8 copy.34
  6.9 0.8 reshape_squeeze.11
  7.7 2.0 collective-permute-start.2
  9.7 1.3 bitcast_convert_fusion.ln
  11.0 1.3 convert_element_type.18.bo
  12.3 1.3 convert_element_type.22.b2
  13.6 1.3 convert_element_type.21.b1
  14.9 12.6 copy.36
  27.5 12.6 copy.37
  40.1 167.0 %collective-permute-done.2 = bf16[1,2304]{1,0:T(2,128)(2,1)S(1)} collective-permute-done((bf16[1,2304]{1,0:T(2,128)(2,1)S(1)}, bf16[1,2304]{1,0:T(2,128)(2,1)S(1)}, u32[]{:S(2)}, u32[]{:S(2)}) %collective-permute-start.2) | collective-permute-done | bytes 4640 | tf_op jit(solution)/shard_map/ppermute | solution.py:601
  207.2 0.6 maximum_convert_fusion.bq
  207.8 2.0 broadcast_select_fusion.3
  209.8 4.4 fusion
  214.2 6.6 copy.39.wo_h
  220.8 5.8 broadcast_select_fusion.1
  226.6 18.4 fusion.1
  245.1 18.6 copy.38.wq_h
  263.6 599.3 %fwd_stage.1 = (bf16[24,256,1536]{2,1,0:T(8,128)(2,1)}, bf16[24,256,4608]{2,1,0:T(8,128)(2,1)}, bf16[24,256,768]{2,1,0:T(8,128)(2,1)}, bf16[24,256,1536]{2,1,0:T...) custom-call(bf16[24,256,1536]{2,1,0:T(8,128)(2,1)} %bitcast.81, ...), custom_call_target="tpu_custom_call" | custom-call | flops 231928233984 | bytes 320864256 | tf_op jit(solution)/shard_map/fwd_stage/pallas_call | solution.py:537
  863.0 12.7 copy.43
  875.7 1035.8 %bwd_stage.1 = (bf16[24,256,1536]{2,1,0:T(8,128)(2,1)}, bf16[24,256,3072]{2,1,0:T(8,128)(2,1)}, bf16[24,256,1536]{2,1,0:T(8,128)(2,1)}, bf16[24,256,2304]{2,1,0:...) custom-call(bf16[24,256,1536]{2,1,0:T(8,128)(2,1)} %bitcast.82, ...), custom_call_target="tpu_custom_call" | custom-call | flops 231928233984 | bytes 320864256 | tf_op jit(solution)/shard_map/bwd_stage/pallas_call | solution.py:571
  1911.5 36.8 %copy.42 = bf16[2304,6144]{1,0:T(8,128)(2,1)} copy(bf16[2304,6144]{0,1:T(8,128)(2,1)} %bitcast.68) | data formatting | bytes 56623104 | tf_op jit(solution)/shard_map/dot_general | solution.py:618
  1949.6 0.6 reduce_sum.48
  1950.2 0.7 reduce_sum.47
  1951.0 0.7 broadcast_in_dim_reshape.4
  1951.7 70.0 %convolution_bitcast_fusion = f32[1,3072,1536]{2,1,0:T(8,128)} fusion(bf16[24,256,3072]{2,1,0:T(8,128)(2,1)} %get-tuple-element.46, bf16[24,256,1536]{2,1,0:T(8,128)(2,1)} %get-tuple-element.47), kind=kOutput, calls=%fused_computation.1 | convolution fusion | flops 57982058496 | bytes 75497472 | tf_op jit(solution)/shard_map/dot_general | solution.py:618
  2021.6 69.7 %convolution_bitcast_fusion.1 = f32[1,1536,3072]{2,1,0:T(8,128)} fusion(bf16[24,256,1536]{2,1,0:T(8,128)(2,1)} %get-tuple-element.43, bf16[24,256,3072]{2,1,0:T(8,128)(2,1)} %get-tuple-element.44), kind=kOutput, calls=%fused_computation.2 | convolution fusion | flops 57982058496 | bytes 75497472 | tf_op jit(solution)/shard_map/dot_general | solution.py:618
  2091.4 21.0 convolution_bitcast_fusion.3
  2112.4 55.1 %convolution_bitcast_fusion.2 = f32[1,3,1536,8,96]{2,4,3,1,0:T(8,128)} fusion(bf16[6144,1536,1,1]{1,0,3,2:T(8,128)(2,1)} %bitcast.83, bf16[3,8,96,6144]{3,2,1,0:T(8,128)(2,1)} %bitcast.67), kind=kOutput, calls=%fused_computation.5 | convolution fusion | flops 43486543872 | bytes 61341696 | tf_op jit(solution)/shard_map/dot_general | solution.py:618
  2167.5 17.6 copy.53
  2185.0 1.4 copy-done
  2186.5 6.8 copy.54
  (21 shorter events, 1.4 us)
Async XLA Ops:
  0.6 220.2 %collective-permute-start = (bf16[1536,2304]{0,1:T(8,128)(2,1)}, bf16[1536,2304]{0,1:T(8,128)(2,1)}, u32[]{:S(2)}, u32[]{:S(2)}) collective-permute-start(bf16[1536,2304]{0,1:T(8,128)(2,1)} %bitcast.77), channel_id=1, source_target_pairs={{0,4},{4,0},{1,5},{5,1},{2,6},{6,2},{3,7},{7,3}} | collective-permute-start | bytes 21233672 | tf_op jit(solution)/shard_map/ppermute | solution.py:601
  6.9 200.9 %collective-permute-start.1 = (bf16[768,1536]{0,1:T(8,128)(2,1)S(1)}, bf16[768,1536]{0,1:T(8,128)(2,1)}, u32[]{:S(2)}, u32[]{:S(2)}) collective-permute-start(bf16[768,1536]{0,1:T(8,128)(2,1)S(1)} %copy.34), channel_id=1, source_target_pairs={{0,4},{4,0},{1,5},{5,1},{2,6},{6,2},{3,7},{7,3}} | collective-permute-start | bytes 7077896 | tf_op jit(solution)/shard_map/ppermute | solution.py:601
  7.7 199.5 %collective-permute-start.2 = (bf16[1,2304]{1,0:T(2,128)(2,1)S(1)}, bf16[1,2304]{1,0:T(2,128)(2,1)S(1)}, u32[]{:S(2)}, u32[]{:S(2)}) collective-permute-start(bf16[1,2304]{1,0:T(2,128)(2,1)S(1)} %reshape_squeeze.11), channel_id=1, source_target_pairs={{0,4},{4,0},{1,5},{5,1},{2,6},{6,2},{3,7},{7,3}} | collective-permute-start | bytes 13832 | tf_op jit(solution)/shard_map/ppermute | solution.py:601
  1911.5 36.8 %copy-start.5 = (f32[8,1536]{1,0:T(8,128)S(1)}, f32[8,1536]{1,0:T(8,128)}, u32[]{:S(2)}) copy-start(f32[8,1536]{1,0:T(8,128)} %get-tuple-element.41) | copy-start | bytes 147460
  1911.5 37.4 %copy-start.4 = (f32[8,1536]{1,0:T(8,128)S(1)}, f32[8,1536]{1,0:T(8,128)}, u32[]{:S(2)}) copy-start(f32[8,1536]{1,0:T(8,128)} %get-tuple-element.48) | copy-start | bytes 147460
  1911.5 38.0 %copy-start.3 = (f32[8,3072]{1,0:T(8,128)S(1)}, f32[8,3072]{1,0:T(8,128)}, u32[]{:S(2)}) copy-start(f32[8,3072]{1,0:T(8,128)} %get-tuple-element.45) | copy-start | bytes 294916
  1911.5 38.7 %copy-start.2 = (f32[8,4608]{1,0:T(8,128)S(1)}, f32[8,4608]{1,0:T(8,128)}, u32[]{:S(2)}) copy-start(f32[8,4608]{1,0:T(8,128)} %get-tuple-element.38) | copy-start | bytes 442372
  1911.5 38.7 %copy-start.1 = (f32[4,8,1536]{2,1,0:T(8,128)S(1)}, f32[4,8,1536]{2,1,0:T(8,128)}, u32[]{:S(2)}) copy-start(f32[4,8,1536]{2,1,0:T(8,128)} %get-tuple-element.42) | copy-start | bytes 589828
  2167.5 19.0 copy-start

commit v2 on v1

--- a/solution.py
+++ b/solution.py
@@ -15,6 +15,8 @@
 ROW_CHUNK = 32
 GELU_C = 0.7978845608028654
 GELU_K = 0.044715
+LOG2_E = 1.4426950408889634
+SOFT_ROWS = 64
 
 WINDOWS = ((0, 128, 0), (0, 256, 96), (128, 256, 64), (256, 128, 32))
 
@@ -64,9 +66,9 @@
 
 
 def fwd_kernel(subs, stages, width, tile,
-               x_in, wq_h, wo_h, w1_h, w2_h, bq, bo, ln, b1, b2,
+               x_in, wq_h, wq_p, wo_h, wo_p, w1_h, w2_h, bq, bo, ln, b1, b2,
                x_all, qkv_all, o_all, mid_all, h1_all, h2_all, u_all, a_all, y_all, part_all,
-               wq, wo, w1, w2, xb, h1b, qkvb, ob, midb, h2b, ub, ab, partb, rb, yb,
+               wq, wo, w1, w2, xb, h1b, qkvb, ob, midb, h2b, ub, ab, partb, rb, yb, sb, pb,
                w_sem, in_sem, out_sem, mid_sem, y_sem, part_send, part_recv, y_send, x_recv):
     stage = lax.axis_index("pp")
     tp_me = lax.axis_index("tp")
@@ -76,10 +78,17 @@
     half = d_model // 2
     ff = ub.shape[1]
     scale = width ** -0.5
-
-    loads = [pltpu.make_async_copy(src, dst, w_sem.at[i]) for i, (src, dst) in enumerate(((wq_h, wq), (wo_h, wo), (w1_h, w1), (w2_h, w2)))]
+    log2_scale = scale * LOG2_E
+
+    mine = pl.ds(pl.multiple_of(tp_me * half, 128), half)
+    theirs = pl.ds(pl.multiple_of(tp_peer * half, 128), half)
+    mine_q = pl.ds(pl.multiple_of(tp_me * (3 * half), 128), 3 * half)
+    theirs_q = pl.ds(pl.multiple_of(tp_peer * (3 * half), 128), 3 * half)
+    loads = [pltpu.make_async_copy(src, dst, w_sem.at[i]) for i, (src, dst) in enumerate((
+        (wq_h, wq.at[:, mine_q]), (wq_p, wq.at[:, theirs_q]), (wo_h, wo.at[mine, :]), (wo_p, wo.at[theirs, :]), (w1_h, w1), (w2_h, w2)))]
     for load in loads:
         load.start()
+    pb[:, :, 0:128, 128:rows] = jnp.zeros((2, 4, 128, rows - 128), BF16)
     neighbour_barrier(stage, tp_peer, stages)
 
     def outs(m):
@@ -114,25 +123,42 @@
             normed, _ = norm_stats(src[r:r + ROW_CHUNK, :].astype(F32))
             dst[r:r + ROW_CHUNK, :] = (normed * gain + shift).astype(BF16)
 
-    def attend(group, carry):
-        base = pl.multiple_of((group // 2) * (3 * half) + lax.rem(group, 2) * (4 * width), 128)
-        out_base = pl.multiple_of(group * (4 * width), 128)
-        for blk in range(rows // 128):
-            r0, keys = blk * 128, (blk + 1) * 128
-            row = lax.broadcasted_iota(jnp.int32, (128, keys), 0) + r0
-            col = lax.broadcasted_iota(jnp.int32, (128, keys), 1)
-            parts = []
-            for start, size, offset in WINDOWS:
-                query = head_only(qkvb[r0:r0 + 128, pl.ds(base + start, size)], offset, width)
-                key = qkvb[0:keys, pl.ds(base + half + start, size)]
-                value = qkvb[0:keys, pl.ds(base + 2 * half + start, size)]
-                score = jnp.where(row >= col, dot_nt(query, key) * scale, NEG)
-                weight = jnp.exp(score - jnp.max(score, axis=1, keepdims=True))
-                prob = (weight * (1.0 / jnp.sum(weight, axis=1, keepdims=True))).astype(BF16)
-                parts.append(dot_nn(prob, value))
+    def group_base(group):
+        return (group // 2) * (3 * half) + (group % 2) * (4 * width)
+
+    def attend():
+        def scores(group):
+            base = group_base(group)
+            for j, (start, size, offset) in enumerate(WINDOWS):
+                query = head_only(qkvb[:, base + start:base + start + size], offset, width)
+                key = qkvb[:, base + half + start:base + half + start + size]
+                sb[group % 2, j] = dot_nt(query, key)
+
+        def softmax(group):
+            for j in range(4):
+                for r0 in range(0, rows, SOFT_ROWS):
+                    keys = 128 * (r0 // 128 + 1)
+                    row = lax.broadcasted_iota(jnp.int32, (SOFT_ROWS, keys), 0) + r0
+                    col = lax.broadcasted_iota(jnp.int32, (SOFT_ROWS, keys), 1)
+                    score = jnp.where(row >= col, sb[group % 2, j, r0:r0 + SOFT_ROWS, 0:keys], NEG)
+                    weight = jnp.exp2((score - jnp.max(score, axis=1, keepdims=True)) * log2_scale)
+                    inv = 1.0 / jnp.sum(weight, axis=1, keepdims=True)
+                    pb[group % 2, j, r0:r0 + SOFT_ROWS, 0:keys] = (weight * inv).astype(BF16)
+
+        def values(group):
+            base = group_base(group) + 2 * half
+            parts = [dot_nn(pb[group % 2, j], qkvb[:, base + start:base + start + size]) for j, (start, size, _) in enumerate(WINDOWS)]
             for i, piece in enumerate(join_heads(parts, width)):
-                ob[r0:r0 + 128, pl.ds(out_base + i * 128, 128)] = piece.astype(BF16)
-        return carry
+                first = group * (4 * width) + i * 128
+                ob[:, first:first + 128] = piece.astype(BF16)
+
+        groups = d_model // (4 * width)
+        scores(0)
+        for group in range(groups):
+            if group + 1 < groups:
+                scores(group + 1)
+            softmax(group)
+            values(group)
 
     def finish(m):
         slot = lax.rem(m, 2)
@@ -160,7 +186,7 @@
         y_out(m).start()
         part_copy(m).wait_send()
 
-    def one_sub(m, carry):
+    def one_sub(m):
         slot = lax.rem(m, 2)
         prev = jnp.maximum(m - 1, 0)
         h1_o, qkv_o, o_o, h2_o, u_o, a_o, x_o = outs(m)
@@ -197,16 +223,17 @@
         @pl.when(m == 0)
         def _():
             loads[0].wait()
+            loads[1].wait()
 
         for n in range(0, 3 * d_model, tile):
             qkvb[:, n:n + tile] = (dot_nn(h1b[...], wq[:, n:n + tile]) + bq[:, n:n + tile]).astype(BF16)
         qkv_o.start()
-        lax.fori_loop(0, d_model // (4 * width), attend, 0)
+        attend()
         o_o.start()
 
         @pl.when(m == 0)
         def _():
-            for load in loads[1:]:
+            for load in loads[2:]:
                 load.wait()
 
         @pl.when(m >= 2)
@@ -235,14 +262,18 @@
             partb[slot, :, n:n + tile] = dot_nn(ab[...], w2[:, n:n + tile]).astype(BF16)
         part_copy(m).start()
 
+    def step(m, carry):
+        @pl.when(m < subs)
+        def _():
+            one_sub(m)
+
         @pl.when(m > 0)
         def _():
             finish(m - 1)
 
         return carry
 
-    lax.fori_loop(0, subs, one_sub, 0)
-    finish(subs - 1)
+    lax.fori_loop(0, subs + 1, step, 0)
     h1_o, qkv_o, o_o, h2_o, u_o, a_o, x_o = outs(subs - 1)
     for copy in (h1_o, qkv_o, o_o, h2_o, u_o, a_o):
         copy.wait()
@@ -261,9 +292,9 @@
 
 
 def bwd_kernel(subs, stages, width, tile,
-               dy_in, x_all, mid_all, u_all, qkv_all, w2t_h, w1t_h, wot_h, wqt_h, ln,
+               dy_in, x_all, mid_all, u_all, qkv_all, w2t_h, w1t_h, wot_h, wot_p, wqt_h, wqt_p, ln,
                dy_all, dpre_all, gmid_all, dqkv_all, gin_all, part_all, db1, db2, dbo, dbq, dln,
-               w2t, w1t, wot, wqt, dyb, ub, dpb, partb, rb, midb, xb, gmb, qkvb, gib,
+               w2t, w1t, wot, wqt, dyb, ub, dpb, partb, rb, midb, xb, gmb, qkvb, gib, sb, db, pb, dsb,
                w_sem, in_sem, pre_sem, out_sem, dy_sem, gi_sem, part_send, part_recv, gi_send, dy_recv):
     stage = lax.axis_index("pp")
     tp_me = lax.axis_index("tp")
@@ -273,8 +304,14 @@
     half = d_model // 2
     ff = ub.shape[1]
     scale = width ** -0.5
-
-    loads = [pltpu.make_async_copy(src, dst, w_sem.at[i]) for i, (src, dst) in enumerate(((w2t_h, w2t), (w1t_h, w1t), (wot_h, wot), (wqt_h, wqt)))]
+    log2_scale = scale * LOG2_E
+
+    mine = pl.ds(pl.multiple_of(tp_me * half, 128), half)
+    theirs = pl.ds(pl.multiple_of(tp_peer * half, 128), half)
+    mine_q = pl.ds(pl.multiple_of(tp_me * (3 * half), 128), 3 * half)
+    theirs_q = pl.ds(pl.multiple_of(tp_peer * (3 * half), 128), 3 * half)
+    loads = [pltpu.make_async_copy(src, dst, w_sem.at[i]) for i, (src, dst) in enumerate((
+        (w2t_h, w2t), (w1t_h, w1t), (wot_h, wot.at[:, mine]), (wot_p, wot.at[:, theirs]), (wqt_h, wqt.at[mine_q, :]), (wqt_p, wqt.at[theirs_q, :])))]
     for load in loads:
         load.start()
 
@@ -288,6 +325,8 @@
         copy.start()
     for acc in (db1, db2, dbo, dbq, dln):
         acc[...] = jnp.zeros_like(acc)
+    for acc in (pb, dsb):
+        acc[:, 128:rows, 0:128] = jnp.zeros((4, rows - 128, 128), BF16)
     neighbour_barrier(stage, tp_peer, stages)
 
     def outs(m):
@@ -375,52 +414,55 @@
             partb[slot, :, n:n + tile] = dot_nn(dpb[...], w1t[:, n:n + tile]).astype(BF16)
         part_copy(m).start()
 
-    def attend_grad(group, carry):
-        base = pl.multiple_of((group // 2) * (3 * half) + lax.rem(group, 2) * (4 * width), 128)
-        do_base = pl.multiple_of(group * (4 * width), 128)
-        key_rows = rows
-        d_query = [[], []]
-        d_key, d_value = [], []
-        for start, size, offset in WINDOWS:
-            dk_sum = dv_sum = None
-            for blk in range(rows // 128):
-                r0, keys = blk * 128, (blk + 1) * 128
-                query = qkvb[r0:r0 + 128, pl.ds(base + start, size)]
-                d_out = rb[r0:r0 + 128, pl.ds(do_base + start, size)]
-                key = qkvb[0:keys, pl.ds(base + half + start, size)]
-                value = qkvb[0:keys, pl.ds(base + 2 * half + start, size)]
-                krow = lax.broadcasted_iota(jnp.int32, (keys, 128), 0)
-                qcol = lax.broadcasted_iota(jnp.int32, (keys, 128), 1) + r0
-                score = jnp.where(qcol >= krow, dot_nt(key, head_only(query, offset, width)) * scale, NEG)
-                weight = jnp.exp(score - jnp.max(score, axis=0, keepdims=True))
-                prob = weight * (1.0 / jnp.sum(weight, axis=0, keepdims=True))
-                d_prob = dot_nt(value, head_only(d_out, offset, width))
-                d_score = prob * (d_prob - jnp.sum(prob * d_prob, axis=0, keepdims=True))
-                d_score = d_score.astype(BF16)
-                d_query[blk].append(dot_tn(d_score, key) * scale)
-                dk_new = dot_nn(d_score, query) * scale
-                dv_new = dot_nn(prob.astype(BF16), d_out)
-                if keys < key_rows:
-                    rest = jnp.zeros((key_rows - keys, size), F32)
-                    dk_new = jnp.concatenate([dk_new, rest], axis=0)
-                    dv_new = jnp.concatenate([dv_new, rest], axis=0)
-                dk_sum = dk_new if dk_sum is None else dk_sum + dk_new
-                dv_sum = dv_new if dv_sum is None else dv_sum + dv_new
-            d_key.append(dk_sum)
-            d_value.append(dv_sum)
-        for blk in range(rows // 128):
-            for i, piece in enumerate(join_heads(d_query[blk], width)):
-                piece = piece.astype(BF16)
-                lanes = pl.ds(base + i * 128, 128)
-                qkvb[blk * 128:(blk + 1) * 128, lanes] = piece
-                dbq[:, lanes] += fold_rows(piece.astype(F32))
-        for c, parts in ((1, d_key), (2, d_value)):
-            for i, piece in enumerate(join_heads(parts, width)):
-                piece = piece.astype(BF16)
-                lanes = pl.ds(base + c * half + i * 128, 128)
-                qkvb[:, lanes] = piece
-                dbq[:, lanes] += fold_rows(piece.astype(F32))
-        return carry
+    def attend_grad():
+        def window(base, spec):
+            start, size, offset = spec
+            return slice(base + start, base + start + size), offset
+
+        def scores(group, base):
+            for j, spec in enumerate(WINDOWS):
+                q_lanes, offset = window(base, spec)
+                k_lanes, _ = window(base + half, spec)
+                v_lanes, _ = window(base + 2 * half, spec)
+                d_lanes, _ = window(group * (4 * width), spec)
+                sb[j] = dot_nt(qkvb[:, k_lanes], head_only(qkvb[:, q_lanes], offset, width))
+                db[j] = dot_nt(qkvb[:, v_lanes], head_only(rb[:, d_lanes], offset, width))
+
+        def softmax():
+            for j in range(4):
+                for q0 in range(0, rows, 128):
+                    keys, lanes = q0 + 128, slice(q0, q0 + 128)
+                    krow = lax.broadcasted_iota(jnp.int32, (keys, 128), 0)
+                    qcol = lax.broadcasted_iota(jnp.int32, (keys, 128), 1) + q0
+                    score = jnp.where(qcol >= krow, sb[j, 0:keys, lanes], NEG)
+                    weight = jnp.exp2((score - jnp.max(score, axis=0, keepdims=True)) * log2_scale)
+                    prob = weight * (1.0 / jnp.sum(weight, axis=0, keepdims=True))
+                    pb[j, 0:keys, lanes] = prob.astype(BF16)
+                    d_prob = db[j, 0:keys, lanes]
+                    d_score = prob * (d_prob - jnp.sum(prob * d_prob, axis=0, keepdims=True))
+                    dsb[j, 0:keys, lanes] = d_score.astype(BF16)
+
+        def products(group, base):
+            d_query, d_key, d_value = [], [], []
+            for j, spec in enumerate(WINDOWS):
+                q_lanes, _ = window(base, spec)
+                k_lanes, _ = window(base + half, spec)
+                d_lanes, _ = window(group * (4 * width), spec)
+                d_value.append(dot_nn(pb[j], rb[:, d_lanes]))
+                d_key.append(dot_nn(dsb[j], qkvb[:, q_lanes]) * scale)
+                d_query.append(dot_tn(dsb[j], qkvb[:, k_lanes]) * scale)
+            for c, parts in enumerate((d_query, d_key, d_value)):
+                for i, piece in enumerate(join_heads(parts, width)):
+                    piece = piece.astype(BF16)
+                    first = base + c * half + i * 128
+                    qkvb[:, first:first + 128] = piece
+                    dbq[:, first:first + 128] += fold_rows(piece.astype(F32))
+
+        for group in range(d_model // (4 * width)):
+            base = (group // 2) * (3 * half) + (group % 2) * (4 * width)
+            scores(group, base)
+            softmax()
+            products(group, base)
 
     def attn_part(m):
         slot = lax.rem(m, 2)
@@ -437,8 +479,8 @@
 
         @pl.when(m == 0)
         def _():
-            loads[2].wait()
-            loads[3].wait()
+            for load in loads[2:]:
+                load.wait()
 
         load.wait()
         for r in range(0, rows, ROW_CHUNK):
@@ -456,7 +498,7 @@
         for n in range(0, d_model, tile):
             rb[:, n:n + tile] = dot_nn(gmb[...], wot[:, n:n + tile]).astype(BF16)
         qkv_f.wait()
-        lax.fori_loop(0, d_model // (4 * width), attend_grad, 0)
+        attend_grad()
         dq_o.start()
         part_copy(m).wait_send()
         for n in range(0, d_model, tile):
@@ -488,8 +530,10 @@
             fetch(m + 1)[2].start()
             fetch(m + 1)[3].start()
 
-    def one_sub(m, carry):
-        mlp_part(m)
+    def step(m, carry):
+        @pl.when(m < subs)
+        def _():
+            mlp_part(m)
 
         @pl.when(m > 0)
         def _():
@@ -497,8 +541,7 @@
 
         return carry
 
-    lax.fori_loop(0, subs, one_sub, 0)
-    attn_part(subs - 1)
+    lax.fori_loop(0, subs + 1, step, 0)
     for copy in outs(subs - 1)[:2]:
         copy.wait()
     for m in (subs - 2, subs - 1):
@@ -519,7 +562,7 @@
 VMEM_LIMIT = 67043328
 
 
-def fwd_call(stages, width, tile, x_in, wq, wo, w1, w2, bq, bo, ln, b1, b2):
+def fwd_call(stages, width, tile, x_in, wq_own, wq_peer, wo_own, wo_peer, w1, w2, bq, bo, ln, b1, b2):
     subs, rows, d_model = x_in.shape
     ff = w1.shape[1]
     half = d_model // 2
@@ -538,19 +581,20 @@
         functools.partial(fwd_kernel, subs, stages, width, tile),
         name="fwd_stage",
         out_shape=(hbm(d_model), hbm(3 * d_model), hbm(half), hbm(d_model), hbm(d_model), hbm(d_model), hbm(ff, F32), hbm(ff), hbm(d_model), hbm(d_model)),
-        in_specs=[ANY] * 5 + [VMEM] * 5,
+        in_specs=[ANY] * 7 + [VMEM] * 5,
         out_specs=[ANY] * 10,
         scratch_shapes=[
-            pltpu.VMEM(wq.shape, BF16), pltpu.VMEM(wo.shape, BF16), pltpu.VMEM(w1.shape, BF16), pltpu.VMEM(w2.shape, BF16),
+            pltpu.VMEM((d_model, 3 * d_model), BF16), pltpu.VMEM((d_model, d_model), BF16), pltpu.VMEM(w1.shape, BF16), pltpu.VMEM(w2.shape, BF16),
             buf(d_model), buf(d_model), buf(3 * d_model), buf(d_model), two(d_model), buf(d_model), buf(ff, F32), buf(ff), two(d_model), buf(d_model), two(d_model),
-            DMA((4,)), DMA, DMA((7,)), DMA((2,)), DMA((2,)), DMA((2,)), DMA((subs,)), DMA((2,)), DMA((subs,)),
+            pltpu.VMEM((2, 4, rows, rows), F32), pltpu.VMEM((2, 4, rows, rows), BF16),
+            DMA((6,)), DMA, DMA((7,)), DMA((2,)), DMA((2,)), DMA((2,)), DMA((subs,)), DMA((2,)), DMA((subs,)),
         ],
         cost_estimate=pl.CostEstimate(flops=subs * rows * weights, bytes_accessed=weights + subs * rows * d_model * 30, transcendentals=subs * rows * (ff + rows * 16)),
         compiler_params=pltpu.CompilerParams(collective_id=0, has_side_effects=True, vmem_limit_bytes=VMEM_LIMIT),
-    )(x_in, wq, wo, w1, w2, bq, bo, ln, b1, b2)
-
-
-def bwd_call(stages, width, tile, dy_in, x_all, mid_all, u_all, qkv_all, w2t, w1t, wot, wqt, ln):
+    )(x_in, wq_own, wq_peer, wo_own, wo_peer, w1, w2, bq, bo, ln, b1, b2)
+
+
+def bwd_call(stages, width, tile, dy_in, x_all, mid_all, u_all, qkv_all, w2t, w1t, wot_own, wot_peer, wqt_own, wqt_peer, ln):
     subs, rows, d_model = dy_in.shape
     ff = u_all.shape[2]
     half = d_model // 2
@@ -573,16 +617,17 @@
         name="bwd_stage",
         out_shape=(hbm(d_model), hbm(ff), hbm(d_model), hbm(3 * half), hbm(d_model), hbm(d_model),
                    acc(8, ff), acc(8, d_model), acc(8, d_model), acc(8, 3 * d_model), acc(4, 8, d_model)),
-        in_specs=[ANY] * 9 + [VMEM],
+        in_specs=[ANY] * 11 + [VMEM],
         out_specs=[ANY] * 6 + [VMEM] * 5,
         scratch_shapes=[
-            pltpu.VMEM(w2t.shape, BF16), pltpu.VMEM(w1t.shape, BF16), pltpu.VMEM(wot.shape, BF16), pltpu.VMEM(wqt.shape, BF16),
+            pltpu.VMEM(w2t.shape, BF16), pltpu.VMEM(w1t.shape, BF16), pltpu.VMEM((d_model, d_model), BF16), pltpu.VMEM((3 * d_model, d_model), BF16),
             two(d_model), buf(ff, F32), buf(ff), two(d_model), buf(d_model), buf(d_model), buf(d_model), buf(d_model), buf(3 * d_model), two(d_model),
-            DMA((4,)), DMA, DMA((4,)), DMA((3,)), DMA((2,)), DMA((2,)), DMA((2,)), DMA((subs,)), DMA((2,)), DMA((subs,)),
+            pltpu.VMEM((4, rows, rows), F32), pltpu.VMEM((4, rows, rows), F32), pltpu.VMEM((4, rows, rows), BF16), pltpu.VMEM((4, rows, rows), BF16),
+            DMA((6,)), DMA, DMA((4,)), DMA((3,)), DMA((2,)), DMA((2,)), DMA((2,)), DMA((subs,)), DMA((2,)), DMA((subs,)),
         ],
         cost_estimate=pl.CostEstimate(flops=subs * rows * weights, bytes_accessed=weights + subs * rows * d_model * 30, transcendentals=subs * rows * (ff + rows * 16)),
         compiler_params=pltpu.CompilerParams(collective_id=1, has_side_effects=True, vmem_limit_bytes=VMEM_LIMIT),
-    )(dy_in, x_all, mid_all, u_all, qkv_all, w2t, w1t, wot, wqt, ln)
+    )(dy_in, x_all, mid_all, u_all, qkv_all, w2t, w1t, wot_own, wot_peer, wqt_own, wqt_peer, ln)
 
 
 def solution(mesh):
@@ -597,30 +642,28 @@
         tile = half
         tp_me = lax.axis_index("tp")
 
-        def both_halves(own, axis):
-            other = lax.ppermute(own, "tp", swap)
-            first = jnp.where(tp_me == 0, own, other)
-            second = jnp.where(tp_me == 0, other, own)
-            return jnp.concatenate([first, second], axis=axis)
-
-        wq_own = jnp.transpose(w_qkv[0].reshape(3, d_model, half), (1, 0, 2)).reshape(d_model, 3 * half)
-        wq = both_halves(wq_own, 1)
-        wo = both_halves(w_out[0].reshape(half, d_model), 0)
-        bq = both_halves(b_qkv[0].reshape(1, 3 * half), 1).astype(F32)
+        wqt_own = jnp.transpose(w_qkv[0], (0, 2, 3, 1)).reshape(3 * half, d_model)
+        wqt_peer = lax.ppermute(wqt_own, "tp", swap)
+        wo_own = w_out[0].reshape(half, d_model)
+        wo_peer = lax.ppermute(wo_own, "tp", swap)
+        bq_own = b_qkv[0].reshape(1, 3 * half)
+        bq_peer = lax.ppermute(bq_own, "tp", swap)
+        bq = jnp.concatenate([jnp.where(tp_me == 0, bq_own, bq_peer), jnp.where(tp_me == 0, bq_peer, bq_own)], axis=1).astype(F32)
         w1, w2 = w_fc1[0], w_fc2[0]
         ln = ln_par[0].astype(F32)
         x_all, qkv_all, o_all, mid_all, h1_all, h2_all, u_all, a_all, y_all, _ = fwd_call(
-            stages, width, tile, x_in.reshape(subs, rows, d_model), wq, wo, w1, w2, bq, b_out.astype(F32), ln, b_fc1.astype(F32), b_fc2.astype(F32))
+            stages, width, tile, x_in.reshape(subs, rows, d_model), wqt_own.T, wqt_peer.T, wo_own, wo_peer, w1, w2, bq, b_out.astype(F32), ln, b_fc1.astype(F32), b_fc2.astype(F32))
         dy_all, dpre_all, gmid_all, dqkv_all, gin_all, _, db1, db2, dbo, dbq, dln = bwd_call(
-            stages, width, tile, dy_out.reshape(subs, rows, d_model), x_all, mid_all, u_all, qkv_all, w2.T, w1.T, wo.T, wq.T, ln)
+            stages, width, tile, dy_out.reshape(subs, rows, d_model), x_all, mid_all, u_all, qkv_all, w2.T, w1.T, wo_own.T, wo_peer.T, wqt_own, wqt_peer, ln)
 
         def weight_grad(left, right):
-            return lax.dot_general(left.reshape(subs * rows, -1), right.reshape(subs * rows, -1), (((0,), (0,)), ((), ())), preferred_element_type=F32)
+            product = dot_tn(left.reshape(subs * rows, -1), right.reshape(subs * rows, -1))
+            return lax.optimization_barrier(product)
 
         g_w_fc2 = weight_grad(a_all, dy_all)
         g_w_fc1 = weight_grad(h2_all, dpre_all)
         g_w_out = weight_grad(o_all, gmid_all).reshape(heads, width, d_model)
-        g_w_qkv = jnp.transpose(weight_grad(h1_all, dqkv_all).reshape(d_model, 3, heads, width), (1, 0, 2, 3))
+        g_w_qkv = jnp.transpose(weight_grad(dqkv_all, h1_all).reshape(3, heads, width, d_model), (0, 3, 1, 2))
         g_b_qkv = lax.dynamic_slice_in_dim(jnp.sum(dbq, axis=0), tp_me * (3 * half), 3 * half).reshape(3, heads, width)
         act = (1, micro, batch, rows, d_model)
         return (y_all.reshape(act), gin_all.reshape(act), g_w_qkv[None], g_b_qkv[None], g_w_out[None], jnp.sum(dbo, axis=0)[None],

time: 2200 us -> 1690 us (0.77)
  Pallas kernels: 1640 us -> 1210 us
  local copies, waits for them, and re-layouts: 131 us -> 88.9 us
  other arithmetic: 37.8 us -> 7.23 us
    pallas_call x1, Pallas kernels: 1040 us -> 769 us  [bwd_call(): pl.pallas_call(functools.partial(bwd_kernel, subs, stages, width, tile),...]
    pallas_call x1, Pallas kernels: 599 us -> 438 us  [fwd_call(): pl.pallas_call(functools.partial(fwd_kernel, subs, stages, width, tile),...]
    dot_general x2 -> x0, local copies, waits for them, and re-layouts: 49.4 us -> none  [weight_grad(): lax.dot_general(left.reshape(subs * rows, -1), right.reshape(subs * rows,...]
    concatenate x2 -> x0, local copies, waits for them, and re-layouts: 25.2 us -> none  [both_halves(): return jnp.concatenate([first, second], axis=axis)]
    transpose x2 -> x0, other arithmetic: 22.8 us -> none  [stage_program(): dy_all, dpre_all, gmid_all, dqkv_all, gin_all, _, db1, db2, dbo, dbq, dln...]
  transfers between devices with their start and end apart: 3 -> 3, of which waited for: 1 -> 1; matrix products, arithmetic and copies ran while one was open for 2% -> 3% of each run, Pallas kernels for 0% -> 0%
where the time goes in v2:
time: 1690 us; the launch traced here: 1680 us
  Pallas kernels  1210 us (72%)
  matrix products  215 us (13%)
  waiting for transfers between devices  157 us (9%)
  local copies, waits for them, and re-layouts  88.9 us (5%)
    pallas_call x1, Pallas kernels, bwd_call(): pl.pallas_call(functools.partial(bwd_kernel, subs, stages, width, tile),...  769 us
    pallas_call x1, Pallas kernels, fwd_call(): pl.pallas_call(functools.partial(fwd_kernel, subs, stages, width, tile),...  438 us
    dot_general x4, matrix products, dot_tn(): lax.dot_general(lhs, rhs, (((0,), (0,)), ((), ())), preferred_element_typ...  215 us
    ppermute x1, waiting for transfers between devices, stage_program(): bq_peer = lax.ppermute(bq_own, 'tp', swap)  157 us
    unnamed x16, local copies, waits for them, and re-layouts  58.5 us
  transfers between devices with their start and end apart: 3, of which 1 were waited for; matrix products, arithmetic and copies ran while one was open for 3% of the time, Pallas kernels for 0%

profile of v2, /device:TPU:0, one launch (start us, length us, event | category | flops | bytes accessed | tf_op | source)
XLA Modules:
  0.0 1681.4 jit_solution(16305861834484774636)
XLA Ops:
  0.6 3.4 collective-permute-start
  4.0 2.8 copy.35
  6.9 0.0 copy-start
  6.9 0.0 collective-permute-start.1
  6.9 0.8 reshape_squeeze.7
  7.7 2.0 collective-permute-start.2
  9.7 1.3 bitcast_convert_fusion.ln
  11.1 1.3 convert_element_type.18.bo
  12.3 1.3 convert_element_type.22.b2
  13.6 1.3 convert_element_type.21.b1
  15.0 10.3 copy.38.wq_h
  25.2 12.6 copy.36
  37.8 12.6 copy.37
  50.4 156.7 %collective-permute-done.2 = bf16[1,2304]{1,0:T(2,128)(2,1)S(1)} collective-permute-done((bf16[1,2304]{1,0:T(2,128)(2,1)S(1)}, bf16[1,2304]{1,0:T(2,128)(2,1)S(1)}, u32[]{:S(2)}, u32[]{:S(2)}) %collective-permute-start.2) | collective-permute-done | bytes 4640 | tf_op jit(solution)/shard_map/ppermute | solution.py:650
  207.2 0.6 maximum_convert_fusion.bq
  207.8 0.0 collective-permute-done.1
  207.8 4.3 copy.40.wo_p
  212.1 10.3 copy.39.wq_p
  222.3 437.5 %fwd_stage.1 = (bf16[24,256,1536]{2,1,0:T(8,128)(2,1)}, bf16[24,256,4608]{2,1,0:T(8,128)(2,1)}, bf16[24,256,768]{2,1,0:T(8,128)(2,1)}, bf16[24,256,1536]{2,1,0:T...) custom-call(bf16[24,256,1536]{2,1,0:T(8,128)(2,1)} %bitcast.68, ...), custom_call_target="tpu_custom_call" | custom-call | flops 231928233984 | bytes 320864256 | tf_op jit(solution)/shard_map/fwd_stage/pallas_call | solution.py:580
  659.9 769.2 %bwd_stage.1 = (bf16[24,256,1536]{2,1,0:T(8,128)(2,1)}, bf16[24,256,3072]{2,1,0:T(8,128)(2,1)}, bf16[24,256,1536]{2,1,0:T(8,128)(2,1)}, bf16[24,256,2304]{2,1,0:...) custom-call(bf16[24,256,1536]{2,1,0:T(8,128)(2,1)} %bitcast.69, ...), custom_call_target="tpu_custom_call" | custom-call | flops 231928233984 | bytes 320864256 | tf_op jit(solution)/shard_map/bwd_stage/pallas_call | solution.py:615
  1429.1 70.0 %convolution_bitcast_fusion = f32[3072,1536]{1,0:T(8,128)} fusion(bf16[24,256,3072]{2,1,0:T(8,128)(2,1)} %get-tuple-element.46, bf16[24,256,1536]{2,1,0:T(8,128)(2,1)} %get-tuple-element.47), kind=kOutput, calls=%fused_computation | convolution fusion | flops 57982058496 | bytes 75497472 | tf_op jit(solution)/shard_map/dot_general | solution.py:33
  1499.1 69.5 %convolution_bitcast_fusion.1 = f32[1536,3072]{1,0:T(8,128)} fusion(bf16[24,256,1536]{2,1,0:T(8,128)(2,1)} %get-tuple-element.43, bf16[24,256,3072]{2,1,0:T(8,128)(2,1)} %get-tuple-element.44), kind=kOutput, calls=%fused_computation.1 | convolution fusion | flops 57982058496 | bytes 75497472 | tf_op jit(solution)/shard_map/dot_general | solution.py:33
  1568.6 21.4 %convolution_bitcast_fusion.3 = f32[768,1536]{1,0:T(8,128)} fusion(bf16[24,256,768]{2,1,0:T(8,128)(2,1)} %get-tuple-element.39, bf16[24,256,1536]{2,1,0:T(8,128)(2,1)} %get-tuple-element.40), kind=kOutput, calls=%fused_computation.3 | convolution fusion | flops 14495514624 | bytes 33030144 | tf_op jit(solution)/shard_map/dot_general | solution.py:33
  1590.0 54.6 %convolution_bitcast_fusion.2 = f32[2304,1536]{1,0:T(8,128)} fusion(bf16[24,256,2304]{2,1,0:T(8,128)(2,1)} %get-tuple-element.36, bf16[24,256,1536]{2,1,0:T(8,128)(2,1)} %get-tuple-element.37), kind=kOutput, calls=%fused_computation.2 | convolution fusion | flops 43486543872 | bytes 61341696 | tf_op jit(solution)/shard_map/dot_general | solution.py:33
  1644.6 0.6 broadcast_in_dim.22
  1645.3 0.6 broadcast_in_dim.27
  1645.9 0.6 reduce_sum.48
  1646.5 0.7 reduce_sum.47
  1647.2 0.1 dynamic_slice.3
  1647.3 0.7 broadcast_in_dim_reshape.6
  1648.0 16.6 copy.56
  1664.6 16.6 copy.57
  (16 shorter events, 0.1 us)
Async XLA Ops:
  0.6 211.4 %collective-permute-start = (bf16[2304,1536]{1,0:T(8,128)(2,1)}, bf16[2304,1536]{1,0:T(8,128)(2,1)}, u32[]{:S(2)}, u32[]{:S(2)}) collective-permute-start(bf16[2304,1536]{1,0:T(8,128)(2,1)} %bitcast.60), channel_id=1, source_target_pairs={{0,4},{4,0},{1,5},{5,1},{2,6},{6,2},{3,7},{7,3}} | collective-permute-start | bytes 21233672 | tf_op jit(solution)/shard_map/ppermute | solution.py:646
  6.9 43.5 %copy-start = (bf16[768,1536]{0,1:T(8,128)(2,1)}, bf16[768,1536]{0,1:T(8,128)(2,1)S(1)}, u32[]{:S(2)}) copy-start(bf16[768,1536]{0,1:T(8,128)(2,1)S(1)} %copy.35) | copy-start | bytes 7077892
  6.9 200.9 %collective-permute-start.1 = (bf16[768,1536]{0,1:T(8,128)(2,1)S(1)}, bf16[768,1536]{0,1:T(8,128)(2,1)}, u32[]{:S(2)}, u32[]{:S(2)}) collective-permute-start(bf16[768,1536]{0,1:T(8,128)(2,1)S(1)} %copy.35), channel_id=1, source_target_pairs={{0,4},{4,0},{1,5},{5,1},{2,6},{6,2},{3,7},{7,3}} | collective-permute-start | bytes 7077896 | tf_op jit(solution)/shard_map/ppermute | solution.py:648
  7.7 199.4 %collective-permute-start.2 = (bf16[1,2304]{1,0:T(2,128)(2,1)S(1)}, bf16[1,2304]{1,0:T(2,128)(2,1)S(1)}, u32[]{:S(2)}, u32[]{:S(2)}) collective-permute-start(bf16[1,2304]{1,0:T(2,128)(2,1)S(1)} %reshape_squeeze.7), channel_id=1, source_target_pairs={{0,4},{4,0},{1,5},{5,1},{2,6},{6,2},{3,7},{7,3}} | collective-permute-start | bytes 13832 | tf_op jit(solution)/shard_map/ppermute | solution.py:650
  1590.0 54.6 %copy-start.5 = (f32[8,1536]{1,0:T(8,128)S(1)}, f32[8,1536]{1,0:T(8,128)}, u32[]{:S(2)}) copy-start(f32[8,1536]{1,0:T(8,128)} %get-tuple-element.41) | copy-start | bytes 147460
  1590.0 55.2 %copy-start.4 = (f32[8,1536]{1,0:T(8,128)S(1)}, f32[8,1536]{1,0:T(8,128)}, u32[]{:S(2)}) copy-start(f32[8,1536]{1,0:T(8,128)} %get-tuple-element.48) | copy-start | bytes 147460
  1590.0 55.8 %copy-start.3 = (f32[8,3072]{1,0:T(8,128)S(1)}, f32[8,3072]{1,0:T(8,128)}, u32[]{:S(2)}) copy-start(f32[8,3072]{1,0:T(8,128)} %get-tuple-element.45) | copy-start | bytes 294916
  1590.0 56.5 %copy-start.2 = (f32[8,4608]{1,0:T(8,128)S(1)}, f32[8,4608]{1,0:T(8,128)}, u32[]{:S(2)}) copy-start(f32[8,4608]{1,0:T(8,128)} %get-tuple-element.38) | copy-start | bytes 442372
  1590.0 56.5 %copy-start.1 = (f32[4,8,1536]{2,1,0:T(8,128)S(1)}, f32[4,8,1536]{2,1,0:T(8,128)}, u32[]{:S(2)}) copy-start(f32[4,8,1536]{2,1,0:T(8,128)} %get-tuple-element.42) | copy-start | bytes 589828

commit v3 on v2

--- a/solution.py
+++ b/solution.py
@@ -17,6 +17,7 @@
 GELU_K = 0.044715
 LOG2_E = 1.4426950408889634
 SOFT_ROWS = 64
+RING = 4
 
 WINDOWS = ((0, 128, 0), (0, 256, 96), (128, 256, 64), (256, 128, 32))
 
@@ -67,8 +68,8 @@
 
 def fwd_kernel(subs, stages, width, tile,
                x_in, wq_h, wq_p, wo_h, wo_p, w1_h, w2_h, bq, bo, ln, b1, b2,
-               x_all, qkv_all, o_all, mid_all, h1_all, h2_all, u_all, a_all, y_all, part_all,
-               wq, wo, w1, w2, xb, h1b, qkvb, ob, midb, h2b, ub, ab, partb, rb, yb, sb, pb,
+               x_all, qkv_all, o_all, mid_all, h1_all, h2_all, s_all, a_all, y_all,
+               wq, wo, w1, w2, xb, h1b, qkvb, ob, midb, h2b, slb, ab, partb, peerb, yb, sb, pb,
                w_sem, in_sem, out_sem, mid_sem, y_sem, part_send, part_recv, y_send, x_recv):
     stage = lax.axis_index("pp")
     tp_me = lax.axis_index("tp")
@@ -76,7 +77,7 @@
     last_stage = stages - 1
     rows, d_model = xb.shape
     half = d_model // 2
-    ff = ub.shape[1]
+    ff = slb.shape[1]
     scale = width ** -0.5
     log2_scale = scale * LOG2_E
 
@@ -96,7 +97,7 @@
                 pltpu.make_async_copy(qkvb, qkv_all.at[m], out_sem.at[1]),
                 pltpu.make_async_copy(ob.at[:, pl.ds(pl.multiple_of(tp_me * half, 128), half)], o_all.at[m], out_sem.at[2]),
                 pltpu.make_async_copy(h2b, h2_all.at[m], out_sem.at[3]),
-                pltpu.make_async_copy(ub, u_all.at[m], out_sem.at[4]),
+                pltpu.make_async_copy(slb, s_all.at[m], out_sem.at[4]),
                 pltpu.make_async_copy(ab, a_all.at[m], out_sem.at[5]),
                 pltpu.make_async_copy(xb, x_all.at[m], out_sem.at[6]))
 
@@ -110,7 +111,7 @@
 
     def part_copy(m):
         slot = lax.rem(m, 2)
-        return pltpu.make_async_remote_copy(src_ref=partb.at[slot], dst_ref=part_all.at[m], send_sem=part_send.at[slot], recv_sem=part_recv.at[m],
+        return pltpu.make_async_remote_copy(src_ref=partb.at[slot], dst_ref=peerb.at[lax.rem(m, RING)], send_sem=part_send.at[slot], recv_sem=part_recv.at[m],
                                             device_id={"tp": tp_peer}, device_id_type=MESH)
 
     def next_copy(m):
@@ -162,9 +163,8 @@
 
     def finish(m):
         slot = lax.rem(m, 2)
+        peer_slot = lax.rem(m, RING)
         part_copy(m).wait_recv()
-        load = pltpu.make_async_copy(part_all.at[m], rb, in_sem)
-        load.start()
 
         @pl.when(m >= 2)
         def _():
@@ -174,9 +174,8 @@
             def _():
                 next_copy(m - 2).wait_send()
 
-        load.wait()
         for r in range(0, rows, ROW_CHUNK):
-            both = partb[slot, r:r + ROW_CHUNK, :].astype(F32) + rb[r:r + ROW_CHUNK, :].astype(F32)
+            both = partb[slot, r:r + ROW_CHUNK, :].astype(F32) + peerb[peer_slot, r:r + ROW_CHUNK, :].astype(F32)
             yb[slot, r:r + ROW_CHUNK, :] = (midb[slot, r:r + ROW_CHUNK, :].astype(F32) + both + b2[...]).astype(BF16)
 
         @pl.when(stage < last_stage)
@@ -189,8 +188,8 @@
     def one_sub(m):
         slot = lax.rem(m, 2)
         prev = jnp.maximum(m - 1, 0)
-        h1_o, qkv_o, o_o, h2_o, u_o, a_o, x_o = outs(m)
-        h1_p, qkv_p, o_p, h2_p, u_p, a_p, x_p = outs(prev)
+        h1_o, qkv_o, o_o, h2_o, s_o, a_o, x_o = outs(m)
+        h1_p, qkv_p, o_p, h2_p, s_p, a_p, x_p = outs(prev)
 
         @pl.when(stage == 0)
         def _():
@@ -248,15 +247,17 @@
 
         @pl.when(m > 0)
         def _():
-            u_p.wait()
+            s_p.wait()
             a_p.wait()
 
         for n in range(0, ff, tile):
             pre = dot_nn(h2b[...], w1[:, n:n + tile]) + b1[:, n:n + tile]
-            ub[:, n:n + tile] = pre
-            cdf = 0.5 * (1.0 + jnp.tanh(GELU_C * (pre + GELU_K * (pre * pre * pre))))
+            square = pre * pre
+            bend = jnp.tanh(pre * (GELU_C + (GELU_C * GELU_K) * square))
+            cdf = 0.5 + 0.5 * bend
             ab[:, n:n + tile] = (pre * cdf).astype(BF16)
-        u_o.start()
+            slb[:, n:n + tile] = cdf + (0.5 * pre) * (1.0 - bend * bend) * (GELU_C + (3.0 * GELU_C * GELU_K) * square)
+        s_o.start()
         a_o.start()
         for n in range(0, d_model, tile):
             partb[slot, :, n:n + tile] = dot_nn(ab[...], w2[:, n:n + tile]).astype(BF16)
@@ -274,8 +275,8 @@
         return carry
 
     lax.fori_loop(0, subs + 1, step, 0)
-    h1_o, qkv_o, o_o, h2_o, u_o, a_o, x_o = outs(subs - 1)
-    for copy in (h1_o, qkv_o, o_o, h2_o, u_o, a_o):
+    h1_o, qkv_o, o_o, h2_o, s_o, a_o, x_o = outs(subs - 1)
+    for copy in (h1_o, qkv_o, o_o, h2_o, s_o, a_o):
         copy.wait()
 
     @pl.when(stage == 0)
@@ -292,17 +293,17 @@
 
 
 def bwd_kernel(subs, stages, width, tile,
-               dy_in, x_all, mid_all, u_all, qkv_all, w2t_h, w1t_h, wot_h, wot_p, wqt_h, wqt_p, ln,
-               dy_all, dpre_all, gmid_all, dqkv_all, gin_all, part_all, db1, db2, dbo, dbq, dln,
-               w2t, w1t, wot, wqt, dyb, ub, dpb, partb, rb, midb, xb, gmb, qkvb, gib, sb, db, pb, dsb,
-               w_sem, in_sem, pre_sem, out_sem, dy_sem, gi_sem, part_send, part_recv, gi_send, dy_recv):
+               dy_in, x_all, mid_all, s_all, qkv_all, w2t_h, w1t_h, wot_h, wot_p, wqt_h, wqt_p, ln,
+               dy_all, dpre_all, gmid_all, dqkv_all, gin_all, db1, db2, dbo, dbq, dln,
+               w2t, w1t, wot, wqt, dyb, slb, dpb, partb, peerb, rb, midb, xb, gmb, qkvb, gib, sb, db, pb, dsb,
+               w_sem, in_sem, pre_sem, out_sem, dy_sem, gi_sem, part_send, part_recv, gi_send, dy_recv, dy_free):
     stage = lax.axis_index("pp")
     tp_me = lax.axis_index("tp")
     tp_peer = 1 - tp_me
     last_stage = stages - 1
     rows, d_model = xb.shape
     half = d_model // 2
-    ff = ub.shape[1]
+    ff = slb.shape[1]
     scale = width ** -0.5
     log2_scale = scale * LOG2_E
 
@@ -316,7 +317,7 @@
         load.start()
 
     def fetch(m):
-        return (pltpu.make_async_copy(u_all.at[m], ub, pre_sem.at[0]),
+        return (pltpu.make_async_copy(s_all.at[m], slb, pre_sem.at[0]),
                 pltpu.make_async_copy(mid_all.at[m], midb, pre_sem.at[1]),
                 pltpu.make_async_copy(qkv_all.at[m], qkvb, pre_sem.at[2]),
                 pltpu.make_async_copy(x_all.at[m], xb, pre_sem.at[3]))
@@ -334,9 +335,11 @@
                 pltpu.make_async_copy(gmb, gmid_all.at[m], out_sem.at[1]),
                 pltpu.make_async_copy(qkvb.at[:, pl.ds(pl.multiple_of(tp_me * (3 * half), 128), 3 * half)], dqkv_all.at[m], out_sem.at[2]))
 
+    def dy_load(m):
+        return pltpu.make_async_copy(dy_in.at[m], dyb.at[lax.rem(m, RING)], in_sem.at[lax.rem(m, 2)])
+
     def dy_out(m):
-        slot = lax.rem(m, 2)
-        return pltpu.make_async_copy(dyb.at[slot], dy_all.at[m], dy_sem.at[slot])
+        return pltpu.make_async_copy(dyb.at[lax.rem(m, RING)], dy_all.at[m], dy_sem.at[lax.rem(m, 2)])
 
     def gi_out(m):
         slot = lax.rem(m, 2)
@@ -344,13 +347,17 @@
 
     def part_copy(m):
         slot = lax.rem(m, 2)
-        return pltpu.make_async_remote_copy(src_ref=partb.at[slot], dst_ref=part_all.at[m], send_sem=part_send.at[slot], recv_sem=part_recv.at[m],
+        return pltpu.make_async_remote_copy(src_ref=partb.at[slot], dst_ref=peerb.at[lax.rem(m, RING)], send_sem=part_send.at[slot], recv_sem=part_recv.at[m],
                                             device_id={"tp": tp_peer}, device_id_type=MESH)
 
     def prev_copy(m):
         slot = lax.rem(m, 2)
-        return pltpu.make_async_remote_copy(src_ref=gib.at[slot], dst_ref=dy_all.at[m], send_sem=gi_send.at[slot], recv_sem=dy_recv.at[m],
+        return pltpu.make_async_remote_copy(src_ref=gib.at[slot], dst_ref=dyb.at[lax.rem(m, RING)], send_sem=gi_send.at[slot], recv_sem=dy_recv.at[m],
                                             device_id={"pp": jnp.maximum(stage - 1, 0)}, device_id_type=MESH)
+
+    @pl.when(stage == last_stage)
+    def _():
+        dy_load(0).start()
 
     def norm_grad(x_rows, grad, gain, which):
         normed, inv_std = norm_stats(x_rows)
@@ -363,25 +370,23 @@
 
     def mlp_part(m):
         slot = lax.rem(m, 2)
-        u_f = fetch(m)[0]
+        slope_f = fetch(m)[0]
+
+        dy_slot = lax.rem(m, RING)
 
         @pl.when(stage == last_stage)
         def _():
-            @pl.when(m >= 2)
+            dy_load(m).wait()
+
+            @pl.when(m + 1 < subs)
             def _():
-                dy_out(m - 2).wait()
-
-            load = pltpu.make_async_copy(dy_in.at[m], dyb.at[slot], in_sem)
-            load.start()
-            load.wait()
-            dy_out(m).start()
+                dy_load(m + 1).start()
 
         @pl.when(stage < last_stage)
         def _():
             prev_copy(m).wait_recv()
-            load = pltpu.make_async_copy(dy_all.at[m], dyb.at[slot], in_sem)
-            load.start()
-            load.wait()
+
+        dy_out(m).start()
 
         @pl.when(m == 0)
         def _():
@@ -392,16 +397,9 @@
         def _():
             outs(m - 1)[0].wait()
 
-        u_f.wait()
-        for r in range(0, rows, ROW_CHUNK):
-            db2[...] += fold_rows(dyb[slot, r:r + ROW_CHUNK, :].astype(F32))
+        slope_f.wait()
         for n in range(0, ff, tile):
-            grad = dot_nn(dyb[slot], w2t[:, n:n + tile]).astype(BF16).astype(F32)
-            pre = ub[:, n:n + tile]
-            square = pre * pre
-            bend = jnp.tanh(GELU_C * (pre + GELU_K * (square * pre)))
-            slope = 0.5 * (1.0 + bend) + (0.5 * GELU_C) * pre * (1.0 - bend * bend) * (1.0 + (3.0 * GELU_K) * square)
-            grad = grad * slope
+            grad = dot_nn(dyb[dy_slot], w2t[:, n:n + tile]).astype(BF16).astype(F32) * slb[:, n:n + tile]
             db1[:, n:n + tile] += fold_rows(grad)
             dpb[:, n:n + tile] = grad.astype(BF16)
         outs(m)[0].start()
@@ -468,9 +466,8 @@
         slot = lax.rem(m, 2)
         _, mid_f, qkv_f, x_f = fetch(m)
         _, gm_o, dq_o = outs(m)
-        part_copy(m).wait_recv()
-        load = pltpu.make_async_copy(part_all.at[m], rb, in_sem)
-        load.start()
+        peer_slot = lax.rem(m, RING)
+        dy_slot = lax.rem(m, RING)
         mid_f.wait()
 
         @pl.when(m > 0)
@@ -482,14 +479,21 @@
             for load in loads[2:]:
                 load.wait()
 
-        load.wait()
+        part_copy(m).wait_recv()
         for r in range(0, rows, ROW_CHUNK):
             rr = slice(r, r + ROW_CHUNK)
-            grad = (partb[slot, rr, :].astype(F32) + rb[rr, :].astype(F32)).astype(BF16).astype(F32)
-            total = dyb[slot, rr, :].astype(F32) + norm_grad(midb[rr, :].astype(F32), grad, ln[2:3, :], 2)
+            grad = (partb[slot, rr, :].astype(F32) + peerb[peer_slot, rr, :].astype(F32)).astype(BF16).astype(F32)
+            d_y = dyb[dy_slot, rr, :].astype(F32)
+            db2[...] += fold_rows(d_y)
+            total = d_y + norm_grad(midb[rr, :].astype(F32), grad, ln[2:3, :], 2)
             gmb[rr, :] = total.astype(BF16)
             dbo[...] += fold_rows(total)
         gm_o.start()
+        dy_out(m).wait()
+
+        @pl.when((stage < last_stage) & (m < subs - RING))
+        def _():
+            pl.semaphore_signal(dy_free, inc=1, device_id={"pp": jnp.minimum(stage + 1, last_stage)}, device_id_type=MESH)
 
         @pl.when(m + 1 < subs)
         def _():
@@ -520,6 +524,10 @@
 
         @pl.when(stage > 0)
         def _():
+            @pl.when(m >= RING)
+            def _():
+                pl.semaphore_wait(dy_free, 1)
+
             prev_copy(m).start()
 
         gi_out(m).start()
@@ -551,10 +559,6 @@
         def _():
             prev_copy(m).wait_send()
 
-        @pl.when(stage == last_stage)
-        def _():
-            dy_out(m).wait()
-
 
 ANY = pl.BlockSpec(memory_space=pl.ANY)
 VMEM = pl.BlockSpec(memory_space=pltpu.VMEM)
@@ -580,12 +584,12 @@
     return pl.pallas_call(
         functools.partial(fwd_kernel, subs, stages, width, tile),
         name="fwd_stage",
-        out_shape=(hbm(d_model), hbm(3 * d_model), hbm(half), hbm(d_model), hbm(d_model), hbm(d_model), hbm(ff, F32), hbm(ff), hbm(d_model), hbm(d_model)),
+        out_shape=(hbm(d_model), hbm(3 * d_model), hbm(half), hbm(d_model), hbm(d_model), hbm(d_model), hbm(ff, F32), hbm(ff), hbm(d_model)),
         in_specs=[ANY] * 7 + [VMEM] * 5,
-        out_specs=[ANY] * 10,
+        out_specs=[ANY] * 9,
         scratch_shapes=[
             pltpu.VMEM((d_model, 3 * d_model), BF16), pltpu.VMEM((d_model, d_model), BF16), pltpu.VMEM(w1.shape, BF16), pltpu.VMEM(w2.shape, BF16),
-            buf(d_model), buf(d_model), buf(3 * d_model), buf(d_model), two(d_model), buf(d_model), buf(ff, F32), buf(ff), two(d_model), buf(d_model), two(d_model),
+            buf(d_model), buf(d_model), buf(3 * d_model), buf(d_model), two(d_model), buf(d_model), buf(ff, F32), buf(ff), two(d_model), pltpu.VMEM((RING, rows, d_model), BF16), two(d_model),
             pltpu.VMEM((2, 4, rows, rows), F32), pltpu.VMEM((2, 4, rows, rows), BF16),
             DMA((6,)), DMA, DMA((7,)), DMA((2,)), DMA((2,)), DMA((2,)), DMA((subs,)), DMA((2,)), DMA((subs,)),
         ],
@@ -594,9 +598,9 @@
     )(x_in, wq_own, wq_peer, wo_own, wo_peer, w1, w2, bq, bo, ln, b1, b2)
 
 
-def bwd_call(stages, width, tile, dy_in, x_all, mid_all, u_all, qkv_all, w2t, w1t, wot_own, wot_peer, wqt_own, wqt_peer, ln):
+def bwd_call(stages, width, tile, dy_in, x_all, mid_all, s_all, qkv_all, w2t, w1t, wot_own, wot_peer, wqt_own, wqt_peer, ln):
     subs, rows, d_model = dy_in.shape
-    ff = u_all.shape[2]
+    ff = s_all.shape[2]
     half = d_model // 2
 
     def hbm(cols, dtype=BF16):
@@ -607,6 +611,8 @@
 
     def two(cols):
         return pltpu.VMEM((2, rows, cols), BF16)
+
+    ring = pltpu.VMEM((RING, rows, d_model), BF16)
 
     def acc(*shape):
         return jax.ShapeDtypeStruct(shape, F32)
@@ -615,19 +621,19 @@
     return pl.pallas_call(
         functools.partial(bwd_kernel, subs, stages, width, tile),
         name="bwd_stage",
-        out_shape=(hbm(d_model), hbm(ff), hbm(d_model), hbm(3 * half), hbm(d_model), hbm(d_model),
+        out_shape=(hbm(d_model), hbm(ff), hbm(d_model), hbm(3 * half), hbm(d_model),
                    acc(8, ff), acc(8, d_model), acc(8, d_model), acc(8, 3 * d_model), acc(4, 8, d_model)),
         in_specs=[ANY] * 11 + [VMEM],
-        out_specs=[ANY] * 6 + [VMEM] * 5,
+        out_specs=[ANY] * 5 + [VMEM] * 5,
         scratch_shapes=[
             pltpu.VMEM(w2t.shape, BF16), pltpu.VMEM(w1t.shape, BF16), pltpu.VMEM((d_model, d_model), BF16), pltpu.VMEM((3 * d_model, d_model), BF16),
-            two(d_model), buf(ff, F32), buf(ff), two(d_model), buf(d_model), buf(d_model), buf(d_model), buf(d_model), buf(3 * d_model), two(d_model),
+            ring, buf(ff, F32), buf(ff), two(d_model), ring, buf(d_model), buf(d_model), buf(d_model), buf(d_model), buf(3 * d_model), two(d_model),
             pltpu.VMEM((4, rows, rows), F32), pltpu.VMEM((4, rows, rows), F32), pltpu.VMEM((4, rows, rows), BF16), pltpu.VMEM((4, rows, rows), BF16),
-            DMA((6,)), DMA, DMA((4,)), DMA((3,)), DMA((2,)), DMA((2,)), DMA((2,)), DMA((subs,)), DMA((2,)), DMA((subs,)),
+            DMA((6,)), DMA((2,)), DMA((4,)), DMA((3,)), DMA((2,)), DMA((2,)), DMA((2,)), DMA((subs,)), DMA((2,)), DMA((subs,)), pltpu.SemaphoreType.REGULAR,
         ],
         cost_estimate=pl.CostEstimate(flops=subs * rows * weights, bytes_accessed=weights + subs * rows * d_model * 30, transcendentals=subs * rows * (ff + rows * 16)),
         compiler_params=pltpu.CompilerParams(collective_id=1, has_side_effects=True, vmem_limit_bytes=VMEM_LIMIT),
-    )(dy_in, x_all, mid_all, u_all, qkv_all, w2t, w1t, wot_own, wot_peer, wqt_own, wqt_peer, ln)
+    )(dy_in, x_all, mid_all, s_all, qkv_all, w2t, w1t, wot_own, wot_peer, wqt_own, wqt_peer, ln)
 
 
 def solution(mesh):
@@ -643,18 +649,18 @@
         tp_me = lax.axis_index("tp")
 
         wqt_own = jnp.transpose(w_qkv[0], (0, 2, 3, 1)).reshape(3 * half, d_model)
-        wqt_peer = lax.ppermute(wqt_own, "tp", swap)
         wo_own = w_out[0].reshape(half, d_model)
         wo_peer = lax.ppermute(wo_own, "tp", swap)
+        wqt_peer = lax.ppermute(wqt_own, "tp", swap)
         bq_own = b_qkv[0].reshape(1, 3 * half)
         bq_peer = lax.ppermute(bq_own, "tp", swap)
         bq = jnp.concatenate([jnp.where(tp_me == 0, bq_own, bq_peer), jnp.where(tp_me == 0, bq_peer, bq_own)], axis=1).astype(F32)
         w1, w2 = w_fc1[0], w_fc2[0]
         ln = ln_par[0].astype(F32)
-        x_all, qkv_all, o_all, mid_all, h1_all, h2_all, u_all, a_all, y_all, _ = fwd_call(
+        x_all, qkv_all, o_all, mid_all, h1_all, h2_all, s_all, a_all, y_all = fwd_call(
             stages, width, tile, x_in.reshape(subs, rows, d_model), wqt_own.T, wqt_peer.T, wo_own, wo_peer, w1, w2, bq, b_out.astype(F32), ln, b_fc1.astype(F32), b_fc2.astype(F32))
-        dy_all, dpre_all, gmid_all, dqkv_all, gin_all, _, db1, db2, dbo, dbq, dln = bwd_call(
-            stages, width, tile, dy_out.reshape(subs, rows, d_model), x_all, mid_all, u_all, qkv_all, w2.T, w1.T, wo_own.T, wo_peer.T, wqt_own, wqt_peer, ln)
+        dy_all, dpre_all, gmid_all, dqkv_all, gin_all, db1, db2, dbo, dbq, dln = bwd_call(
+            stages, width, tile, dy_out.reshape(subs, rows, d_model), x_all, mid_all, s_all, qkv_all, w2.T, w1.T, wo_own.T, wo_peer.T, wqt_own, wqt_peer, ln)
 
         def weight_grad(left, right):
             product = dot_tn(left.reshape(subs * rows, -1), right.reshape(subs * rows, -1))

time: 1690 us -> 1570 us (0.929)
  Pallas kernels: 1210 us -> 1080 us
    pallas_call x1, Pallas kernels: 769 us -> 649 us  [bwd_call(): pl.pallas_call(functools.partial(bwd_kernel, subs, stages, width, tile),...]
where the time goes in v3:
time: 1570 us; the launch traced here: 1560 us
  Pallas kernels  1080 us (69%)
  matrix products  215 us (14%)
  waiting for transfers between devices  157 us (10%)
  local copies, waits for them, and re-layouts  88.9 us (6%)
    pallas_call x1, Pallas kernels, bwd_call(): pl.pallas_call(functools.partial(bwd_kernel, subs, stages, width, tile),...  649 us
    pallas_call x1, Pallas kernels, fwd_call(): pl.pallas_call(functools.partial(fwd_kernel, subs, stages, width, tile),...  434 us
    dot_general x4, matrix products, dot_tn(): lax.dot_general(lhs, rhs, (((0,), (0,)), ((), ())), preferred_element_typ...  215 us
    ppermute x1, waiting for transfers between devices, stage_program(): bq_peer = lax.ppermute(bq_own, 'tp', swap)  157 us
    unnamed x16, local copies, waits for them, and re-layouts  58.5 us
  transfers between devices with their start and end apart: 3, of which 1 were waited for; matrix products, arithmetic and copies ran while one was open for 3% of the time, Pallas kernels for 0%

profile of v3, /device:TPU:0, one launch (start us, length us, event | category | flops | bytes accessed | tf_op | source)
XLA Modules:
  0.0 1557.4 jit_solution(14495297798497098191)
XLA Ops:
  0.6 3.4 collective-permute-start
  4.0 2.8 copy.35
  6.9 0.0 copy-start
  6.9 0.0 collective-permute-start.1
  6.9 0.8 reshape_squeeze.7
  7.7 2.0 collective-permute-start.2
  9.7 1.3 bitcast_convert_fusion.ln
  11.1 1.3 convert_element_type.18.bo
  12.3 1.3 convert_element_type.22.b2
  13.6 1.3 convert_element_type.21.b1
  15.0 10.3 copy.38.wq_h
  25.2 12.6 copy.36
  37.8 12.6 copy.37
  50.4 156.7 %collective-permute-done.2 = bf16[1,2304]{1,0:T(2,128)(2,1)S(1)} collective-permute-done((bf16[1,2304]{1,0:T(2,128)(2,1)S(1)}, bf16[1,2304]{1,0:T(2,128)(2,1)S(1)}, u32[]{:S(2)}, u32[]{:S(2)}) %collective-permute-start.2) | collective-permute-done | bytes 4640 | tf_op jit(solution)/shard_map/ppermute | solution.py:656
  207.2 0.6 maximum_convert_fusion.bq
  207.8 0.0 collective-permute-done.1
  207.8 4.3 copy.40.wo_p
  212.1 10.3 copy.39.wq_p
  222.3 433.7 %fwd_stage.1 = (bf16[24,256,1536]{2,1,0:T(8,128)(2,1)}, bf16[24,256,4608]{2,1,0:T(8,128)(2,1)}, bf16[24,256,768]{2,1,0:T(8,128)(2,1)}, bf16[24,256,1536]{2,1,0:T...) custom-call(bf16[24,256,1536]{2,1,0:T(8,128)(2,1)} %bitcast.68, ...), custom_call_target="tpu_custom_call" | custom-call | flops 231928233984 | bytes 320864256 | tf_op jit(solution)/shard_map/fwd_stage/pallas_call | solution.py:584
  656.1 649.0 %bwd_stage.1 = (bf16[24,256,1536]{2,1,0:T(8,128)(2,1)}, bf16[24,256,3072]{2,1,0:T(8,128)(2,1)}, bf16[24,256,1536]{2,1,0:T(8,128)(2,1)}, bf16[24,256,2304]{2,1,0:...) custom-call(bf16[24,256,1536]{2,1,0:T(8,128)(2,1)} %bitcast.69, ...), custom_call_target="tpu_custom_call" | custom-call | flops 231928233984 | bytes 320864256 | tf_op jit(solution)/shard_map/bwd_stage/pallas_call | solution.py:621
  1305.1 70.0 %convolution_bitcast_fusion = f32[3072,1536]{1,0:T(8,128)} fusion(bf16[24,256,3072]{2,1,0:T(8,128)(2,1)} %get-tuple-element.46, bf16[24,256,1536]{2,1,0:T(8,128)(2,1)} %get-tuple-element.47), kind=kOutput, calls=%fused_computation | convolution fusion | flops 57982058496 | bytes 75497472 | tf_op jit(solution)/shard_map/dot_general | solution.py:34
  1375.1 69.5 %convolution_bitcast_fusion.1 = f32[1536,3072]{1,0:T(8,128)} fusion(bf16[24,256,1536]{2,1,0:T(8,128)(2,1)} %get-tuple-element.43, bf16[24,256,3072]{2,1,0:T(8,128)(2,1)} %get-tuple-element.44), kind=kOutput, calls=%fused_computation.1 | convolution fusion | flops 57982058496 | bytes 75497472 | tf_op jit(solution)/shard_map/dot_general | solution.py:34
  1444.6 21.4 %convolution_bitcast_fusion.3 = f32[768,1536]{1,0:T(8,128)} fusion(bf16[24,256,768]{2,1,0:T(8,128)(2,1)} %get-tuple-element.39, bf16[24,256,1536]{2,1,0:T(8,128)(2,1)} %get-tuple-element.40), kind=kOutput, calls=%fused_computation.3 | convolution fusion | flops 14495514624 | bytes 33030144 | tf_op jit(solution)/shard_map/dot_general | solution.py:34
  1466.0 54.6 %convolution_bitcast_fusion.2 = f32[2304,1536]{1,0:T(8,128)} fusion(bf16[24,256,2304]{2,1,0:T(8,128)(2,1)} %get-tuple-element.36, bf16[24,256,1536]{2,1,0:T(8,128)(2,1)} %get-tuple-element.37), kind=kOutput, calls=%fused_computation.2 | convolution fusion | flops 43486543872 | bytes 61341696 | tf_op jit(solution)/shard_map/dot_general | solution.py:34
  1520.6 0.6 broadcast_in_dim.22
  1521.2 0.6 broadcast_in_dim.27
  1521.8 0.6 reduce_sum.48
  1522.5 0.7 reduce_sum.47
  1523.2 0.1 dynamic_slice.3
  1523.2 0.7 broadcast_in_dim_reshape.6
  1523.9 16.6 %copy.56 = bf16[1,2,12,256,1536]{4,3,2,1,0:T(8,128)(2,1)} copy(bf16[1,2,12,256,1536]{4,3,2,1,0:T(8,128)(2,1)} %bitcast.54) | data formatting | bytes 37748736
  1540.6 16.6 %copy.57 = bf16[1,2,12,256,1536]{4,3,2,1,0:T(8,128)(2,1)} copy(bf16[1,2,12,256,1536]{4,3,2,1,0:T(8,128)(2,1)} %bitcast.55) | data formatting | bytes 37748736
  (16 shorter events, 0.1 us)
Async XLA Ops:
  0.6 211.4 %collective-permute-start = (bf16[2304,1536]{1,0:T(8,128)(2,1)}, bf16[2304,1536]{1,0:T(8,128)(2,1)}, u32[]{:S(2)}, u32[]{:S(2)}) collective-permute-start(bf16[2304,1536]{1,0:T(8,128)(2,1)} %bitcast.60), channel_id=1, source_target_pairs={{0,4},{4,0},{1,5},{5,1},{2,6},{6,2},{3,7},{7,3}} | collective-permute-start | bytes 21233672 | tf_op jit(solution)/shard_map/ppermute | solution.py:654
  6.9 43.5 %copy-start = (bf16[768,1536]{0,1:T(8,128)(2,1)}, bf16[768,1536]{0,1:T(8,128)(2,1)S(1)}, u32[]{:S(2)}) copy-start(bf16[768,1536]{0,1:T(8,128)(2,1)S(1)} %copy.35) | copy-start | bytes 7077892
  6.9 200.9 %collective-permute-start.1 = (bf16[768,1536]{0,1:T(8,128)(2,1)S(1)}, bf16[768,1536]{0,1:T(8,128)(2,1)}, u32[]{:S(2)}, u32[]{:S(2)}) collective-permute-start(bf16[768,1536]{0,1:T(8,128)(2,1)S(1)} %copy.35), channel_id=1, source_target_pairs={{0,4},{4,0},{1,5},{5,1},{2,6},{6,2},{3,7},{7,3}} | collective-permute-start | bytes 7077896 | tf_op jit(solution)/shard_map/ppermute | solution.py:653
  7.7 199.4 %collective-permute-start.2 = (bf16[1,2304]{1,0:T(2,128)(2,1)S(1)}, bf16[1,2304]{1,0:T(2,128)(2,1)S(1)}, u32[]{:S(2)}, u32[]{:S(2)}) collective-permute-start(bf16[1,2304]{1,0:T(2,128)(2,1)S(1)} %reshape_squeeze.7), channel_id=1, source_target_pairs={{0,4},{4,0},{1,5},{5,1},{2,6},{6,2},{3,7},{7,3}} | collective-permute-start | bytes 13832 | tf_op jit(solution)/shard_map/ppermute | solution.py:656
  1466.0 54.6 %copy-start.5 = (f32[8,1536]{1,0:T(8,128)S(1)}, f32[8,1536]{1,0:T(8,128)}, u32[]{:S(2)}) copy-start(f32[8,1536]{1,0:T(8,128)} %get-tuple-element.41) | copy-start | bytes 147460
  1466.0 55.2 %copy-start.4 = (f32[8,1536]{1,0:T(8,128)S(1)}, f32[8,1536]{1,0:T(8,128)}, u32[]{:S(2)}) copy-start(f32[8,1536]{1,0:T(8,128)} %get-tuple-element.48) | copy-start | bytes 147460
  1466.0 55.8 %copy-start.3 = (f32[8,3072]{1,0:T(8,128)S(1)}, f32[8,3072]{1,0:T(8,128)}, u32[]{:S(2)}) copy-start(f32[8,3072]{1,0:T(8,128)} %get-tuple-element.45) | copy-start | bytes 294916
  1466.0 56.5 %copy-start.2 = (f32[8,4608]{1,0:T(8,128)S(1)}, f32[8,4608]{1,0:T(8,128)}, u32[]{:S(2)}) copy-start(f32[8,4608]{1,0:T(8,128)} %get-tuple-element.38) | copy-start | bytes 442372
  1466.0 56.5 %copy-start.1 = (f32[4,8,1536]{2,1,0:T(8,128)S(1)}, f32[4,8,1536]{2,1,0:T(8,128)}, u32[]{:S(2)}) copy-start(f32[4,8,1536]{2,1,0:T(8,128)} %get-tuple-element.42) | copy-start | bytes 589828

commit v4 on v3

--- a/solution.py
+++ b/solution.py
@@ -185,11 +185,11 @@
         y_out(m).start()
         part_copy(m).wait_send()
 
-    def one_sub(m):
+    def attn_part(m):
         slot = lax.rem(m, 2)
         prev = jnp.maximum(m - 1, 0)
-        h1_o, qkv_o, o_o, h2_o, s_o, a_o, x_o = outs(m)
-        h1_p, qkv_p, o_p, h2_p, s_p, a_p, x_p = outs(prev)
+        h1_o, qkv_o, o_o, h2_o, _, _, x_o = outs(m)
+        h1_p, qkv_p, o_p, h2_p, _, _, x_p = outs(prev)
 
         @pl.when(stage == 0)
         def _():
@@ -244,6 +244,11 @@
         mid_out(m).start()
         layer_norm(midb.at[slot], h2b, ln[2:3, :], ln[3:4, :])
         h2_o.start()
+
+    def mlp_part(m):
+        slot = lax.rem(m, 2)
+        _, _, _, _, s_o, a_o, _ = outs(m)
+        _, _, _, _, s_p, a_p, _ = outs(jnp.maximum(m - 1, 0))
 
         @pl.when(m > 0)
         def _():
@@ -266,11 +271,15 @@
     def step(m, carry):
         @pl.when(m < subs)
         def _():
-            one_sub(m)
+            attn_part(m)
 
         @pl.when(m > 0)
         def _():
             finish(m - 1)
+
+        @pl.when(m < subs)
+        def _():
+            mlp_part(m)
 
         return carry
 
@@ -636,6 +645,52 @@
     )(dy_in, x_all, mid_all, s_all, qkv_all, w2t, w1t, wot_own, wot_peer, wqt_own, wqt_peer, ln)
 
 
+def grad_kernel(n_tile, left, right, *refs):
+    if len(refs) == 3:
+        kept, out, kept_out = refs
+        kept_out[...] = kept[...]
+    else:
+        out, = refs
+
+    @pl.when(pl.program_id(1) == 0)
+    def _():
+        out[...] = jnp.zeros_like(out)
+
+    for n in range(0, out.shape[1], n_tile):
+        lanes = slice(n, n + n_tile)
+        out[:, lanes] += dot_tn(left[...], right[:, lanes])
+
+
+def grad_call(left, right, m_block, n_block, k_block, kept=None):
+    tokens, m_size = left.shape
+    n_size = right.shape[1]
+    m_count = m_size // m_block
+    grid = (m_count * (n_size // n_block), tokens // k_block)
+    in_specs = [pl.BlockSpec((k_block, m_block), lambda i, k: (k, i % m_count)), pl.BlockSpec((k_block, n_block), lambda i, k: (k, i // m_count))]
+    out_specs = [pl.BlockSpec((m_block, n_block), lambda i, k: (i % m_count, i // m_count))]
+    out_shape = [jax.ShapeDtypeStruct((m_size, n_size), F32)]
+    args = [left, right]
+    if kept is not None:
+        steps = grid[0] * grid[1]
+        assert kept.shape[0] % steps == 0
+        spec = pl.BlockSpec((kept.shape[0] // steps,) + kept.shape[1:], lambda i, k: (i * grid[1] + k, 0, 0))
+        in_specs.append(spec)
+        out_specs.append(spec)
+        out_shape.append(jax.ShapeDtypeStruct(kept.shape, kept.dtype))
+        args.append(kept)
+    moved = 2 * tokens * (m_size * (n_size // n_block) + n_size * m_count) + 4 * m_size * n_size
+    return pl.pallas_call(
+        functools.partial(grad_kernel, 512),
+        name="weight_grad",
+        grid=grid,
+        in_specs=in_specs,
+        out_specs=out_specs,
+        out_shape=out_shape,
+        cost_estimate=pl.CostEstimate(flops=2 * tokens * m_size * n_size, bytes_accessed=moved, transcendentals=0),
+        compiler_params=pltpu.CompilerParams(dimension_semantics=("arbitrary", "arbitrary"), vmem_limit_bytes=VMEM_LIMIT),
+    )(*args)
+
+
 def solution(mesh):
     stages = mesh.shape["pp"]
     swap = [(0, 1), (1, 0)]
@@ -662,17 +717,18 @@
         dy_all, dpre_all, gmid_all, dqkv_all, gin_all, db1, db2, dbo, dbq, dln = bwd_call(
             stages, width, tile, dy_out.reshape(subs, rows, d_model), x_all, mid_all, s_all, qkv_all, w2.T, w1.T, wo_own.T, wo_peer.T, wqt_own, wqt_peer, ln)
 
-        def weight_grad(left, right):
-            product = dot_tn(left.reshape(subs * rows, -1), right.reshape(subs * rows, -1))
-            return lax.optimization_barrier(product)
-
-        g_w_fc2 = weight_grad(a_all, dy_all)
-        g_w_fc1 = weight_grad(h2_all, dpre_all)
-        g_w_out = weight_grad(o_all, gmid_all).reshape(heads, width, d_model)
-        g_w_qkv = jnp.transpose(weight_grad(dqkv_all, h1_all).reshape(3, heads, width, d_model), (0, 3, 1, 2))
+        def flat(stack):
+            return stack.reshape(subs * rows, -1)
+
+        g_w_fc2, h_out = grad_call(flat(a_all), flat(dy_all), 1024, d_model, 768, y_all)
+        g_w_fc1, g_in = grad_call(flat(h2_all), flat(dpre_all), d_model, 1024, 768, gin_all)
+        g_w_out, = grad_call(flat(o_all), flat(gmid_all), half, d_model, 768)
+        g_w_qkv, = grad_call(flat(dqkv_all), flat(h1_all), half, d_model, 768)
+        g_w_out = g_w_out.reshape(heads, width, d_model)
+        g_w_qkv = jnp.transpose(g_w_qkv.reshape(3, heads, width, d_model), (0, 3, 1, 2))
         g_b_qkv = lax.dynamic_slice_in_dim(jnp.sum(dbq, axis=0), tp_me * (3 * half), 3 * half).reshape(3, heads, width)
         act = (1, micro, batch, rows, d_model)
-        return (y_all.reshape(act), gin_all.reshape(act), g_w_qkv[None], g_b_qkv[None], g_w_out[None], jnp.sum(dbo, axis=0)[None],
+        return (h_out.reshape(act), g_in.reshape(act), g_w_qkv[None], g_b_qkv[None], g_w_out[None], jnp.sum(dbo, axis=0)[None],
                 jnp.sum(dln, axis=1)[None], g_w_fc1[None], jnp.sum(db1, axis=0)[None], g_w_fc2[None], jnp.sum(db2, axis=0)[None])
 
     act_spec = P(None, "dp", None, None)

time: 1570 us -> 1570 us (level)
  Pallas kernels: 1080 us -> 1330 us
  matrix products: 215 us -> 0 us
  local copies, waits for them, and re-layouts: 88.9 us -> 55.6 us
    pallas_call x0 -> x4, Pallas kernels: none -> 230 us  [grad_call(): pl.pallas_call(functools.partial(grad_kernel, 512), name='weight_grad', g...]
    dot_general x4 -> x0, matrix products: 215 us -> none  [dot_tn(): lax.dot_general(lhs, rhs, (((0,), (0,)), ((), ())), preferred_element_typ...]
    unnamed x16 -> x4, local copies, waits for them, and re-layouts: 58.5 us -> 25.2 us
    pallas_call x1, Pallas kernels: 434 us -> 460 us  [fwd_call(): pl.pallas_call(functools.partial(fwd_kernel, subs, stages, width, tile),...]
where the time goes in v4:
time: 1570 us; the launch traced here: 1560 us
  Pallas kernels  1330 us (85%)
  waiting for transfers between devices  157 us (10%)
  local copies, waits for them, and re-layouts  55.6 us (4%)
    pallas_call x1, Pallas kernels, bwd_call(): pl.pallas_call(functools.partial(bwd_kernel, subs, stages, width, tile),...  637 us
    pallas_call x1, Pallas kernels, fwd_call(): pl.pallas_call(functools.partial(fwd_kernel, subs, stages, width, tile),...  460 us
    pallas_call x4, Pallas kernels, grad_call(): pl.pallas_call(functools.partial(grad_kernel, 512), name='weight_grad', g...  230 us
    ppermute x1, waiting for transfers between devices, stage_program(): bq_peer = lax.ppermute(bq_own, 'tp', swap)  157 us
  transfers between devices with their start and end apart: 3, of which 1 were waited for; matrix products, arithmetic and copies ran while one was open for 3% of the time, Pallas kernels for 0%

profile of v4, /device:TPU:0, one launch (start us, length us, event | category | flops | bytes accessed | tf_op | source)
XLA Modules:
  0.0 1557.2 jit_solution(2340801522780693473)
XLA Ops:
  0.6 3.4 collective-permute-start
  4.0 2.8 copy.31
  6.9 0.0 copy-start
  6.9 0.0 collective-permute-start.1
  6.9 0.8 reshape_squeeze.7
  7.7 2.0 collective-permute-start.2
  9.7 1.3 bitcast_convert_fusion.ln
  11.1 1.3 convert_element_type.18.bo
  12.3 1.3 convert_element_type.22.b2
  13.6 1.3 convert_element_type.21.b1
  15.0 10.3 copy.34.wq_h
  25.2 12.6 copy.32
  37.8 12.6 copy.33
  50.4 156.7 %collective-permute-done.2 = bf16[1,2304]{1,0:T(2,128)(2,1)S(1)} collective-permute-done((bf16[1,2304]{1,0:T(2,128)(2,1)S(1)}, bf16[1,2304]{1,0:T(2,128)(2,1)S(1)}, u32[]{:S(2)}, u32[]{:S(2)}) %collective-permute-start.2) | collective-permute-done | bytes 4640 | tf_op jit(solution)/shard_map/ppermute | solution.py:711
  207.2 0.6 maximum_convert_fusion.bq
  207.8 4.3 copy.36.wo_p
  212.1 10.3 copy.35.wq_p
  222.3 460.1 %fwd_stage.1 = (bf16[24,256,1536]{2,1,0:T(8,128)(2,1)}, bf16[24,256,4608]{2,1,0:T(8,128)(2,1)}, bf16[24,256,768]{2,1,0:T(8,128)(2,1)}, bf16[24,256,1536]{2,1,0:T...) custom-call(bf16[24,256,1536]{2,1,0:T(8,128)(2,1)} %bitcast.58, ...), custom_call_target="tpu_custom_call" | custom-call | flops 231928233984 | bytes 320864256 | tf_op jit(solution)/shard_map/fwd_stage/pallas_call | solution.py:593
  682.4 636.5 %bwd_stage.1 = (bf16[24,256,1536]{2,1,0:T(8,128)(2,1)}, bf16[24,256,3072]{2,1,0:T(8,128)(2,1)}, bf16[24,256,1536]{2,1,0:T(8,128)(2,1)}, bf16[24,256,2304]{2,1,0:...) custom-call(bf16[24,256,1536]{2,1,0:T(8,128)(2,1)} %bitcast.59, ...), custom_call_target="tpu_custom_call" | custom-call | flops 231928233984 | bytes 320864256 | tf_op jit(solution)/shard_map/bwd_stage/pallas_call | solution.py:630
  1319.0 0.8 reduce_sum.46
  1319.8 0.6 broadcast_in_dim.22
  1320.4 0.8 reduce_sum.49
  1321.2 0.6 broadcast_in_dim.27
  1321.8 1.5 reduce_sum.48
  1323.3 0.9 reduce_sum.45
  1324.3 1.6 reduce_sum.47
  1325.9 0.1 dynamic_slice.3
  1326.0 0.7 broadcast_in_dim_reshape.6
  1326.6 20.9 %weight_grad.7 = f32[768,1536]{1,0:T(8,128)} custom-call(bf16[6144,768]{1,0:T(8,128)(2,1)} %bitcast.72, bf16[6144,1536]{1,0:T(8,128)(2,1)} %bitcast.66), custom_call_target="tpu_custom_call" | custom-call | flops 14495514624 | bytes 33030144 | tf_op jit(solution)/shard_map/weight_grad/pallas_call | solution.py:682
  1347.5 57.6 %weight_grad.6 = f32[2304,1536]{1,0:T(8,128)} custom-call(bf16[6144,2304]{1,0:T(8,128)(2,1)} %bitcast.62, bf16[6144,1536]{1,0:T(8,128)(2,1)} %bitcast.64), custom_call_target="tpu_custom_call" | custom-call | flops 43486543872 | bytes 99090432 | tf_op jit(solution)/shard_map/weight_grad/pallas_call | solution.py:682
  1405.1 75.8 %weight_grad.4 = (f32[3072,1536]{1,0:T(8,128)}, bf16[24,256,1536]{2,1,0:T(8,128)(2,1)}) custom-call(bf16[6144,3072]{1,0:T(8,128)(2,1)} %bitcast.60, bf16[6144,1536]{1,0:T(8,128)(2,1)} %bitcast.65, bf16[24,256,1536]{2,1,0:T(8,128)(2,1)} %get-tuple-element.40.refs_0_), custom_call_target="tpu_custom_call" | custom-call | flops 57982058496 | bytes 113246208 | tf_op jit(solution)/shard_map/weight_grad/pallas_call | solution.py:682
  1480.9 75.9 %weight_grad.5 = (f32[1536,3072]{1,0:T(8,128)}, bf16[24,256,1536]{2,1,0:T(8,128)(2,1)}) custom-call(bf16[6144,1536]{1,0:T(8,128)(2,1)} %bitcast.63, bf16[6144,3072]{1,0:T(8,128)(2,1)} %bitcast.61, bf16[24,256,1536]{2,1,0:T(8,128)(2,1)} %get-tuple-element.44.refs_0_), custom_call_target="tpu_custom_call" | custom-call | flops 57982058496 | bytes 113246208 | tf_op jit(solution)/shard_map/weight_grad/pallas_call | solution.py:682
  (4 shorter events, 0.0 us)
Async XLA Ops:
  0.6 211.4 %collective-permute-start = (bf16[2304,1536]{1,0:T(8,128)(2,1)}, bf16[2304,1536]{1,0:T(8,128)(2,1)}, u32[]{:S(2)}, u32[]{:S(2)}) collective-permute-start(bf16[2304,1536]{1,0:T(8,128)(2,1)} %bitcast.50), channel_id=1, source_target_pairs={{0,4},{4,0},{1,5},{5,1},{2,6},{6,2},{3,7},{7,3}} | collective-permute-start | bytes 21233672 | tf_op jit(solution)/shard_map/ppermute | solution.py:709
  6.9 43.5 %copy-start = (bf16[768,1536]{0,1:T(8,128)(2,1)}, bf16[768,1536]{0,1:T(8,128)(2,1)S(1)}, u32[]{:S(2)}) copy-start(bf16[768,1536]{0,1:T(8,128)(2,1)S(1)} %copy.31) | copy-start | bytes 7077892
  6.9 200.9 %collective-permute-start.1 = (bf16[768,1536]{0,1:T(8,128)(2,1)S(1)}, bf16[768,1536]{0,1:T(8,128)(2,1)}, u32[]{:S(2)}, u32[]{:S(2)}) collective-permute-start(bf16[768,1536]{0,1:T(8,128)(2,1)S(1)} %copy.31), channel_id=1, source_target_pairs={{0,4},{4,0},{1,5},{5,1},{2,6},{6,2},{3,7},{7,3}} | collective-permute-start | bytes 7077896 | tf_op jit(solution)/shard_map/ppermute | solution.py:708
  7.7 199.4 %collective-permute-start.2 = (bf16[1,2304]{1,0:T(2,128)(2,1)S(1)}, bf16[1,2304]{1,0:T(2,128)(2,1)S(1)}, u32[]{:S(2)}, u32[]{:S(2)}) collective-permute-start(bf16[1,2304]{1,0:T(2,128)(2,1)S(1)} %reshape_squeeze.7), channel_id=1, source_target_pairs={{0,4},{4,0},{1,5},{5,1},{2,6},{6,2},{3,7},{7,3}} | collective-permute-start | bytes 13832 | tf_op jit(solution)/shard_map/ppermute | solution.py:711

commit v5 on v4

--- a/solution.py
+++ b/solution.py
@@ -69,13 +69,13 @@
 def fwd_kernel(subs, stages, width, tile,
                x_in, wq_h, wq_p, wo_h, wo_p, w1_h, w2_h, bq, bo, ln, b1, b2,
                x_all, qkv_all, o_all, mid_all, h1_all, h2_all, s_all, a_all, y_all,
-               wq, wo, w1, w2, xb, h1b, qkvb, ob, midb, h2b, slb, ab, partb, peerb, yb, sb, pb,
-               w_sem, in_sem, out_sem, mid_sem, y_sem, part_send, part_recv, y_send, x_recv):
+               wq, wo, w1, w2, xr, h1b, qkvb, ob, midb, h2b, slb, ab, partb, peerb, yb, sb, pb,
+               w_sem, in_sem, out_sem, mid_sem, y_sem, part_send, part_recv, y_send, x_recv, x_free):
     stage = lax.axis_index("pp")
     tp_me = lax.axis_index("tp")
     tp_peer = 1 - tp_me
     last_stage = stages - 1
-    rows, d_model = xb.shape
+    _, rows, d_model = xr.shape
     half = d_model // 2
     ff = slb.shape[1]
     scale = width ** -0.5
@@ -99,7 +99,7 @@
                 pltpu.make_async_copy(h2b, h2_all.at[m], out_sem.at[3]),
                 pltpu.make_async_copy(slb, s_all.at[m], out_sem.at[4]),
                 pltpu.make_async_copy(ab, a_all.at[m], out_sem.at[5]),
-                pltpu.make_async_copy(xb, x_all.at[m], out_sem.at[6]))
+                pltpu.make_async_copy(xr.at[lax.rem(m, RING)], x_all.at[m], out_sem.at[6]))
 
     def mid_out(m):
         slot = lax.rem(m, 2)
@@ -116,8 +116,15 @@
 
     def next_copy(m):
         slot = lax.rem(m, 2)
-        return pltpu.make_async_remote_copy(src_ref=yb.at[slot], dst_ref=x_all.at[m], send_sem=y_send.at[slot], recv_sem=x_recv.at[m],
+        return pltpu.make_async_remote_copy(src_ref=yb.at[slot], dst_ref=xr.at[lax.rem(m, RING)], send_sem=y_send.at[slot], recv_sem=x_recv.at[m],
                                             device_id={"pp": jnp.minimum(stage + 1, last_stage)}, device_id_type=MESH)
+
+    def x_load(m):
+        return pltpu.make_async_copy(x_in.at[m], xr.at[lax.rem(m, RING)], in_sem.at[lax.rem(m, 2)])
+
+    @pl.when(stage == 0)
+    def _():
+        x_load(0).start()
 
     def layer_norm(src, dst, gain, shift):
         for r in range(0, rows, ROW_CHUNK):
@@ -180,6 +187,10 @@
 
         @pl.when(stage < last_stage)
         def _():
+            @pl.when(m >= RING)
+            def _():
+                pl.semaphore_wait(x_free, 1)
+
             next_copy(m).start()
 
         y_out(m).start()
@@ -193,21 +204,18 @@
 
         @pl.when(stage == 0)
         def _():
-            @pl.when(m > 0)
+            x_load(m).wait()
+
+            @pl.when(m + 1 < subs)
             def _():
-                x_p.wait()
-
-            load = pltpu.make_async_copy(x_in.at[m], xb, in_sem)
-            load.start()
-            load.wait()
-            x_o.start()
+                x_load(m + 1).start()
 
         @pl.when(stage > 0)
         def _():
             next_copy(m).wait_recv()
-            load = pltpu.make_async_copy(x_all.at[m], xb, in_sem)
-            load.start()
-            load.wait()
+
+        x_o.start()
+        xb = xr.at[lax.rem(m, RING)]
 
         @pl.when(m > 0)
         def _():
@@ -242,6 +250,12 @@
         for n in range(0, d_model, tile):
             midb[slot, :, n:n + tile] = (xb[:, n:n + tile].astype(F32) + dot_nn(ob[...], wo[:, n:n + tile]) + bo[:, n:n + tile]).astype(BF16)
         mid_out(m).start()
+        x_o.wait()
+
+        @pl.when((stage > 0) & (m < subs - RING))
+        def _():
+            pl.semaphore_signal(x_free, inc=1, device_id={"pp": jnp.maximum(stage - 1, 0)}, device_id_type=MESH)
+
         layer_norm(midb.at[slot], h2b, ln[2:3, :], ln[3:4, :])
         h2_o.start()
 
@@ -272,14 +286,11 @@
         @pl.when(m < subs)
         def _():
             attn_part(m)
+            mlp_part(m)
 
         @pl.when(m > 0)
         def _():
             finish(m - 1)
-
-        @pl.when(m < subs)
-        def _():
-            mlp_part(m)
 
         return carry
 
@@ -288,10 +299,6 @@
     for copy in (h1_o, qkv_o, o_o, h2_o, s_o, a_o):
         copy.wait()
 
-    @pl.when(stage == 0)
-    def _():
-        x_o.wait()
-
     for m in (subs - 2, subs - 1):
         mid_out(m).wait()
         y_out(m).wait()
@@ -303,8 +310,8 @@
 
 def bwd_kernel(subs, stages, width, tile,
                dy_in, x_all, mid_all, s_all, qkv_all, w2t_h, w1t_h, wot_h, wot_p, wqt_h, wqt_p, ln,
-               dy_all, dpre_all, gmid_all, dqkv_all, gin_all, db1, db2, dbo, dbq, dln,
-               w2t, w1t, wot, wqt, dyb, slb, dpb, partb, peerb, rb, midb, xb, gmb, qkvb, gib, sb, db, pb, dsb,
+               dy_all, dpre_all, gmid_all, dqkv_all, gin_all, db1_o, db2_o, dbo_o, dbq_o, dln_o,
+               w2t, w1t, wot, wqt, dyb, slb, dpb, partb, peerb, rb, midb, xb, gmb, qkvb, gib, sb, db, pb, dsb, db1, db2, dbo, dbq, dln,
                w_sem, in_sem, pre_sem, out_sem, dy_sem, gi_sem, part_send, part_recv, gi_send, dy_recv, dy_free):
     stage = lax.axis_index("pp")
     tp_me = lax.axis_index("tp")
@@ -559,6 +566,10 @@
         return carry
 
     lax.fori_loop(0, subs + 1, step, 0)
+    for acc, out in ((db1, db1_o), (db2, db2_o), (dbo, dbo_o)):
+        out[...] = jnp.sum(acc[...], axis=0, keepdims=True)
+    dbq_o[...] = jnp.sum(dbq[:, mine_q], axis=0, keepdims=True)
+    dln_o[...] = jnp.sum(dln[...], axis=1)
     for copy in outs(subs - 1)[:2]:
         copy.wait()
     for m in (subs - 2, subs - 1):
@@ -598,9 +609,9 @@
         out_specs=[ANY] * 9,
         scratch_shapes=[
             pltpu.VMEM((d_model, 3 * d_model), BF16), pltpu.VMEM((d_model, d_model), BF16), pltpu.VMEM(w1.shape, BF16), pltpu.VMEM(w2.shape, BF16),
-            buf(d_model), buf(d_model), buf(3 * d_model), buf(d_model), two(d_model), buf(d_model), buf(ff, F32), buf(ff), two(d_model), pltpu.VMEM((RING, rows, d_model), BF16), two(d_model),
+            pltpu.VMEM((RING, rows, d_model), BF16), buf(d_model), buf(3 * d_model), buf(d_model), two(d_model), buf(d_model), buf(ff, F32), buf(ff), two(d_model), pltpu.VMEM((RING, rows, d_model), BF16), two(d_model),
             pltpu.VMEM((2, 4, rows, rows), F32), pltpu.VMEM((2, 4, rows, rows), BF16),
-            DMA((6,)), DMA, DMA((7,)), DMA((2,)), DMA((2,)), DMA((2,)), DMA((subs,)), DMA((2,)), DMA((subs,)),
+            DMA((6,)), DMA((2,)), DMA((7,)), DMA((2,)), DMA((2,)), DMA((2,)), DMA((subs,)), DMA((2,)), DMA((subs,)), pltpu.SemaphoreType.REGULAR,
         ],
         cost_estimate=pl.CostEstimate(flops=subs * rows * weights, bytes_accessed=weights + subs * rows * d_model * 30, transcendentals=subs * rows * (ff + rows * 16)),
         compiler_params=pltpu.CompilerParams(collective_id=0, has_side_effects=True, vmem_limit_bytes=VMEM_LIMIT),
@@ -631,13 +642,14 @@
         functools.partial(bwd_kernel, subs, stages, width, tile),
         name="bwd_stage",
         out_shape=(hbm(d_model), hbm(ff), hbm(d_model), hbm(3 * half), hbm(d_model),
-                   acc(8, ff), acc(8, d_model), acc(8, d_model), acc(8, 3 * d_model), acc(4, 8, d_model)),
+                   acc(1, ff), acc(1, d_model), acc(1, d_model), acc(1, 3 * half), acc(4, d_model)),
         in_specs=[ANY] * 11 + [VMEM],
         out_specs=[ANY] * 5 + [VMEM] * 5,
         scratch_shapes=[
             pltpu.VMEM(w2t.shape, BF16), pltpu.VMEM(w1t.shape, BF16), pltpu.VMEM((d_model, d_model), BF16), pltpu.VMEM((3 * d_model, d_model), BF16),
             ring, buf(ff, F32), buf(ff), two(d_model), ring, buf(d_model), buf(d_model), buf(d_model), buf(d_model), buf(3 * d_model), two(d_model),
             pltpu.VMEM((4, rows, rows), F32), pltpu.VMEM((4, rows, rows), F32), pltpu.VMEM((4, rows, rows), BF16), pltpu.VMEM((4, rows, rows), BF16),
+            pltpu.VMEM((8, ff), F32), pltpu.VMEM((8, d_model), F32), pltpu.VMEM((8, d_model), F32), pltpu.VMEM((8, 3 * d_model), F32), pltpu.VMEM((4, 8, d_model), F32),
             DMA((6,)), DMA((2,)), DMA((4,)), DMA((3,)), DMA((2,)), DMA((2,)), DMA((2,)), DMA((subs,)), DMA((2,)), DMA((subs,)), pltpu.SemaphoreType.REGULAR,
         ],
         cost_estimate=pl.CostEstimate(flops=subs * rows * weights, bytes_accessed=weights + subs * rows * d_model * 30, transcendentals=subs * rows * (ff + rows * 16)),
@@ -720,16 +732,16 @@
         def flat(stack):
             return stack.reshape(subs * rows, -1)
 
-        g_w_fc2, h_out = grad_call(flat(a_all), flat(dy_all), 1024, d_model, 768, y_all)
-        g_w_fc1, g_in = grad_call(flat(h2_all), flat(dpre_all), d_model, 1024, 768, gin_all)
-        g_w_out, = grad_call(flat(o_all), flat(gmid_all), half, d_model, 768)
-        g_w_qkv, = grad_call(flat(dqkv_all), flat(h1_all), half, d_model, 768)
+        g_w_fc2, h_out = grad_call(flat(a_all), flat(dy_all), 1024, d_model, 1536, y_all)
+        g_w_fc1, g_in = grad_call(flat(h2_all), flat(dpre_all), d_model, 1024, 1536, gin_all)
+        g_w_out, = grad_call(flat(o_all), flat(gmid_all), half, d_model, 1536)
+        g_w_qkv = lax.optimization_barrier(dot_tn(flat(dqkv_all), flat(h1_all)))
         g_w_out = g_w_out.reshape(heads, width, d_model)
         g_w_qkv = jnp.transpose(g_w_qkv.reshape(3, heads, width, d_model), (0, 3, 1, 2))
-        g_b_qkv = lax.dynamic_slice_in_dim(jnp.sum(dbq, axis=0), tp_me * (3 * half), 3 * half).reshape(3, heads, width)
+        g_b_qkv = dbq.reshape(3, heads, width)
         act = (1, micro, batch, rows, d_model)
-        return (h_out.reshape(act), g_in.reshape(act), g_w_qkv[None], g_b_qkv[None], g_w_out[None], jnp.sum(dbo, axis=0)[None],
-                jnp.sum(dln, axis=1)[None], g_w_fc1[None], jnp.sum(db1, axis=0)[None], g_w_fc2[None], jnp.sum(db2, axis=0)[None])
+        return (h_out.reshape(act), g_in.reshape(act), g_w_qkv[None], g_b_qkv[None], g_w_out[None], dbo,
+                dln[None], g_w_fc1[None], db1, g_w_fc2[None], db2)
 
     act_spec = P(None, "dp", None, None)
     arg_specs = (act_spec, act_spec,

time: 1570 us -> 1540 us (0.981)
  Pallas kernels: 1330 us -> 1240 us
  matrix products: 0 us -> 54.5 us
    pallas_call x4 -> x3, Pallas kernels: 230 us -> 165 us  [grad_call(): pl.pallas_call(functools.partial(grad_kernel, 512), name='weight_grad', g...]
    dot_general x0 -> x1, matrix products: none -> 54.5 us  [dot_tn(): lax.dot_general(lhs, rhs, (((0,), (0,)), ((), ())), preferred_element_typ...]
    pallas_call x1, Pallas kernels: 460 us -> 430 us  [fwd_call(): pl.pallas_call(functools.partial(fwd_kernel, subs, stages, width, tile),...]
where the time goes in v5:
time: 1540 us; the launch traced here: 1530 us
  Pallas kernels  1240 us (81%)
  waiting for transfers between devices  157 us (10%)
  local copies, waits for them, and re-layouts  59.6 us (4%)
  matrix products  54.5 us (4%)
    pallas_call x1, Pallas kernels, bwd_call(): pl.pallas_call(functools.partial(bwd_kernel, subs, stages, width, tile),...  649 us
    pallas_call x1, Pallas kernels, fwd_call(): pl.pallas_call(functools.partial(fwd_kernel, subs, stages, width, tile),...  430 us
    pallas_call x3, Pallas kernels, grad_call(): pl.pallas_call(functools.partial(grad_kernel, 512), name='weight_grad', g...  165 us
    ppermute x1, waiting for transfers between devices, stage_program(): bq_peer = lax.ppermute(bq_own, 'tp', swap)  157 us
    dot_general x1, matrix products, dot_tn(): lax.dot_general(lhs, rhs, (((0,), (0,)), ((), ())), preferred_element_typ...  54.5 us
  transfers between devices with their start and end apart: 3, of which 1 were waited for; matrix products, arithmetic and copies ran while one was open for 3% of the time, Pallas kernels for 0%

profile of v5, /device:TPU:0, one launch (start us, length us, event | category | flops | bytes accessed | tf_op | source)
XLA Modules:
  0.0 1527.0 jit_solution(1105392975869977925)
XLA Ops:
  0.6 3.4 collective-permute-start
  4.0 2.8 copy.32
  6.9 0.0 copy-start
  6.9 0.0 collective-permute-start.1
  6.9 0.8 reshape_squeeze.7
  7.7 2.0 collective-permute-start.2
  9.7 1.3 bitcast_convert_fusion.ln
  11.1 1.3 convert_element_type.18.bo
  12.3 1.3 convert_element_type.22.b2
  13.6 1.3 convert_element_type.21.b1
  15.0 10.3 copy.35.wq_h
  25.2 12.6 copy.33
  37.8 12.6 copy.34
  50.4 156.7 %collective-permute-done.2 = bf16[1,2304]{1,0:T(2,128)(2,1)S(1)} collective-permute-done((bf16[1,2304]{1,0:T(2,128)(2,1)S(1)}, bf16[1,2304]{1,0:T(2,128)(2,1)S(1)}, u32[]{:S(2)}, u32[]{:S(2)}) %collective-permute-start.2) | collective-permute-done | bytes 4640 | tf_op jit(solution)/shard_map/ppermute | solution.py:723
  207.2 0.6 maximum_convert_fusion.bq
  207.8 0.0 collective-permute-done.1
  207.8 4.3 copy.37.wo_p
  212.1 0.0 collective-permute-done.wqt_p
  212.1 10.3 copy.36.wq_p
  222.3 429.9 %fwd_stage.1 = (bf16[24,256,1536]{2,1,0:T(8,128)(2,1)}, bf16[24,256,4608]{2,1,0:T(8,128)(2,1)}, bf16[24,256,768]{2,1,0:T(8,128)(2,1)}, bf16[24,256,1536]{2,1,0:T...) custom-call(bf16[24,256,1536]{2,1,0:T(8,128)(2,1)} %bitcast.58, ...), custom_call_target="tpu_custom_call" | custom-call | flops 231928233984 | bytes 320864256 | tf_op jit(solution)/shard_map/fwd_stage/pallas_call | solution.py:604
  652.2 648.7 %bwd_stage.1 = (bf16[24,256,1536]{2,1,0:T(8,128)(2,1)}, bf16[24,256,3072]{2,1,0:T(8,128)(2,1)}, bf16[24,256,1536]{2,1,0:T(8,128)(2,1)}, bf16[24,256,2304]{2,1,0:...) custom-call(bf16[24,256,1536]{2,1,0:T(8,128)(2,1)} %bitcast.59, ...), custom_call_target="tpu_custom_call" | custom-call | flops 231928233984 | bytes 320864256 | tf_op jit(solution)/shard_map/bwd_stage/pallas_call | solution.py:641
  1300.9 0.0 copy-start.1
  1301.0 54.5 %convolution_bitcast_fusion = f32[2304,1536]{1,0:T(8,128)} fusion(bf16[24,256,2304]{2,1,0:T(8,128)(2,1)} %get-tuple-element.46, bf16[24,256,1536]{2,1,0:T(8,128)(2,1)} %get-tuple-element.47), kind=kOutput, calls=%fused_computation | convolution fusion | flops 43486543872 | bytes 61341696 | tf_op jit(solution)/shard_map/dot_general | solution.py:34
  1355.5 0.0 copy-done.1
  1355.5 0.7 broadcast_in_dim_reshape.6
  1356.2 21.0 %weight_grad.5 = f32[768,1536]{1,0:T(8,128)} custom-call(bf16[6144,768]{1,0:T(8,128)(2,1)} %bitcast.70, bf16[6144,1536]{1,0:T(8,128)(2,1)} %bitcast.68), custom_call_target="tpu_custom_call" | custom-call | flops 14495514624 | bytes 33030144 | tf_op jit(solution)/shard_map/weight_grad/pallas_call | solution.py:694
  1377.2 72.0 %weight_grad.3 = (f32[3072,1536]{1,0:T(8,128)}, bf16[24,256,1536]{2,1,0:T(8,128)(2,1)}) custom-call(bf16[6144,3072]{1,0:T(8,128)(2,1)} %bitcast.60, bf16[6144,1536]{1,0:T(8,128)(2,1)} %bitcast.65, bf16[24,256,1536]{2,1,0:T(8,128)(2,1)} %get-tuple-element.40.refs_0_), custom_call_target="tpu_custom_call" | custom-call | flops 57982058496 | bytes 113246208 | tf_op jit(solution)/shard_map/weight_grad/pallas_call | solution.py:694
  1449.2 72.1 %weight_grad.4 = (f32[1536,3072]{1,0:T(8,128)}, bf16[24,256,1536]{2,1,0:T(8,128)(2,1)}) custom-call(bf16[6144,1536]{1,0:T(8,128)(2,1)} %bitcast.62, bf16[6144,3072]{1,0:T(8,128)(2,1)} %bitcast.61, bf16[24,256,1536]{2,1,0:T(8,128)(2,1)} %get-tuple-element.44.refs_0_), custom_call_target="tpu_custom_call" | custom-call | flops 57982058496 | bytes 113246208 | tf_op jit(solution)/shard_map/weight_grad/pallas_call | solution.py:694
  1521.3 1.3 copy.49
  1522.6 1.3 copy.50
  1523.9 1.3 copy.51
  1525.2 1.3 copy.52
  (3 shorter events, 0.1 us)
Async XLA Ops:
  0.6 211.4 %collective-permute-start = (bf16[2304,1536]{1,0:T(8,128)(2,1)}, bf16[2304,1536]{1,0:T(8,128)(2,1)}, u32[]{:S(2)}, u32[]{:S(2)}) collective-permute-start(bf16[2304,1536]{1,0:T(8,128)(2,1)} %bitcast.51), channel_id=1, source_target_pairs={{0,4},{4,0},{1,5},{5,1},{2,6},{6,2},{3,7},{7,3}} | collective-permute-start | bytes 21233672 | tf_op jit(solution)/shard_map/ppermute | solution.py:721
  6.9 43.5 %copy-start = (bf16[768,1536]{0,1:T(8,128)(2,1)}, bf16[768,1536]{0,1:T(8,128)(2,1)S(1)}, u32[]{:S(2)}) copy-start(bf16[768,1536]{0,1:T(8,128)(2,1)S(1)} %copy.32) | copy-start | bytes 7077892
  6.9 200.9 %collective-permute-start.1 = (bf16[768,1536]{0,1:T(8,128)(2,1)S(1)}, bf16[768,1536]{0,1:T(8,128)(2,1)}, u32[]{:S(2)}, u32[]{:S(2)}) collective-permute-start(bf16[768,1536]{0,1:T(8,128)(2,1)S(1)} %copy.32), channel_id=1, source_target_pairs={{0,4},{4,0},{1,5},{5,1},{2,6},{6,2},{3,7},{7,3}} | collective-permute-start | bytes 7077896 | tf_op jit(solution)/shard_map/ppermute | solution.py:720
  7.7 199.4 %collective-permute-start.2 = (bf16[1,2304]{1,0:T(2,128)(2,1)S(1)}, bf16[1,2304]{1,0:T(2,128)(2,1)S(1)}, u32[]{:S(2)}, u32[]{:S(2)}) collective-permute-start(bf16[1,2304]{1,0:T(2,128)(2,1)S(1)} %reshape_squeeze.7), channel_id=1, source_target_pairs={{0,4},{4,0},{1,5},{5,1},{2,6},{6,2},{3,7},{7,3}} | collective-permute-start | bytes 13832 | tf_op jit(solution)/shard_map/ppermute | solution.py:723
  1300.9 54.5 %copy-start.1 = (f32[1,2304]{1,0:T(1,128)S(1)}, f32[1,2304]{1,0:T(1,128)}, u32[]{:S(2)}) copy-start(f32[1,2304]{1,0:T(1,128)} %get-tuple-element.48) | copy-start | bytes 27652

commit v6 on v5

--- a/solution.py
+++ b/solution.py
@@ -18,8 +18,18 @@
 LOG2_E = 1.4426950408889634
 SOFT_ROWS = 64
 RING = 4
+LANES = 128
+RELAYED = 2
 
 WINDOWS = ((0, 128, 0), (0, 256, 96), (128, 256, 64), (256, 128, 32))
+
+
+def parity(m):
+    return lax.rem(m, 2)
+
+
+def ring_slot(m):
+    return lax.rem(m, RING)
 
 
 def dot_nn(lhs, rhs):
@@ -40,10 +50,10 @@
 
 
 def join_heads(parts, width):
-    lane = lax.broadcasted_iota(jnp.int32, (parts[0].shape[0], 128), 1)
-    first = jnp.where(lane < width, parts[0], parts[1][:, :128])
-    second = jnp.where(lane < 2 * width - 128, parts[1][:, 128:], parts[2][:, :128])
-    third = jnp.where(lane < 3 * width - 256, parts[2][:, 128:], parts[3])
+    lane = lax.broadcasted_iota(jnp.int32, (parts[0].shape[0], LANES), 1)
+    first = jnp.where(lane < width, parts[0], parts[1][:, :LANES])
+    second = jnp.where(lane < 2 * width - LANES, parts[1][:, LANES:], parts[2][:, :LANES])
+    third = jnp.where(lane < 3 * width - 256, parts[2][:, LANES:], parts[3])
     return first, second, third
 
 
@@ -61,16 +71,16 @@
 def neighbour_barrier(stage, tp_peer, stages):
     barrier = pltpu.get_barrier_semaphore()
     pl.semaphore_signal(barrier, inc=1, device_id={"tp": tp_peer}, device_id_type=MESH)
-    pl.semaphore_signal(barrier, inc=1, device_id={"pp": lax.rem(stage + 1, stages)}, device_id_type=MESH)
-    pl.semaphore_signal(barrier, inc=1, device_id={"pp": lax.rem(stage + stages - 1, stages)}, device_id_type=MESH)
-    pl.semaphore_wait(barrier, 3)
+    for step in range(1, stages):
+        pl.semaphore_signal(barrier, inc=1, device_id={"pp": lax.rem(stage + step, stages)}, device_id_type=MESH)
+    pl.semaphore_wait(barrier, stages)
 
 
 def fwd_kernel(subs, stages, width, tile,
-               x_in, wq_h, wq_p, wo_h, wo_p, w1_h, w2_h, bq, bo, ln, b1, b2,
-               x_all, qkv_all, o_all, mid_all, h1_all, h2_all, s_all, a_all, y_all,
-               wq, wo, w1, w2, xr, h1b, qkvb, ob, midb, h2b, slb, ab, partb, peerb, yb, sb, pb,
-               w_sem, in_sem, out_sem, mid_sem, y_sem, part_send, part_recv, y_send, x_recv, x_free):
+               x_in, wqt_h, wo_h, w1_h, w2_h, bq, bo_h, b1_h, b2_h, ln_h,
+               x_all, qkv_all, o_all, mid_all, h1_all, h2_all, s_all, a_all, y_all, wqt_p, wot_o, w1t_o, w2t_o, relay_in, relay_out,
+               wq, wo, w1, w2, xr, h1b, qkvb, ob, midb, h2b, slb, ab, partb, peerb, yb, sb, pb, bqb, tb, par,
+               w_sem, t_sem, wq_send, wq_recv, wo_send, wo_recv, bq_send, bq_recv, relay_send, relay_recv, in_sem, out_sem, mid_sem, y_sem, part_send, part_recv, y_send, x_recv, x_free):
     stage = lax.axis_index("pp")
     tp_me = lax.axis_index("tp")
     tp_peer = 1 - tp_me
@@ -81,46 +91,141 @@
     scale = width ** -0.5
     log2_scale = scale * LOG2_E
 
-    mine = pl.ds(pl.multiple_of(tp_me * half, 128), half)
-    theirs = pl.ds(pl.multiple_of(tp_peer * half, 128), half)
-    mine_q = pl.ds(pl.multiple_of(tp_me * (3 * half), 128), 3 * half)
-    theirs_q = pl.ds(pl.multiple_of(tp_peer * (3 * half), 128), 3 * half)
-    loads = [pltpu.make_async_copy(src, dst, w_sem.at[i]) for i, (src, dst) in enumerate((
-        (wq_h, wq.at[:, mine_q]), (wq_p, wq.at[:, theirs_q]), (wo_h, wo.at[mine, :]), (wo_p, wo.at[theirs, :]), (w1_h, w1), (w2_h, w2)))]
-    for load in loads:
-        load.start()
-    pb[:, :, 0:128, 128:rows] = jnp.zeros((2, 4, 128, rows - 128), BF16)
+    first = 0
+    rows_of = []
+    for row in (bo_h, b1_h, b2_h, *(ln_h.at[i:i + 1, :] for i in range(4))):
+        lanes = slice(first, first + row.shape[1])
+        par[:, lanes] = row[...].astype(F32)
+        rows_of.append(par.at[:, lanes])
+        first = lanes.stop
+    bo, b1, b2, *ln = rows_of
+    mine = pl.ds(pl.multiple_of(tp_me * half, LANES), half)
+    piece = 256
+    pieces = 3 * half // piece
+    peer_id = {"device_id": {"tp": tp_peer}, "device_id_type": MESH}
+    loads = [pltpu.make_async_copy(src, dst, w_sem.at[i]) for i, (src, dst) in enumerate(((wo_h, wo.at[mine, :]), (w1_h, w1), (w2_h, w2)))]
+
+    def cut(p):
+        return pl.ds(pl.multiple_of(p * piece, piece), piece)
+
+    def wq_copy(p):
+        return pltpu.make_async_remote_copy(src_ref=wqt_h.at[cut(p), :], dst_ref=wqt_p.at[cut(p), :], send_sem=wq_send.at[p], recv_sem=wq_recv.at[p], **peer_id)
+
+    wo_copy = pltpu.make_async_remote_copy(src_ref=wo_h, dst_ref=wo.at[mine, :], send_sem=wo_send, recv_sem=wo_recv, **peer_id)
+    bq_copy = pltpu.make_async_remote_copy(src_ref=bq, dst_ref=bqb.at[tp_me], send_sem=bq_send, recv_sem=bq_recv, **peer_id)
+
+    column = stages // 2
+    direct = pieces - RELAYED
+
+    def relay_copy(leg, r):
+        src = (wqt_h.at[cut(direct + r), :], relay_in.at[r], relay_out.at[r])[leg]
+        dst = (relay_in.at[r], relay_out.at[r], wqt_p.at[cut(direct + r), :])[leg]
+        there = ({"pp": jnp.minimum(stage + column, last_stage)}, {"tp": tp_peer}, {"pp": jnp.maximum(stage - column, 0)})[leg]
+        recv_sem = wq_recv.at[direct + r] if leg == 2 else relay_recv.at[leg, r]
+        return pltpu.make_async_remote_copy(src_ref=src, dst_ref=dst, send_sem=relay_send.at[leg, r], recv_sem=recv_sem, device_id=there, device_id_type=MESH)
+
+    def moved(src, dst):
+        copy = pltpu.make_async_copy(src, dst, t_sem)
+        copy.start()
+        copy.wait()
+
+    def turn(source, owner, p):
+        moved(source.at[cut(p), :], h1b)
+        wq[:, pl.ds(pl.multiple_of(owner * (3 * half) + p * piece, LANES), piece)] = jnp.transpose(h1b[...])
+
+    def exchange_weights():
+        def send(p, carry):
+            wq_copy(p).start()
+            return carry
+
+        def own(p, carry):
+            turn(wqt_h, tp_me, p)
+            return carry
+
+        def turn_w1(p, carry):
+            h2b[...] = jnp.transpose(w1[:, cut(p)])
+            moved(h2b, w1t_o.at[cut(p), :])
+            return carry
+
+        def turn_w2(p, carry):
+            tb[...] = jnp.transpose(w2[cut(p), :])
+            moved(tb, w2t_o.at[:, cut(p)])
+            return carry
+
+        def received(p, carry):
+            wq_copy(p).wait_recv()
+            turn(wqt_p, tp_peer, p)
+            return carry
+
+        bq_copy.start()
+        for load in loads:
+            load.start()
+        lax.fori_loop(0, RELAYED, send, 0)
+
+        @pl.when(stage < column)
+        def _():
+            for r in range(RELAYED):
+                relay_copy(0, r).start()
+            lax.fori_loop(RELAYED, direct, send, 0)
+
+        @pl.when(stage >= column)
+        def _():
+            for r in range(RELAYED):
+                relay_copy(0, r).wait_recv()
+                relay_copy(1, r).start()
+            lax.fori_loop(RELAYED, pieces, send, 0)
+
+        wo_copy.start()
+        bqb[tp_me] = bq[...]
+        lax.fori_loop(0, pieces, own, 0)
+        for load in loads:
+            load.wait()
+        lax.fori_loop(0, ff // piece, turn_w1, 0)
+        lax.fori_loop(0, ff // piece, turn_w2, 0)
+
+        @pl.when(stage >= column)
+        def _():
+            for r in range(RELAYED):
+                relay_copy(1, r).wait_recv()
+                relay_copy(2, r).start()
+
+        bq_copy.wait_recv()
+        middle = direct // 2
+        for first, last in ((0, middle), (direct, pieces), (middle, direct)):
+            lax.fori_loop(first, last, received, 0)
+
+    pb[:, :, 0:LANES, LANES:rows] = jnp.zeros((2, 4, LANES, rows - LANES), BF16)
     neighbour_barrier(stage, tp_peer, stages)
 
     def outs(m):
         return (pltpu.make_async_copy(h1b, h1_all.at[m], out_sem.at[0]),
                 pltpu.make_async_copy(qkvb, qkv_all.at[m], out_sem.at[1]),
-                pltpu.make_async_copy(ob.at[:, pl.ds(pl.multiple_of(tp_me * half, 128), half)], o_all.at[m], out_sem.at[2]),
+                pltpu.make_async_copy(ob.at[:, pl.ds(pl.multiple_of(tp_me * half, LANES), half)], o_all.at[m], out_sem.at[2]),
                 pltpu.make_async_copy(h2b, h2_all.at[m], out_sem.at[3]),
                 pltpu.make_async_copy(slb, s_all.at[m], out_sem.at[4]),
                 pltpu.make_async_copy(ab, a_all.at[m], out_sem.at[5]),
-                pltpu.make_async_copy(xr.at[lax.rem(m, RING)], x_all.at[m], out_sem.at[6]))
+                pltpu.make_async_copy(xr.at[ring_slot(m)], x_all.at[m], out_sem.at[6]))
 
     def mid_out(m):
-        slot = lax.rem(m, 2)
+        slot = parity(m)
         return pltpu.make_async_copy(midb.at[slot], mid_all.at[m], mid_sem.at[slot])
 
     def y_out(m):
-        slot = lax.rem(m, 2)
+        slot = parity(m)
         return pltpu.make_async_copy(yb.at[slot], y_all.at[m], y_sem.at[slot])
 
     def part_copy(m):
-        slot = lax.rem(m, 2)
-        return pltpu.make_async_remote_copy(src_ref=partb.at[slot], dst_ref=peerb.at[lax.rem(m, RING)], send_sem=part_send.at[slot], recv_sem=part_recv.at[m],
+        slot = parity(m)
+        return pltpu.make_async_remote_copy(src_ref=partb.at[slot], dst_ref=peerb.at[ring_slot(m)], send_sem=part_send.at[slot], recv_sem=part_recv.at[m],
                                             device_id={"tp": tp_peer}, device_id_type=MESH)
 
     def next_copy(m):
-        slot = lax.rem(m, 2)
-        return pltpu.make_async_remote_copy(src_ref=yb.at[slot], dst_ref=xr.at[lax.rem(m, RING)], send_sem=y_send.at[slot], recv_sem=x_recv.at[m],
+        slot = parity(m)
+        return pltpu.make_async_remote_copy(src_ref=yb.at[slot], dst_ref=xr.at[ring_slot(m)], send_sem=y_send.at[slot], recv_sem=x_recv.at[m],
                                             device_id={"pp": jnp.minimum(stage + 1, last_stage)}, device_id_type=MESH)
 
     def x_load(m):
-        return pltpu.make_async_copy(x_in.at[m], xr.at[lax.rem(m, RING)], in_sem.at[lax.rem(m, 2)])
+        return pltpu.make_async_copy(x_in.at[m], xr.at[ring_slot(m)], in_sem.at[parity(m)])
 
     @pl.when(stage == 0)
     def _():
@@ -145,7 +250,7 @@
         def softmax(group):
             for j in range(4):
                 for r0 in range(0, rows, SOFT_ROWS):
-                    keys = 128 * (r0 // 128 + 1)
+                    keys = LANES * (r0 // LANES + 1)
                     row = lax.broadcasted_iota(jnp.int32, (SOFT_ROWS, keys), 0) + r0
                     col = lax.broadcasted_iota(jnp.int32, (SOFT_ROWS, keys), 1)
                     score = jnp.where(row >= col, sb[group % 2, j, r0:r0 + SOFT_ROWS, 0:keys], NEG)
@@ -157,8 +262,8 @@
             base = group_base(group) + 2 * half
             parts = [dot_nn(pb[group % 2, j], qkvb[:, base + start:base + start + size]) for j, (start, size, _) in enumerate(WINDOWS)]
             for i, piece in enumerate(join_heads(parts, width)):
-                first = group * (4 * width) + i * 128
-                ob[:, first:first + 128] = piece.astype(BF16)
+                first = group * (4 * width) + i * LANES
+                ob[:, first:first + LANES] = piece.astype(BF16)
 
         groups = d_model // (4 * width)
         scores(0)
@@ -169,8 +274,8 @@
             values(group)
 
     def finish(m):
-        slot = lax.rem(m, 2)
-        peer_slot = lax.rem(m, RING)
+        slot = parity(m)
+        peer_slot = ring_slot(m)
         part_copy(m).wait_recv()
 
         @pl.when(m >= 2)
@@ -197,7 +302,7 @@
         part_copy(m).wait_send()
 
     def attn_part(m):
-        slot = lax.rem(m, 2)
+        slot = parity(m)
         prev = jnp.maximum(m - 1, 0)
         h1_o, qkv_o, o_o, h2_o, _, _, x_o = outs(m)
         h1_p, qkv_p, o_p, h2_p, _, _, x_p = outs(prev)
@@ -215,7 +320,7 @@
             next_copy(m).wait_recv()
 
         x_o.start()
-        xb = xr.at[lax.rem(m, RING)]
+        xb = xr.at[ring_slot(m)]
 
         @pl.when(m > 0)
         def _():
@@ -224,24 +329,19 @@
             o_p.wait()
             h2_p.wait()
 
-        layer_norm(xb, h1b, ln[0:1, :], ln[1:2, :])
+        layer_norm(xb, h1b, ln[0][...], ln[1][...])
         h1_o.start()
 
-        @pl.when(m == 0)
-        def _():
-            loads[0].wait()
-            loads[1].wait()
-
         for n in range(0, 3 * d_model, tile):
-            qkvb[:, n:n + tile] = (dot_nn(h1b[...], wq[:, n:n + tile]) + bq[:, n:n + tile]).astype(BF16)
+            owner, lane = divmod(n, 3 * half)
+            qkvb[:, n:n + tile] = (dot_nn(h1b[...], wq[:, n:n + tile]) + bqb[owner, :, lane:lane + tile].astype(F32)).astype(BF16)
         qkv_o.start()
         attend()
         o_o.start()
 
         @pl.when(m == 0)
         def _():
-            for load in loads[2:]:
-                load.wait()
+            wo_copy.wait_recv()
 
         @pl.when(m >= 2)
         def _():
@@ -256,11 +356,11 @@
         def _():
             pl.semaphore_signal(x_free, inc=1, device_id={"pp": jnp.maximum(stage - 1, 0)}, device_id_type=MESH)
 
-        layer_norm(midb.at[slot], h2b, ln[2:3, :], ln[3:4, :])
+        layer_norm(midb.at[slot], h2b, ln[2][...], ln[3][...])
         h2_o.start()
 
     def mlp_part(m):
-        slot = lax.rem(m, 2)
+        slot = parity(m)
         _, _, _, _, s_o, a_o, _ = outs(m)
         _, _, _, _, s_p, a_p, _ = outs(jnp.maximum(m - 1, 0))
 
@@ -288,13 +388,40 @@
             attn_part(m)
             mlp_part(m)
 
+        @pl.when((m >= 1) & (m <= d_model // piece))
+        def _():
+            tb[...] = jnp.transpose(wo[cut(m - 1), :])
+            moved(tb, wot_o.at[:, cut(m - 1)])
+
         @pl.when(m > 0)
         def _():
             finish(m - 1)
 
         return carry
 
+    exchange_weights()
     lax.fori_loop(0, subs + 1, step, 0)
+
+    def sent(p, carry):
+        wq_copy(p).wait_send()
+        return carry
+
+    lax.fori_loop(0, direct, sent, 0)
+
+    @pl.when(stage < column)
+    def _():
+        for r in range(RELAYED):
+            relay_copy(0, r).wait_send()
+
+    @pl.when(stage >= column)
+    def _():
+        lax.fori_loop(direct, pieces, sent, 0)
+        for r in range(RELAYED):
+            relay_copy(1, r).wait_send()
+            relay_copy(2, r).wait_send()
+
+    wo_copy.wait_send()
+    bq_copy.wait_send()
     h1_o, qkv_o, o_o, h2_o, s_o, a_o, x_o = outs(subs - 1)
     for copy in (h1_o, qkv_o, o_o, h2_o, s_o, a_o):
         copy.wait()
@@ -309,9 +436,9 @@
 
 
 def bwd_kernel(subs, stages, width, tile,
-               dy_in, x_all, mid_all, s_all, qkv_all, w2t_h, w1t_h, wot_h, wot_p, wqt_h, wqt_p, ln,
+               dy_in, x_all, mid_all, s_all, qkv_all, w2t_h, w1t_h, wot_h, wqt_h, wqt_p, ln_h,
                dy_all, dpre_all, gmid_all, dqkv_all, gin_all, db1_o, db2_o, dbo_o, dbq_o, dln_o,
-               w2t, w1t, wot, wqt, dyb, slb, dpb, partb, peerb, rb, midb, xb, gmb, qkvb, gib, sb, db, pb, dsb, db1, db2, dbo, dbq, dln,
+               w2t, w1t, wot, wqt, dyb, slb, dpb, partb, peerb, rb, midb, xb, gmb, qkvb, gib, sb, db, pb, dsb, db1, db2, dbo, dbq, dln, ln,
                w_sem, in_sem, pre_sem, out_sem, dy_sem, gi_sem, part_send, part_recv, gi_send, dy_recv, dy_free):
     stage = lax.axis_index("pp")
     tp_me = lax.axis_index("tp")
@@ -323,14 +450,11 @@
     scale = width ** -0.5
     log2_scale = scale * LOG2_E
 
-    mine = pl.ds(pl.multiple_of(tp_me * half, 128), half)
-    theirs = pl.ds(pl.multiple_of(tp_peer * half, 128), half)
-    mine_q = pl.ds(pl.multiple_of(tp_me * (3 * half), 128), 3 * half)
-    theirs_q = pl.ds(pl.multiple_of(tp_peer * (3 * half), 128), 3 * half)
+    ln[...] = ln_h[...].astype(F32)
+    mine_q = pl.ds(pl.multiple_of(tp_me * (3 * half), LANES), 3 * half)
+    theirs_q = pl.ds(pl.multiple_of(tp_peer * (3 * half), LANES), 3 * half)
     loads = [pltpu.make_async_copy(src, dst, w_sem.at[i]) for i, (src, dst) in enumerate((
-        (w2t_h, w2t), (w1t_h, w1t), (wot_h, wot.at[:, mine]), (wot_p, wot.at[:, theirs]), (wqt_h, wqt.at[mine_q, :]), (wqt_p, wqt.at[theirs_q, :])))]
-    for load in loads:
-        load.start()
+        (w2t_h, w2t), (w1t_h, w1t), (wot_h, wot), (wqt_h, wqt.at[mine_q, :]), (wqt_p, wqt.at[theirs_q, :])))]
 
     def fetch(m):
         return (pltpu.make_async_copy(s_all.at[m], slb, pre_sem.at[0]),
@@ -338,37 +462,40 @@
                 pltpu.make_async_copy(qkv_all.at[m], qkvb, pre_sem.at[2]),
                 pltpu.make_async_copy(x_all.at[m], xb, pre_sem.at[3]))
 
-    for copy in fetch(0):
+    fetch(0)[0].start()
+    for load in loads[:2]:
+        load.start()
+    for copy in fetch(0)[1:]:
         copy.start()
     for acc in (db1, db2, dbo, dbq, dln):
         acc[...] = jnp.zeros_like(acc)
     for acc in (pb, dsb):
-        acc[:, 128:rows, 0:128] = jnp.zeros((4, rows - 128, 128), BF16)
+        acc[:, LANES:rows, 0:LANES] = jnp.zeros((4, rows - LANES, LANES), BF16)
     neighbour_barrier(stage, tp_peer, stages)
 
     def outs(m):
         return (pltpu.make_async_copy(dpb, dpre_all.at[m], out_sem.at[0]),
                 pltpu.make_async_copy(gmb, gmid_all.at[m], out_sem.at[1]),
-                pltpu.make_async_copy(qkvb.at[:, pl.ds(pl.multiple_of(tp_me * (3 * half), 128), 3 * half)], dqkv_all.at[m], out_sem.at[2]))
+                pltpu.make_async_copy(qkvb.at[:, pl.ds(pl.multiple_of(tp_me * (3 * half), LANES), 3 * half)], dqkv_all.at[m], out_sem.at[2]))
 
     def dy_load(m):
-        return pltpu.make_async_copy(dy_in.at[m], dyb.at[lax.rem(m, RING)], in_sem.at[lax.rem(m, 2)])
+        return pltpu.make_async_copy(dy_in.at[m], dyb.at[ring_slot(m)], in_sem.at[parity(m)])
 
     def dy_out(m):
-        return pltpu.make_async_copy(dyb.at[lax.rem(m, RING)], dy_all.at[m], dy_sem.at[lax.rem(m, 2)])
+        return pltpu.make_async_copy(dyb.at[ring_slot(m)], dy_all.at[m], dy_sem.at[parity(m)])
 
     def gi_out(m):
-        slot = lax.rem(m, 2)
+        slot = parity(m)
         return pltpu.make_async_copy(gib.at[slot], gin_all.at[m], gi_sem.at[slot])
 
     def part_copy(m):
-        slot = lax.rem(m, 2)
-        return pltpu.make_async_remote_copy(src_ref=partb.at[slot], dst_ref=peerb.at[lax.rem(m, RING)], send_sem=part_send.at[slot], recv_sem=part_recv.at[m],
+        slot = parity(m)
+        return pltpu.make_async_remote_copy(src_ref=partb.at[slot], dst_ref=peerb.at[ring_slot(m)], send_sem=part_send.at[slot], recv_sem=part_recv.at[m],
                                             device_id={"tp": tp_peer}, device_id_type=MESH)
 
     def prev_copy(m):
-        slot = lax.rem(m, 2)
-        return pltpu.make_async_remote_copy(src_ref=gib.at[slot], dst_ref=dyb.at[lax.rem(m, RING)], send_sem=gi_send.at[slot], recv_sem=dy_recv.at[m],
+        slot = parity(m)
+        return pltpu.make_async_remote_copy(src_ref=gib.at[slot], dst_ref=dyb.at[ring_slot(m)], send_sem=gi_send.at[slot], recv_sem=dy_recv.at[m],
                                             device_id={"pp": jnp.maximum(stage - 1, 0)}, device_id_type=MESH)
 
     @pl.when(stage == last_stage)
@@ -385,10 +512,10 @@
         return inv_std * (scaled - mean_scaled - normed * mean_proj)
 
     def mlp_part(m):
-        slot = lax.rem(m, 2)
+        slot = parity(m)
         slope_f = fetch(m)[0]
 
-        dy_slot = lax.rem(m, RING)
+        dy_slot = ring_slot(m)
 
         @pl.when(stage == last_stage)
         def _():
@@ -407,7 +534,8 @@
         @pl.when(m == 0)
         def _():
             loads[0].wait()
-            loads[1].wait()
+            for load in loads[2:]:
+                load.start()
 
         @pl.when(m > 0)
         def _():
@@ -423,6 +551,10 @@
         @pl.when(m + 1 < subs)
         def _():
             fetch(m + 1)[0].start()
+
+        @pl.when(m == 0)
+        def _():
+            loads[1].wait()
 
         for n in range(0, d_model, tile):
             partb[slot, :, n:n + tile] = dot_nn(dpb[...], w1t[:, n:n + tile]).astype(BF16)
@@ -444,10 +576,10 @@
 
         def softmax():
             for j in range(4):
-                for q0 in range(0, rows, 128):
-                    keys, lanes = q0 + 128, slice(q0, q0 + 128)
-                    krow = lax.broadcasted_iota(jnp.int32, (keys, 128), 0)
-                    qcol = lax.broadcasted_iota(jnp.int32, (keys, 128), 1) + q0
+                for q0 in range(0, rows, LANES):
+                    keys, lanes = q0 + LANES, slice(q0, q0 + LANES)
+                    krow = lax.broadcasted_iota(jnp.int32, (keys, LANES), 0)
+                    qcol = lax.broadcasted_iota(jnp.int32, (keys, LANES), 1) + q0
                     score = jnp.where(qcol >= krow, sb[j, 0:keys, lanes], NEG)
                     weight = jnp.exp2((score - jnp.max(score, axis=0, keepdims=True)) * log2_scale)
                     prob = weight * (1.0 / jnp.sum(weight, axis=0, keepdims=True))
@@ -468,9 +600,9 @@
             for c, parts in enumerate((d_query, d_key, d_value)):
                 for i, piece in enumerate(join_heads(parts, width)):
                     piece = piece.astype(BF16)
-                    first = base + c * half + i * 128
-                    qkvb[:, first:first + 128] = piece
-                    dbq[:, first:first + 128] += fold_rows(piece.astype(F32))
+                    first = base + c * half + i * LANES
+                    qkvb[:, first:first + LANES] = piece
+                    dbq[:, first:first + LANES] += fold_rows(piece.astype(F32))
 
         for group in range(d_model // (4 * width)):
             base = (group // 2) * (3 * half) + (group % 2) * (4 * width)
@@ -479,11 +611,11 @@
             products(group, base)
 
     def attn_part(m):
-        slot = lax.rem(m, 2)
+        slot = parity(m)
         _, mid_f, qkv_f, x_f = fetch(m)
         _, gm_o, dq_o = outs(m)
-        peer_slot = lax.rem(m, RING)
-        dy_slot = lax.rem(m, RING)
+        peer_slot = ring_slot(m)
+        dy_slot = ring_slot(m)
         mid_f.wait()
 
         @pl.when(m > 0)
@@ -586,7 +718,7 @@
 VMEM_LIMIT = 67043328
 
 
-def fwd_call(stages, width, tile, x_in, wq_own, wq_peer, wo_own, wo_peer, w1, w2, bq, bo, ln, b1, b2):
+def fwd_call(stages, width, tile, x_in, wqt_own, wo_own, w1, w2, bq, bo, b1, b2, ln):
     subs, rows, d_model = x_in.shape
     ff = w1.shape[1]
     half = d_model // 2
@@ -604,21 +736,23 @@
     return pl.pallas_call(
         functools.partial(fwd_kernel, subs, stages, width, tile),
         name="fwd_stage",
-        out_shape=(hbm(d_model), hbm(3 * d_model), hbm(half), hbm(d_model), hbm(d_model), hbm(d_model), hbm(ff, F32), hbm(ff), hbm(d_model)),
-        in_specs=[ANY] * 7 + [VMEM] * 5,
-        out_specs=[ANY] * 9,
+        out_shape=(hbm(d_model), hbm(3 * d_model), hbm(half), hbm(d_model), hbm(d_model), hbm(d_model), hbm(ff, F32), hbm(ff), hbm(d_model),
+                   jax.ShapeDtypeStruct((3 * half, d_model), BF16), jax.ShapeDtypeStruct((d_model, d_model), BF16), jax.ShapeDtypeStruct((ff, d_model), BF16), jax.ShapeDtypeStruct((d_model, ff), BF16),
+                   *[jax.ShapeDtypeStruct((RELAYED, rows, d_model), BF16)] * 2),
+        in_specs=[ANY] * 5 + [VMEM] * 5,
+        out_specs=[ANY] * 15,
         scratch_shapes=[
             pltpu.VMEM((d_model, 3 * d_model), BF16), pltpu.VMEM((d_model, d_model), BF16), pltpu.VMEM(w1.shape, BF16), pltpu.VMEM(w2.shape, BF16),
             pltpu.VMEM((RING, rows, d_model), BF16), buf(d_model), buf(3 * d_model), buf(d_model), two(d_model), buf(d_model), buf(ff, F32), buf(ff), two(d_model), pltpu.VMEM((RING, rows, d_model), BF16), two(d_model),
-            pltpu.VMEM((2, 4, rows, rows), F32), pltpu.VMEM((2, 4, rows, rows), BF16),
-            DMA((6,)), DMA((2,)), DMA((7,)), DMA((2,)), DMA((2,)), DMA((2,)), DMA((subs,)), DMA((2,)), DMA((subs,)), pltpu.SemaphoreType.REGULAR,
+            pltpu.VMEM((2, 4, rows, rows), F32), pltpu.VMEM((2, 4, rows, rows), BF16), pltpu.VMEM((2, 1, 3 * half), BF16), pltpu.VMEM((d_model, 256), BF16), pltpu.VMEM((1, ff + 6 * d_model), F32),
+            DMA((3,)), DMA, DMA((3 * half // 256,)), DMA((3 * half // 256,)), DMA, DMA, DMA, DMA, DMA((3, RELAYED)), DMA((2, RELAYED)), DMA((2,)), DMA((7,)), DMA((2,)), DMA((2,)), DMA((2,)), DMA((subs,)), DMA((2,)), DMA((subs,)), pltpu.SemaphoreType.REGULAR,
         ],
         cost_estimate=pl.CostEstimate(flops=subs * rows * weights, bytes_accessed=weights + subs * rows * d_model * 30, transcendentals=subs * rows * (ff + rows * 16)),
         compiler_params=pltpu.CompilerParams(collective_id=0, has_side_effects=True, vmem_limit_bytes=VMEM_LIMIT),
-    )(x_in, wq_own, wq_peer, wo_own, wo_peer, w1, w2, bq, bo, ln, b1, b2)
-
-
-def bwd_call(stages, width, tile, dy_in, x_all, mid_all, s_all, qkv_all, w2t, w1t, wot_own, wot_peer, wqt_own, wqt_peer, ln):
+    )(x_in, wqt_own, wo_own, w1, w2, bq, bo, b1, b2, ln)
+
+
+def bwd_call(stages, width, tile, dy_in, x_all, mid_all, s_all, qkv_all, w2t, w1t, wot, wqt_own, wqt_peer, ln):
     subs, rows, d_model = dy_in.shape
     ff = s_all.shape[2]
     half = d_model // 2
@@ -643,18 +777,18 @@
         name="bwd_stage",
         out_shape=(hbm(d_model), hbm(ff), hbm(d_model), hbm(3 * half), hbm(d_model),
                    acc(1, ff), acc(1, d_model), acc(1, d_model), acc(1, 3 * half), acc(4, d_model)),
-        in_specs=[ANY] * 11 + [VMEM],
+        in_specs=[ANY] * 10 + [VMEM],
         out_specs=[ANY] * 5 + [VMEM] * 5,
         scratch_shapes=[
             pltpu.VMEM(w2t.shape, BF16), pltpu.VMEM(w1t.shape, BF16), pltpu.VMEM((d_model, d_model), BF16), pltpu.VMEM((3 * d_model, d_model), BF16),
             ring, buf(ff, F32), buf(ff), two(d_model), ring, buf(d_model), buf(d_model), buf(d_model), buf(d_model), buf(3 * d_model), two(d_model),
             pltpu.VMEM((4, rows, rows), F32), pltpu.VMEM((4, rows, rows), F32), pltpu.VMEM((4, rows, rows), BF16), pltpu.VMEM((4, rows, rows), BF16),
-            pltpu.VMEM((8, ff), F32), pltpu.VMEM((8, d_model), F32), pltpu.VMEM((8, d_model), F32), pltpu.VMEM((8, 3 * d_model), F32), pltpu.VMEM((4, 8, d_model), F32),
-            DMA((6,)), DMA((2,)), DMA((4,)), DMA((3,)), DMA((2,)), DMA((2,)), DMA((2,)), DMA((subs,)), DMA((2,)), DMA((subs,)), pltpu.SemaphoreType.REGULAR,
+            pltpu.VMEM((8, ff), F32), pltpu.VMEM((8, d_model), F32), pltpu.VMEM((8, d_model), F32), pltpu.VMEM((8, 3 * d_model), F32), pltpu.VMEM((4, 8, d_model), F32), pltpu.VMEM((4, d_model), F32),
+            DMA((5,)), DMA((2,)), DMA((4,)), DMA((3,)), DMA((2,)), DMA((2,)), DMA((2,)), DMA((subs,)), DMA((2,)), DMA((subs,)), pltpu.SemaphoreType.REGULAR,
         ],
         cost_estimate=pl.CostEstimate(flops=subs * rows * weights, bytes_accessed=weights + subs * rows * d_model * 30, transcendentals=subs * rows * (ff + rows * 16)),
         compiler_params=pltpu.CompilerParams(collective_id=1, has_side_effects=True, vmem_limit_bytes=VMEM_LIMIT),
-    )(dy_in, x_all, mid_all, s_all, qkv_all, w2t, w1t, wot_own, wot_peer, wqt_own, wqt_peer, ln)
+    )(dy_in, x_all, mid_all, s_all, qkv_all, w2t, w1t, wot, wqt_own, wqt_peer, ln)
 
 
 def grad_kernel(n_tile, left, right, *refs):
@@ -705,7 +839,6 @@
 
 def solution(mesh):
     stages = mesh.shape["pp"]
-    swap = [(0, 1), (1, 0)]
 
     def stage_program(x_in, dy_out, w_qkv, b_qkv, w_out, b_out, ln_par, w_fc1, b_fc1, w_fc2, b_fc2):
         micro, batch, rows, d_model = x_in.shape
@@ -713,21 +846,13 @@
         half = heads * width
         subs = micro * batch
         tile = half
-        tp_me = lax.axis_index("tp")
 
         wqt_own = jnp.transpose(w_qkv[0], (0, 2, 3, 1)).reshape(3 * half, d_model)
-        wo_own = w_out[0].reshape(half, d_model)
-        wo_peer = lax.ppermute(wo_own, "tp", swap)
-        wqt_peer = lax.ppermute(wqt_own, "tp", swap)
-        bq_own = b_qkv[0].reshape(1, 3 * half)
-        bq_peer = lax.ppermute(bq_own, "tp", swap)
-        bq = jnp.concatenate([jnp.where(tp_me == 0, bq_own, bq_peer), jnp.where(tp_me == 0, bq_peer, bq_own)], axis=1).astype(F32)
-        w1, w2 = w_fc1[0], w_fc2[0]
-        ln = ln_par[0].astype(F32)
-        x_all, qkv_all, o_all, mid_all, h1_all, h2_all, s_all, a_all, y_all = fwd_call(
-            stages, width, tile, x_in.reshape(subs, rows, d_model), wqt_own.T, wqt_peer.T, wo_own, wo_peer, w1, w2, bq, b_out.astype(F32), ln, b_fc1.astype(F32), b_fc2.astype(F32))
+        ln = ln_par[0]
+        x_all, qkv_all, o_all, mid_all, h1_all, h2_all, s_all, a_all, y_all, wqt_peer, wot, w1t, w2t, _, _ = fwd_call(
+            stages, width, tile, x_in.reshape(subs, rows, d_model), wqt_own, w_out[0].reshape(half, d_model), w_fc1[0], w_fc2[0], b_qkv.reshape(1, -1), b_out, b_fc1, b_fc2, ln)
         dy_all, dpre_all, gmid_all, dqkv_all, gin_all, db1, db2, dbo, dbq, dln = bwd_call(
-            stages, width, tile, dy_out.reshape(subs, rows, d_model), x_all, mid_all, s_all, qkv_all, w2.T, w1.T, wo_own.T, wo_peer.T, wqt_own, wqt_peer, ln)
+            stages, width, tile, dy_out.reshape(subs, rows, d_model), x_all, mid_all, s_all, qkv_all, w2t, w1t, wot, wqt_own, wqt_peer, ln)
 
         def flat(stack):
             return stack.reshape(subs * rows, -1)

time: 1540 us -> 1480 us (0.961)
  Pallas kernels: 1240 us -> 1400 us
  waiting for transfers between devices: 157 us -> 0 us
  local copies, waits for them, and re-layouts: 59.6 us -> 7.28 us
    ppermute x3 -> x0, waiting for transfers between devices: 157 us -> none  [the longest x1 157 us: stage_program(): bq_peer = lax.ppermute(bq_own, 'tp', swap)]
    pallas_call x1, Pallas kernels: 430 us -> 587 us  [fwd_call(): pl.pallas_call(functools.partial(fwd_kernel, subs, stages, width, tile),...]
    unnamed x10 -> x4, local copies, waits for them, and re-layouts: 30.4 us -> 5.22 us
    transpose x2 -> x0, local copies, waits for them, and re-layouts: 20.5 us -> none  [stage_program(): x_all, qkv_all, o_all, mid_all, h1_all, h2_all, s_all, a_all, y_all = fwd...]
  transfers between devices with their start and end apart: 3 -> 0, of which waited for: 1 -> 0; matrix products, arithmetic and copies ran while one was open for 3% -> 0% of each run, Pallas kernels for 0% -> 0%
where the time goes in v6:
time: 1480 us; the launch traced here: 1470 us
  Pallas kernels  1400 us (95%)
  matrix products  54.5 us (4%)
    pallas_call x1, Pallas kernels, bwd_call(): pl.pallas_call(functools.partial(bwd_kernel, subs, stages, width, tile),...  650 us
    pallas_call x1, Pallas kernels, fwd_call(): pl.pallas_call(functools.partial(fwd_kernel, subs, stages, width, tile),...  587 us
    pallas_call x3, Pallas kernels, grad_call(): pl.pallas_call(functools.partial(grad_kernel, 512), name='weight_grad', g...  165 us
    dot_general x1, matrix products, dot_tn(): lax.dot_general(lhs, rhs, (((0,), (0,)), ((), ())), preferred_element_typ...  54.5 us

profile of v6, /device:TPU:0, one launch (start us, length us, event | category | flops | bytes accessed | tf_op | source)
XLA Modules:
  0.0 1465.7 jit_solution(6631292275591482116)
XLA Ops:
  0.6 1.4 reshape.65.bq
  2.0 586.6 %fwd_stage.1 = (bf16[24,256,1536]{2,1,0:T(8,128)(2,1)}, bf16[24,256,4608]{2,1,0:T(8,128)(2,1)}, bf16[24,256,768]{2,1,0:T(8,128)(2,1)}, bf16[24,256,1536]{2,1,0:T...) custom-call(bf16[24,256,1536]{2,1,0:T(8,128)(2,1)} %bitcast.35, ...), custom_call_target="tpu_custom_call" | custom-call | flops 231928233984 | bytes 320864256 | tf_op jit(solution)/shard_map/fwd_stage/pallas_call | solution.py:736
  588.6 650.3 %bwd_stage.1 = (bf16[24,256,1536]{2,1,0:T(8,128)(2,1)}, bf16[24,256,3072]{2,1,0:T(8,128)(2,1)}, bf16[24,256,1536]{2,1,0:T(8,128)(2,1)}, bf16[24,256,2304]{2,1,0:...) custom-call(bf16[24,256,1536]{2,1,0:T(8,128)(2,1)} %bitcast.36, ...), custom_call_target="tpu_custom_call" | custom-call | flops 231928233984 | bytes 320864256 | tf_op jit(solution)/shard_map/bwd_stage/pallas_call | solution.py:775
  1239.0 21.0 %weight_grad.5 = f32[768,1536]{1,0:T(8,128)} custom-call(bf16[6144,768]{1,0:T(8,128)(2,1)} %bitcast.54, bf16[6144,1536]{1,0:T(8,128)(2,1)} %bitcast.52), custom_call_target="tpu_custom_call" | custom-call | flops 14495514624 | bytes 33030144 | tf_op jit(solution)/shard_map/weight_grad/pallas_call | solution.py:828
  1260.0 54.5 %convolution_bitcast_fusion = f32[2304,1536]{1,0:T(8,128)} fusion(bf16[24,256,2304]{2,1,0:T(8,128)(2,1)} %get-tuple-element.54, bf16[24,256,1536]{2,1,0:T(8,128)(2,1)} %get-tuple-element.55), kind=kOutput, calls=%fused_computation | convolution fusion | flops 43486543872 | bytes 61341696 | tf_op jit(solution)/shard_map/dot_general | solution.py:44
  1314.5 72.0 %weight_grad.3 = (f32[3072,1536]{1,0:T(8,128)}, bf16[24,256,1536]{2,1,0:T(8,128)(2,1)}) custom-call(bf16[6144,3072]{1,0:T(8,128)(2,1)} %bitcast.44, bf16[6144,1536]{1,0:T(8,128)(2,1)} %bitcast.51, bf16[24,256,1536]{2,1,0:T(8,128)(2,1)} %get-tuple-element.48.refs_0_), custom_call_target="tpu_custom_call" | custom-call | flops 57982058496 | bytes 113246208 | tf_op jit(solution)/shard_map/weight_grad/pallas_call | solution.py:828
  1386.5 72.1 %weight_grad.4 = (f32[1536,3072]{1,0:T(8,128)}, bf16[24,256,1536]{2,1,0:T(8,128)(2,1)}) custom-call(bf16[6144,1536]{1,0:T(8,128)(2,1)} %bitcast.46, bf16[6144,3072]{1,0:T(8,128)(2,1)} %bitcast.45, bf16[24,256,1536]{2,1,0:T(8,128)(2,1)} %get-tuple-element.52.refs_0_), custom_call_target="tpu_custom_call" | custom-call | flops 57982058496 | bytes 113246208 | tf_op jit(solution)/shard_map/weight_grad/pallas_call | solution.py:828
  1458.6 0.7 reduce
  1459.3 0.7 broadcast_in_dim_reshape.6
  1460.0 1.3 copy.28
  1461.3 1.3 copy.29
  1462.6 1.3 copy.30
  1464.0 1.3 copy.31

commit v7 on v6

--- a/solution.py
+++ b/solution.py
@@ -24,6 +24,10 @@
 WINDOWS = ((0, 128, 0), (0, 256, 96), (128, 256, 64), (256, 128, 32))
 
 
+def starts(total, step):
+    return range(0, total, step)
+
+
 def parity(m):
     return lax.rem(m, 2)
 
@@ -78,7 +82,7 @@
 
 def fwd_kernel(subs, stages, width, tile,
                x_in, wqt_h, wo_h, w1_h, w2_h, bq, bo_h, b1_h, b2_h, ln_h,
-               x_all, qkv_all, o_all, mid_all, h1_all, h2_all, s_all, a_all, y_all, wqt_p, wot_o, w1t_o, w2t_o, relay_in, relay_out,
+               x_all, qkv_all, o_all, mid_all, h1_all, h2_all, s_all, a_all, y_all, part_all, wqt_p, wot_o, w1t_o, w2t_o, relay_in, relay_out,
                wq, wo, w1, w2, xr, h1b, qkvb, ob, midb, h2b, slb, ab, partb, peerb, yb, sb, pb, bqb, tb, par,
                w_sem, t_sem, wq_send, wq_recv, wo_send, wo_recv, bq_send, bq_recv, relay_send, relay_recv, in_sem, out_sem, mid_sem, y_sem, part_send, part_recv, y_send, x_recv, x_free):
     stage = lax.axis_index("pp")
@@ -87,6 +91,7 @@
     last_stage = stages - 1
     _, rows, d_model = xr.shape
     half = d_model // 2
+    trio = 3 * half
     ff = slb.shape[1]
     scale = width ** -0.5
     log2_scale = scale * LOG2_E
@@ -101,7 +106,7 @@
     bo, b1, b2, *ln = rows_of
     mine = pl.ds(pl.multiple_of(tp_me * half, LANES), half)
     piece = 256
-    pieces = 3 * half // piece
+    pieces = trio // piece
     peer_id = {"device_id": {"tp": tp_peer}, "device_id_type": MESH}
     loads = [pltpu.make_async_copy(src, dst, w_sem.at[i]) for i, (src, dst) in enumerate(((wo_h, wo.at[mine, :]), (w1_h, w1), (w2_h, w2)))]
 
@@ -131,7 +136,7 @@
 
     def turn(source, owner, p):
         moved(source.at[cut(p), :], h1b)
-        wq[:, pl.ds(pl.multiple_of(owner * (3 * half) + p * piece, LANES), piece)] = jnp.transpose(h1b[...])
+        wq[:, pl.ds(pl.multiple_of(owner * trio + p * piece, LANES), piece)] = jnp.transpose(h1b[...])
 
     def exchange_weights():
         def send(p, carry):
@@ -219,6 +224,10 @@
         return pltpu.make_async_remote_copy(src_ref=partb.at[slot], dst_ref=peerb.at[ring_slot(m)], send_sem=part_send.at[slot], recv_sem=part_recv.at[m],
                                             device_id={"tp": tp_peer}, device_id_type=MESH)
 
+    def part_out(m):
+        slot = parity(m)
+        return pltpu.make_async_copy(partb.at[slot], part_all.at[m], y_sem.at[slot])
+
     def next_copy(m):
         slot = parity(m)
         return pltpu.make_async_remote_copy(src_ref=yb.at[slot], dst_ref=xr.at[ring_slot(m)], send_sem=y_send.at[slot], recv_sem=x_recv.at[m],
@@ -232,12 +241,12 @@
         x_load(0).start()
 
     def layer_norm(src, dst, gain, shift):
-        for r in range(0, rows, ROW_CHUNK):
+        for r in starts(rows, ROW_CHUNK):
             normed, _ = norm_stats(src[r:r + ROW_CHUNK, :].astype(F32))
             dst[r:r + ROW_CHUNK, :] = (normed * gain + shift).astype(BF16)
 
     def group_base(group):
-        return (group // 2) * (3 * half) + (group % 2) * (4 * width)
+        return (group // 2) * trio + (group % 2) * (4 * width)
 
     def attend():
         def scores(group):
@@ -249,7 +258,7 @@
 
         def softmax(group):
             for j in range(4):
-                for r0 in range(0, rows, SOFT_ROWS):
+                for r0 in starts(rows, SOFT_ROWS):
                     keys = LANES * (r0 // LANES + 1)
                     row = lax.broadcasted_iota(jnp.int32, (SOFT_ROWS, keys), 0) + r0
                     col = lax.broadcasted_iota(jnp.int32, (SOFT_ROWS, keys), 1)
@@ -281,23 +290,17 @@
         @pl.when(m >= 2)
         def _():
             y_out(m - 2).wait()
-
-            @pl.when(stage < last_stage)
-            def _():
-                next_copy(m - 2).wait_send()
-
-        for r in range(0, rows, ROW_CHUNK):
+            next_copy(m - 2).wait_send()
+
+        for r in starts(rows, ROW_CHUNK):
             both = partb[slot, r:r + ROW_CHUNK, :].astype(F32) + peerb[peer_slot, r:r + ROW_CHUNK, :].astype(F32)
             yb[slot, r:r + ROW_CHUNK, :] = (midb[slot, r:r + ROW_CHUNK, :].astype(F32) + both + b2[...]).astype(BF16)
 
-        @pl.when(stage < last_stage)
-        def _():
-            @pl.when(m >= RING)
-            def _():
-                pl.semaphore_wait(x_free, 1)
-
-            next_copy(m).start()
-
+        @pl.when(m >= RING)
+        def _():
+            pl.semaphore_wait(x_free, 1)
+
+        next_copy(m).start()
         y_out(m).start()
         part_copy(m).wait_send()
 
@@ -332,8 +335,8 @@
         layer_norm(xb, h1b, ln[0][...], ln[1][...])
         h1_o.start()
 
-        for n in range(0, 3 * d_model, tile):
-            owner, lane = divmod(n, 3 * half)
+        for n in starts(3 * d_model, tile):
+            owner, lane = divmod(n, trio)
             qkvb[:, n:n + tile] = (dot_nn(h1b[...], wq[:, n:n + tile]) + bqb[owner, :, lane:lane + tile].astype(F32)).astype(BF16)
         qkv_o.start()
         attend()
@@ -347,7 +350,7 @@
         def _():
             mid_out(m - 2).wait()
 
-        for n in range(0, d_model, tile):
+        for n in starts(d_model, tile):
             midb[slot, :, n:n + tile] = (xb[:, n:n + tile].astype(F32) + dot_nn(ob[...], wo[:, n:n + tile]) + bo[:, n:n + tile]).astype(BF16)
         mid_out(m).start()
         x_o.wait()
@@ -369,7 +372,7 @@
             s_p.wait()
             a_p.wait()
 
-        for n in range(0, ff, tile):
+        for n in starts(ff, tile):
             pre = dot_nn(h2b[...], w1[:, n:n + tile]) + b1[:, n:n + tile]
             square = pre * pre
             bend = jnp.tanh(pre * (GELU_C + (GELU_C * GELU_K) * square))
@@ -378,9 +381,21 @@
             slb[:, n:n + tile] = cdf + (0.5 * pre) * (1.0 - bend * bend) * (GELU_C + (3.0 * GELU_C * GELU_K) * square)
         s_o.start()
         a_o.start()
-        for n in range(0, d_model, tile):
+
+        @pl.when((stage == last_stage) & (m >= 2))
+        def _():
+            part_out(m - 2).wait()
+
+        for n in starts(d_model, tile):
             partb[slot, :, n:n + tile] = dot_nn(ab[...], w2[:, n:n + tile]).astype(BF16)
-        part_copy(m).start()
+
+        @pl.when(stage < last_stage)
+        def _():
+            part_copy(m).start()
+
+        @pl.when(stage == last_stage)
+        def _():
+            part_out(m).start()
 
     def step(m, carry):
         @pl.when(m < subs)
@@ -393,7 +408,7 @@
             tb[...] = jnp.transpose(wo[cut(m - 1), :])
             moved(tb, wot_o.at[:, cut(m - 1)])
 
-        @pl.when(m > 0)
+        @pl.when((m > 0) & (stage < last_stage))
         def _():
             finish(m - 1)
 
@@ -428,11 +443,15 @@
 
     for m in (subs - 2, subs - 1):
         mid_out(m).wait()
-        y_out(m).wait()
 
         @pl.when(stage < last_stage)
         def _():
+            y_out(m).wait()
             next_copy(m).wait_send()
+
+        @pl.when(stage == last_stage)
+        def _():
+            part_out(m).wait()
 
 
 def bwd_kernel(subs, stages, width, tile,
@@ -446,13 +465,14 @@
     last_stage = stages - 1
     rows, d_model = xb.shape
     half = d_model // 2
+    trio = 3 * half
     ff = slb.shape[1]
     scale = width ** -0.5
     log2_scale = scale * LOG2_E
 
     ln[...] = ln_h[...].astype(F32)
-    mine_q = pl.ds(pl.multiple_of(tp_me * (3 * half), LANES), 3 * half)
-    theirs_q = pl.ds(pl.multiple_of(tp_peer * (3 * half), LANES), 3 * half)
+    mine_q = pl.ds(pl.multiple_of(tp_me * trio, LANES), trio)
+    theirs_q = pl.ds(pl.multiple_of(tp_peer * trio, LANES), trio)
     loads = [pltpu.make_async_copy(src, dst, w_sem.at[i]) for i, (src, dst) in enumerate((
         (w2t_h, w2t), (w1t_h, w1t), (wot_h, wot), (wqt_h, wqt.at[mine_q, :]), (wqt_p, wqt.at[theirs_q, :])))]
 
@@ -476,7 +496,7 @@
     def outs(m):
         return (pltpu.make_async_copy(dpb, dpre_all.at[m], out_sem.at[0]),
                 pltpu.make_async_copy(gmb, gmid_all.at[m], out_sem.at[1]),
-                pltpu.make_async_copy(qkvb.at[:, pl.ds(pl.multiple_of(tp_me * (3 * half), LANES), 3 * half)], dqkv_all.at[m], out_sem.at[2]))
+                pltpu.make_async_copy(qkvb.at[:, pl.ds(pl.multiple_of(tp_me * trio, LANES), trio)], dqkv_all.at[m], out_sem.at[2]))
 
     def dy_load(m):
         return pltpu.make_async_copy(dy_in.at[m], dyb.at[ring_slot(m)], in_sem.at[parity(m)])
@@ -542,7 +562,7 @@
             outs(m - 1)[0].wait()
 
         slope_f.wait()
-        for n in range(0, ff, tile):
+        for n in starts(ff, tile):
             grad = dot_nn(dyb[dy_slot], w2t[:, n:n + tile]).astype(BF16).astype(F32) * slb[:, n:n + tile]
             db1[:, n:n + tile] += fold_rows(grad)
             dpb[:, n:n + tile] = grad.astype(BF16)
@@ -556,7 +576,7 @@
         def _():
             loads[1].wait()
 
-        for n in range(0, d_model, tile):
+        for n in starts(d_model, tile):
             partb[slot, :, n:n + tile] = dot_nn(dpb[...], w1t[:, n:n + tile]).astype(BF16)
         part_copy(m).start()
 
@@ -576,7 +596,7 @@
 
         def softmax():
             for j in range(4):
-                for q0 in range(0, rows, LANES):
+                for q0 in starts(rows, LANES):
                     keys, lanes = q0 + LANES, slice(q0, q0 + LANES)
                     krow = lax.broadcasted_iota(jnp.int32, (keys, LANES), 0)
                     qcol = lax.broadcasted_iota(jnp.int32, (keys, LANES), 1) + q0
@@ -605,7 +625,7 @@
                     dbq[:, first:first + LANES] += fold_rows(piece.astype(F32))
 
         for group in range(d_model // (4 * width)):
-            base = (group // 2) * (3 * half) + (group % 2) * (4 * width)
+            base = (group // 2) * trio + (group % 2) * (4 * width)
             scores(group, base)
             softmax()
             products(group, base)
@@ -628,7 +648,7 @@
                 load.wait()
 
         part_copy(m).wait_recv()
-        for r in range(0, rows, ROW_CHUNK):
+        for r in starts(rows, ROW_CHUNK):
             rr = slice(r, r + ROW_CHUNK)
             grad = (partb[slot, rr, :].astype(F32) + peerb[peer_slot, rr, :].astype(F32)).astype(BF16).astype(F32)
             d_y = dyb[dy_slot, rr, :].astype(F32)
@@ -647,13 +667,13 @@
         def _():
             fetch(m + 1)[1].start()
 
-        for n in range(0, d_model, tile):
+        for n in starts(d_model, tile):
             rb[:, n:n + tile] = dot_nn(gmb[...], wot[:, n:n + tile]).astype(BF16)
         qkv_f.wait()
         attend_grad()
         dq_o.start()
         part_copy(m).wait_send()
-        for n in range(0, d_model, tile):
+        for n in starts(d_model, tile):
             rb[:, n:n + tile] = dot_nn(qkvb[...], wqt[:, n:n + tile]).astype(BF16)
         x_f.wait()
 
@@ -665,7 +685,7 @@
             def _():
                 prev_copy(m - 2).wait_send()
 
-        for r in range(0, rows, ROW_CHUNK):
+        for r in starts(rows, ROW_CHUNK):
             rr = slice(r, r + ROW_CHUNK)
             total = gmb[rr, :].astype(F32) + norm_grad(xb[rr, :].astype(F32), rb[rr, :].astype(F32), ln[0:1, :], 0)
             gib[slot, rr, :] = total.astype(BF16)
@@ -722,6 +742,7 @@
     subs, rows, d_model = x_in.shape
     ff = w1.shape[1]
     half = d_model // 2
+    trio = 3 * half
 
     def hbm(cols, dtype=BF16):
         return jax.ShapeDtypeStruct((subs, rows, cols), dtype)
@@ -736,16 +757,16 @@
     return pl.pallas_call(
         functools.partial(fwd_kernel, subs, stages, width, tile),
         name="fwd_stage",
-        out_shape=(hbm(d_model), hbm(3 * d_model), hbm(half), hbm(d_model), hbm(d_model), hbm(d_model), hbm(ff, F32), hbm(ff), hbm(d_model),
-                   jax.ShapeDtypeStruct((3 * half, d_model), BF16), jax.ShapeDtypeStruct((d_model, d_model), BF16), jax.ShapeDtypeStruct((ff, d_model), BF16), jax.ShapeDtypeStruct((d_model, ff), BF16),
+        out_shape=(hbm(d_model), hbm(3 * d_model), hbm(half), hbm(d_model), hbm(d_model), hbm(d_model), hbm(ff, F32), hbm(ff), hbm(d_model), hbm(d_model),
+                   jax.ShapeDtypeStruct((trio, d_model), BF16), jax.ShapeDtypeStruct((d_model, d_model), BF16), jax.ShapeDtypeStruct((ff, d_model), BF16), jax.ShapeDtypeStruct((d_model, ff), BF16),
                    *[jax.ShapeDtypeStruct((RELAYED, rows, d_model), BF16)] * 2),
         in_specs=[ANY] * 5 + [VMEM] * 5,
-        out_specs=[ANY] * 15,
+        out_specs=[ANY] * 16,
         scratch_shapes=[
             pltpu.VMEM((d_model, 3 * d_model), BF16), pltpu.VMEM((d_model, d_model), BF16), pltpu.VMEM(w1.shape, BF16), pltpu.VMEM(w2.shape, BF16),
             pltpu.VMEM((RING, rows, d_model), BF16), buf(d_model), buf(3 * d_model), buf(d_model), two(d_model), buf(d_model), buf(ff, F32), buf(ff), two(d_model), pltpu.VMEM((RING, rows, d_model), BF16), two(d_model),
-            pltpu.VMEM((2, 4, rows, rows), F32), pltpu.VMEM((2, 4, rows, rows), BF16), pltpu.VMEM((2, 1, 3 * half), BF16), pltpu.VMEM((d_model, 256), BF16), pltpu.VMEM((1, ff + 6 * d_model), F32),
-            DMA((3,)), DMA, DMA((3 * half // 256,)), DMA((3 * half // 256,)), DMA, DMA, DMA, DMA, DMA((3, RELAYED)), DMA((2, RELAYED)), DMA((2,)), DMA((7,)), DMA((2,)), DMA((2,)), DMA((2,)), DMA((subs,)), DMA((2,)), DMA((subs,)), pltpu.SemaphoreType.REGULAR,
+            pltpu.VMEM((2, 4, rows, rows), F32), pltpu.VMEM((2, 4, rows, rows), BF16), pltpu.VMEM((2, 1, trio), BF16), pltpu.VMEM((d_model, 256), BF16), pltpu.VMEM((1, ff + 6 * d_model), F32),
+            DMA((3,)), DMA, DMA((trio // 256,)), DMA((trio // 256,)), DMA, DMA, DMA, DMA, DMA((3, RELAYED)), DMA((2, RELAYED)), DMA((2,)), DMA((7,)), DMA((2,)), DMA((2,)), DMA((2,)), DMA((subs,)), DMA((2,)), DMA((subs,)), pltpu.SemaphoreType.REGULAR,
         ],
         cost_estimate=pl.CostEstimate(flops=subs * rows * weights, bytes_accessed=weights + subs * rows * d_model * 30, transcendentals=subs * rows * (ff + rows * 16)),
         compiler_params=pltpu.CompilerParams(collective_id=0, has_side_effects=True, vmem_limit_bytes=VMEM_LIMIT),
@@ -756,6 +777,7 @@
     subs, rows, d_model = dy_in.shape
     ff = s_all.shape[2]
     half = d_model // 2
+    trio = 3 * half
 
     def hbm(cols, dtype=BF16):
         return jax.ShapeDtypeStruct((subs, rows, cols), dtype)
@@ -775,8 +797,8 @@
     return pl.pallas_call(
         functools.partial(bwd_kernel, subs, stages, width, tile),
         name="bwd_stage",
-        out_shape=(hbm(d_model), hbm(ff), hbm(d_model), hbm(3 * half), hbm(d_model),
-                   acc(1, ff), acc(1, d_model), acc(1, d_model), acc(1, 3 * half), acc(4, d_model)),
+        out_shape=(hbm(d_model), hbm(ff), hbm(d_model), hbm(trio), hbm(d_model),
+                   acc(1, ff), acc(1, d_model), acc(1, d_model), acc(1, trio), acc(4, d_model)),
         in_specs=[ANY] * 10 + [VMEM],
         out_specs=[ANY] * 5 + [VMEM] * 5,
         scratch_shapes=[
@@ -791,50 +813,61 @@
     )(dy_in, x_all, mid_all, s_all, qkv_all, w2t, w1t, wot, wqt_own, wqt_peer, ln)
 
 
-def grad_kernel(n_tile, left, right, *refs):
-    if len(refs) == 3:
-        kept, out, kept_out = refs
-        kept_out[...] = kept[...]
+def grad_kernel(last_stage, extra_count, stage, left, right, *refs):
+    extras, out, passed = refs[:extra_count], refs[extra_count], refs[extra_count + 1:]
+    if len(extras) == len(passed):
+        for src, dst in zip(extras, passed):
+            dst[...] = src[...]
     else:
-        out, = refs
+        y, mid, own, peer, b2 = extras
+
+        @pl.when(stage[0] < last_stage)
+        def _():
+            passed[0][...] = y[...]
+
+        @pl.when(stage[0] == last_stage)
+        def _():
+            both = own[...].astype(F32) + peer[...].astype(F32)
+            passed[0][...] = (mid[...].astype(F32) + both + b2[...].astype(F32)).astype(BF16)
 
     @pl.when(pl.program_id(1) == 0)
     def _():
         out[...] = jnp.zeros_like(out)
 
-    for n in range(0, out.shape[1], n_tile):
-        lanes = slice(n, n + n_tile)
-        out[:, lanes] += dot_tn(left[...], right[:, lanes])
-
-
-def grad_call(left, right, m_block, n_block, k_block, kept=None):
+    n_tile = 512
+    for n in starts(out.shape[1], n_tile):
+        out[:, n:n + n_tile] += dot_tn(left[...], right[:, n:n + n_tile])
+
+
+def grad_call(stage, last_stage, left, right, m_block, n_block, k_block, extras=(), passed=0):
     tokens, m_size = left.shape
     n_size = right.shape[1]
     m_count = m_size // m_block
     grid = (m_count * (n_size // n_block), tokens // k_block)
-    in_specs = [pl.BlockSpec((k_block, m_block), lambda i, k: (k, i % m_count)), pl.BlockSpec((k_block, n_block), lambda i, k: (k, i // m_count))]
-    out_specs = [pl.BlockSpec((m_block, n_block), lambda i, k: (i % m_count, i // m_count))]
-    out_shape = [jax.ShapeDtypeStruct((m_size, n_size), F32)]
-    args = [left, right]
-    if kept is not None:
-        steps = grid[0] * grid[1]
-        assert kept.shape[0] % steps == 0
-        spec = pl.BlockSpec((kept.shape[0] // steps,) + kept.shape[1:], lambda i, k: (i * grid[1] + k, 0, 0))
-        in_specs.append(spec)
-        out_specs.append(spec)
-        out_shape.append(jax.ShapeDtypeStruct(kept.shape, kept.dtype))
-        args.append(kept)
+    steps = grid[0] * grid[1]
+
+    def spec(array, used=lambda s: 1):
+        if array.ndim == 2:
+            return pl.BlockSpec(array.shape, lambda i, k, s: (0, 0))
+        block = (array.shape[0] // steps,) + array.shape[1:]
+        return pl.BlockSpec(block, lambda i, k, s: ((i * grid[1] + k) * used(s), 0, 0))
+
+    in_specs = [pl.BlockSpec((k_block, m_block), lambda i, k, s: (k, i % m_count)), pl.BlockSpec((k_block, n_block), lambda i, k, s: (k, i // m_count))]
+    if len(extras) > passed:
+        in_specs += [spec(extras[0], lambda s: 1 - s[0] // last_stage)] + [spec(array, lambda s: s[0] // last_stage) for array in extras[1:]]
+    else:
+        in_specs += [spec(array) for array in extras]
     moved = 2 * tokens * (m_size * (n_size // n_block) + n_size * m_count) + 4 * m_size * n_size
     return pl.pallas_call(
-        functools.partial(grad_kernel, 512),
+        functools.partial(grad_kernel, last_stage, len(extras)),
         name="weight_grad",
-        grid=grid,
-        in_specs=in_specs,
-        out_specs=out_specs,
-        out_shape=out_shape,
+        grid_spec=pltpu.PrefetchScalarGridSpec(
+            num_scalar_prefetch=1, grid=grid, in_specs=in_specs,
+            out_specs=[pl.BlockSpec((m_block, n_block), lambda i, k, s: (i % m_count, i // m_count))] + [spec(array) for array in extras[:passed]]),
+        out_shape=[jax.ShapeDtypeStruct((m_size, n_size), F32)] + [jax.ShapeDtypeStruct(array.shape, array.dtype) for array in extras[:passed]],
         cost_estimate=pl.CostEstimate(flops=2 * tokens * m_size * n_size, bytes_accessed=moved, transcendentals=0),
         compiler_params=pltpu.CompilerParams(dimension_semantics=("arbitrary", "arbitrary"), vmem_limit_bytes=VMEM_LIMIT),
-    )(*args)
+    )(stage, left, right, *extras)
 
 
 def solution(mesh):
@@ -849,7 +882,7 @@
 
         wqt_own = jnp.transpose(w_qkv[0], (0, 2, 3, 1)).reshape(3 * half, d_model)
         ln = ln_par[0]
-        x_all, qkv_all, o_all, mid_all, h1_all, h2_all, s_all, a_all, y_all, wqt_peer, wot, w1t, w2t, _, _ = fwd_call(
+        x_all, qkv_all, o_all, mid_all, h1_all, h2_all, s_all, a_all, y_all, part_all, wqt_peer, wot, w1t, w2t, _, _ = fwd_call(
             stages, width, tile, x_in.reshape(subs, rows, d_model), wqt_own, w_out[0].reshape(half, d_model), w_fc1[0], w_fc2[0], b_qkv.reshape(1, -1), b_out, b_fc1, b_fc2, ln)
         dy_all, dpre_all, gmid_all, dqkv_all, gin_all, db1, db2, dbo, dbq, dln = bwd_call(
             stages, width, tile, dy_out.reshape(subs, rows, d_model), x_all, mid_all, s_all, qkv_all, w2t, w1t, wot, wqt_own, wqt_peer, ln)
@@ -857,9 +890,13 @@
         def flat(stack):
             return stack.reshape(subs * rows, -1)
 
-        g_w_fc2, h_out = grad_call(flat(a_all), flat(dy_all), 1024, d_model, 1536, y_all)
-        g_w_fc1, g_in = grad_call(flat(h2_all), flat(dpre_all), d_model, 1024, 1536, gin_all)
-        g_w_out, = grad_call(flat(o_all), flat(gmid_all), half, d_model, 1536)
+        last_stage = stages - 1
+        stage = lax.axis_index("pp").reshape(1)
+        held, _ = lax.optimization_barrier((part_all, gin_all))
+        peer_part = lax.ppermute(held, ("tp", "pp"), [(last_stage, stages + last_stage), (stages + last_stage, last_stage)])
+        g_w_out, dbo, dln, db1, db2 = grad_call(stage, last_stage, flat(o_all), flat(gmid_all), half, d_model, d_model, (dbo, dln, db1, db2), 4)
+        g_w_fc1, g_in = grad_call(stage, last_stage, flat(h2_all), flat(dpre_all), d_model, 1024, d_model, (gin_all,), 1)
+        g_w_fc2, h_out = grad_call(stage, last_stage, flat(a_all), flat(dy_all), 1024, d_model, d_model, (y_all, mid_all, part_all, peer_part, b_fc2), 1)
         g_w_qkv = lax.optimization_barrier(dot_tn(flat(dqkv_all), flat(h1_all)))
         g_w_out = g_w_out.reshape(heads, width, d_model)
         g_w_qkv = jnp.transpose(g_w_qkv.reshape(3, heads, width, d_model), (0, 3, 1, 2))

time: 1480 us -> 1470 us (level)
  transfers between devices with their start and end apart: 0 -> 1, of which waited for: 0 -> 0; matrix products, arithmetic and copies ran while one was open for 0% -> 4% of each run, Pallas kernels for 0% -> 6%
where the time goes in v7:
time: 1470 us; the launch traced here: 1460 us
  Pallas kernels  1390 us (95%)
  matrix products  54.5 us (4%)
    pallas_call x1, Pallas kernels, bwd_call(): pl.pallas_call(functools.partial(bwd_kernel, subs, stages, width, tile),...  636 us
    pallas_call x1, Pallas kernels, fwd_call(): pl.pallas_call(functools.partial(fwd_kernel, subs, stages, width, tile),...  589 us
    pallas_call x3, Pallas kernels, grad_call(): pl.pallas_call(functools.partial(grad_kernel, last_stage, len(extras)), n...  167 us
    dot_general x1, matrix products, dot_tn(): lax.dot_general(lhs, rhs, (((0,), (0,)), ((), ())), preferred_element_typ...  54.5 us
  transfers between devices with their start and end apart: 1, of which 0 were waited for; matrix products, arithmetic and copies ran while one was open for 4% of the time, Pallas kernels for 6%

profile of v7, /device:TPU:0, one launch (start us, length us, event | category | flops | bytes accessed | tf_op | source)
XLA Modules:
  0.0 1457.3 jit_solution(13903493226634893293)
XLA Ops:
  0.6 1.4 reshape.69.bq
  2.0 589.1 %fwd_stage.1 = (bf16[24,256,1536]{2,1,0:T(8,128)(2,1)}, bf16[24,256,4608]{2,1,0:T(8,128)(2,1)}, bf16[24,256,768]{2,1,0:T(8,128)(2,1)}, bf16[24,256,1536]{2,1,0:T...) custom-call(bf16[24,256,1536]{2,1,0:T(8,128)(2,1)} %bitcast.35, ...), custom_call_target="tpu_custom_call" | custom-call | flops 231928233984 | bytes 320864256 | tf_op jit(solution)/shard_map/fwd_stage/pallas_call | solution.py:757
  591.1 636.0 %bwd_stage.1 = (bf16[24,256,1536]{2,1,0:T(8,128)(2,1)}, bf16[24,256,3072]{2,1,0:T(8,128)(2,1)}, bf16[24,256,1536]{2,1,0:T(8,128)(2,1)}, bf16[24,256,2304]{2,1,0:...) custom-call(bf16[24,256,1536]{2,1,0:T(8,128)(2,1)} %bitcast.36, ...), custom_call_target="tpu_custom_call" | custom-call | flops 231928233984 | bytes 320864256 | tf_op jit(solution)/shard_map/bwd_stage/pallas_call | solution.py:797
  1227.1 7.2 collective-permute-start
  1234.3 0.0 copy-start
  1234.3 54.5 %convolution_bitcast_fusion = f32[2304,1536]{1,0:T(8,128)} fusion(bf16[24,256,2304]{2,1,0:T(8,128)(2,1)} %get-tuple-element.63, bf16[24,256,1536]{2,1,0:T(8,128)(2,1)} %get-tuple-element.64), kind=kOutput, calls=%fused_computation | convolution fusion | flops 43486543872 | bytes 61341696 | tf_op jit(solution)/shard_map/dot_general | solution.py:48
  1288.8 0.0 copy-done
  1288.9 0.7 broadcast_in_dim_reshape.6
  1289.5 21.1 %weight_grad.5 = (f32[768,1536]{1,0:T(8,128)}, f32[1,1536]{1,0:T(1,128)}, f32[4,1536]{1,0:T(4,128)}, f32[1,3072]{1,0:T(1,128)}, f32[1,1536]{1,0:T(1,128)}) custom-call(s32[1]{0:T(128)} %bitcast.stage, bf16[6144,768]{1,0:T(8,128)(2,1)} %bitcast.54, bf16[6144,1536]{1,0:T(8,128)(2,1)} %bitcast.50, f32[1,1536]{1,0:T(1,128)} %get-tuple-element.68.refs_0_, ...), custom_call_target="tpu_custom_call" | custom-call | flops 14495514624 | bytes 33030144 | tf_op jit(solution)/shard_map/weight_grad/pallas_call | solution.py:861
  1310.6 72.4 %weight_grad.4 = (f32[1536,3072]{1,0:T(8,128)}, bf16[24,256,1536]{2,1,0:T(8,128)(2,1)}) custom-call(s32[1]{0:T(128)} %bitcast.stage, bf16[6144,1536]{1,0:T(8,128)(2,1)} %bitcast.46, bf16[6144,3072]{1,0:T(8,128)(2,1)} %bitcast.45, bf16[24,256,1536]{2,1,0:T(8,128)(2,1)} %get-tuple-element.57.refs_0_), custom_call_target="tpu_custom_call" | custom-call | flops 57982058496 | bytes 113246208 | tf_op jit(solution)/shard_map/weight_grad/pallas_call | solution.py:861
  1383.0 0.0 collective-permute-done.refs_3_
  1383.0 73.9 %weight_grad.3 = (f32[3072,1536]{1,0:T(8,128)}, bf16[24,256,1536]{2,1,0:T(8,128)(2,1)}) custom-call(s32[1]{0:T(128)} %bitcast.stage, bf16[6144,3072]{1,0:T(8,128)(2,1)} %bitcast.44, bf16[6144,1536]{1,0:T(8,128)(2,1)} %bitcast.47, bf16[24,256,1536]{2,1,0:T(8,128)(2,1)} %get-tuple-element.55.refs_0_, bf16[24,256,1536]{2,1,0:T(8,128)(2,1)} %get-tuple-element.47.mid_all.refs_1_, ...), custom_call_target="tpu_custom_call" | custom-call | flops 57982058496 | bytes 113246208 | tf_op jit(solution)/shard_map/weight_grad/pallas_call | solution.py:861
  (1 shorter events, 0.0 us)
Async XLA Ops:
  1227.1 155.9 %collective-permute-start = (bf16[24,256,1536]{2,1,0:T(8,128)(2,1)}, bf16[24,256,1536]{2,1,0:T(8,128)(2,1)}, u32[]{:S(2)}, u32[]{:S(2)}) collective-permute-start(bf16[24,256,1536]{2,1,0:T(8,128)(2,1)} %get-tuple-element.58.refs_2_), channel_id=1, source_target_pairs={{3,7},{7,3}} | collective-permute-start | bytes 56623112 | tf_op jit(solution)/shard_map/ppermute | solution.py:896
  1234.3 54.5 %copy-start = (f32[1,2304]{1,0:T(1,128)S(1)}, f32[1,2304]{1,0:T(1,128)}, u32[]{:S(2)}) copy-start(f32[1,2304]{1,0:T(1,128)} %get-tuple-element.65) | copy-start | bytes 27652

commit v8 on v7

--- a/solution.py
+++ b/solution.py
@@ -19,7 +19,7 @@
 SOFT_ROWS = 64
 RING = 4
 LANES = 128
-RELAYED = 2
+RELAYED = 3
 
 WINDOWS = ((0, 128, 0), (0, 256, 96), (128, 256, 64), (256, 128, 32))
 
@@ -401,6 +401,13 @@
         @pl.when(m < subs)
         def _():
             attn_part(m)
+
+        @pl.when((m > 0) & (stage == last_stage - 1))
+        def _():
+            finish(m - 1)
+
+        @pl.when(m < subs)
+        def _():
             mlp_part(m)
 
         @pl.when((m >= 1) & (m <= d_model // piece))
@@ -408,7 +415,7 @@
             tb[...] = jnp.transpose(wo[cut(m - 1), :])
             moved(tb, wot_o.at[:, cut(m - 1)])
 
-        @pl.when((m > 0) & (stage < last_stage))
+        @pl.when((m > 0) & (stage < last_stage - 1))
         def _():
             finish(m - 1)
 
@@ -893,7 +900,7 @@
         last_stage = stages - 1
         stage = lax.axis_index("pp").reshape(1)
         held, _ = lax.optimization_barrier((part_all, gin_all))
-        peer_part = lax.ppermute(held, ("tp", "pp"), [(last_stage, stages + last_stage), (stages + last_stage, last_stage)])
+        peer_part = lax.ppermute(held, ("tp", "pp"), [(i, (i + stages) % (2 * stages) if i % stages == last_stage else i) for i in range(2 * stages)])
         g_w_out, dbo, dln, db1, db2 = grad_call(stage, last_stage, flat(o_all), flat(gmid_all), half, d_model, d_model, (dbo, dln, db1, db2), 4)
         g_w_fc1, g_in = grad_call(stage, last_stage, flat(h2_all), flat(dpre_all), d_model, 1024, d_model, (gin_all,), 1)
         g_w_fc2, h_out = grad_call(stage, last_stage, flat(a_all), flat(dy_all), 1024, d_model, d_model, (y_all, mid_all, part_all, peer_part, b_fc2), 1)

time: 1470 us -> 1650 us (1.12)
  starting transfers between devices: 7.17 us -> 143 us
  Pallas kernels: 1390 us -> 1430 us
    ppermute x1, starting transfers between devices: 7.17 us -> 143 us  [stage_program(): lax.ppermute(held, ('tp', 'pp'), [(i, (i + stages) % (2 * stages) if i %...]
    pallas_call x1, Pallas kernels: 636 us -> 684 us  [bwd_call(): pl.pallas_call(functools.partial(bwd_kernel, subs, stages, width, tile),...]
  transfers between devices with their start and end apart: 1 -> 1, of which waited for: 0 -> 0; matrix products, arithmetic and copies ran while one was open for 4% -> 3% of each run, Pallas kernels for 6% -> 6%
where the time goes in v8:
time: 1650 us; the launch traced here: 1630 us
  Pallas kernels  1430 us (87%)
  starting transfers between devices  143 us (9%)
  matrix products  54.5 us (3%)
    pallas_call x1, Pallas kernels, bwd_call(): pl.pallas_call(functools.partial(bwd_kernel, subs, stages, width, tile),...  684 us
    pallas_call x1, Pallas kernels, fwd_call(): pl.pallas_call(functools.partial(fwd_kernel, subs, stages, width, tile),...  576 us
    pallas_call x3, Pallas kernels, grad_call(): pl.pallas_call(functools.partial(grad_kernel, last_stage, len(extras)), n...  167 us
    ppermute x1, starting transfers between devices, stage_program(): lax.ppermute(held, ('tp', 'pp'), [(i, (i + stages) % (2 * stages) if i %...  143 us
    dot_general x1, matrix products, dot_tn(): lax.dot_general(lhs, rhs, (((0,), (0,)), ((), ())), preferred_element_typ...  54.5 us
  transfers between devices with their start and end apart: 1, of which 0 were waited for; matrix products, arithmetic and copies ran while one was open for 3% of the time, Pallas kernels for 6%

profile of v8, /device:TPU:0, one launch (start us, length us, event | category | flops | bytes accessed | tf_op | source)
XLA Modules:
  0.0 1628.6 jit_solution(13309802165151592084)
XLA Ops:
  0.6 1.4 reshape.69.bq
  2.0 576.5 %fwd_stage.1 = (bf16[24,256,1536]{2,1,0:T(8,128)(2,1)}, bf16[24,256,4608]{2,1,0:T(8,128)(2,1)}, bf16[24,256,768]{2,1,0:T(8,128)(2,1)}, bf16[24,256,1536]{2,1,0:T...) custom-call(bf16[24,256,1536]{2,1,0:T(8,128)(2,1)} %bitcast.35, ...), custom_call_target="tpu_custom_call" | custom-call | flops 231928233984 | bytes 320864256 | tf_op jit(solution)/shard_map/fwd_stage/pallas_call | solution.py:764
  578.5 684.0 %bwd_stage.1 = (bf16[24,256,1536]{2,1,0:T(8,128)(2,1)}, bf16[24,256,3072]{2,1,0:T(8,128)(2,1)}, bf16[24,256,1536]{2,1,0:T(8,128)(2,1)}, bf16[24,256,2304]{2,1,0:...) custom-call(bf16[24,256,1536]{2,1,0:T(8,128)(2,1)} %bitcast.36, ...), custom_call_target="tpu_custom_call" | custom-call | flops 231928233984 | bytes 320864256 | tf_op jit(solution)/shard_map/bwd_stage/pallas_call | solution.py:804
  1262.5 143.0 %collective-permute-start = (bf16[24,256,1536]{2,1,0:T(8,128)(2,1)}, bf16[24,256,1536]{2,1,0:T(8,128)(2,1)}, u32[]{:S(2)}, u32[]{:S(2)}) collective-permute-start(bf16[24,256,1536]{2,1,0:T(8,128)(2,1)} %get-tuple-element.58.refs_2_), channel_id=1, source_target_pairs={{0,0},{1,1},{2,2},{3,7},{4,4},{5,5},{6,6},{7,3}} | collective-permute-start | bytes 56623112 | tf_op jit(solution)/shard_map/ppermute | solution.py:903
  1405.6 0.0 copy-start
  1405.6 54.5 %convolution_bitcast_fusion = f32[2304,1536]{1,0:T(8,128)} fusion(bf16[24,256,2304]{2,1,0:T(8,128)(2,1)} %get-tuple-element.63, bf16[24,256,1536]{2,1,0:T(8,128)(2,1)} %get-tuple-element.64), kind=kOutput, calls=%fused_computation | convolution fusion | flops 43486543872 | bytes 61341696 | tf_op jit(solution)/shard_map/dot_general | solution.py:48
  1460.1 0.0 copy-done
  1460.1 0.7 broadcast_in_dim_reshape.6
  1460.8 21.1 %weight_grad.5 = (f32[768,1536]{1,0:T(8,128)}, f32[1,1536]{1,0:T(1,128)}, f32[4,1536]{1,0:T(4,128)}, f32[1,3072]{1,0:T(1,128)}, f32[1,1536]{1,0:T(1,128)}) custom-call(s32[1]{0:T(128)} %bitcast.stage, bf16[6144,768]{1,0:T(8,128)(2,1)} %bitcast.54, bf16[6144,1536]{1,0:T(8,128)(2,1)} %bitcast.50, f32[1,1536]{1,0:T(1,128)} %get-tuple-element.68.refs_0_, ...), custom_call_target="tpu_custom_call" | custom-call | flops 14495514624 | bytes 33030144 | tf_op jit(solution)/shard_map/weight_grad/pallas_call | solution.py:868
  1481.9 72.4 %weight_grad.4 = (f32[1536,3072]{1,0:T(8,128)}, bf16[24,256,1536]{2,1,0:T(8,128)(2,1)}) custom-call(s32[1]{0:T(128)} %bitcast.stage, bf16[6144,1536]{1,0:T(8,128)(2,1)} %bitcast.46, bf16[6144,3072]{1,0:T(8,128)(2,1)} %bitcast.45, bf16[24,256,1536]{2,1,0:T(8,128)(2,1)} %get-tuple-element.57.refs_0_), custom_call_target="tpu_custom_call" | custom-call | flops 57982058496 | bytes 113246208 | tf_op jit(solution)/shard_map/weight_grad/pallas_call | solution.py:868
  1554.3 0.0 collective-permute-done.refs_3_
  1554.3 73.9 %weight_grad.3 = (f32[3072,1536]{1,0:T(8,128)}, bf16[24,256,1536]{2,1,0:T(8,128)(2,1)}) custom-call(s32[1]{0:T(128)} %bitcast.stage, bf16[6144,3072]{1,0:T(8,128)(2,1)} %bitcast.44, bf16[6144,1536]{1,0:T(8,128)(2,1)} %bitcast.47, bf16[24,256,1536]{2,1,0:T(8,128)(2,1)} %get-tuple-element.55.refs_0_, bf16[24,256,1536]{2,1,0:T(8,128)(2,1)} %get-tuple-element.47.mid_all.refs_1_, ...), custom_call_target="tpu_custom_call" | custom-call | flops 57982058496 | bytes 113246208 | tf_op jit(solution)/shard_map/weight_grad/pallas_call | solution.py:868
  (1 shorter events, 0.0 us)
Async XLA Ops:
  1262.5 291.8 %collective-permute-start = (bf16[24,256,1536]{2,1,0:T(8,128)(2,1)}, bf16[24,256,1536]{2,1,0:T(8,128)(2,1)}, u32[]{:S(2)}, u32[]{:S(2)}) collective-permute-start(bf16[24,256,1536]{2,1,0:T(8,128)(2,1)} %get-tuple-element.58.refs_2_), channel_id=1, source_target_pairs={{0,0},{1,1},{2,2},{3,7},{4,4},{5,5},{6,6},{7,3}} | collective-permute-start | bytes 56623112 | tf_op jit(solution)/shard_map/ppermute | solution.py:903
  1405.6 54.5 %copy-start = (f32[1,2304]{1,0:T(1,128)S(1)}, f32[1,2304]{1,0:T(1,128)}, u32[]{:S(2)}) copy-start(f32[1,2304]{1,0:T(1,128)} %get-tuple-element.65) | copy-start | bytes 27652

commit v9 on v7

--- a/solution.py
+++ b/solution.py
@@ -19,7 +19,7 @@
 SOFT_ROWS = 64
 RING = 4
 LANES = 128
-RELAYED = 2
+RELAYED = 3
 
 WINDOWS = ((0, 128, 0), (0, 256, 96), (128, 256, 64), (256, 128, 32))
 

time: 1470 us -> 1450 us (0.986)
  no operation moved by 1% of the time
where the time goes in v9:
time: 1450 us; the launch traced here: 1440 us
  Pallas kernels  1380 us (95%)
  matrix products  54.5 us (4%)
    pallas_call x1, Pallas kernels, bwd_call(): pl.pallas_call(functools.partial(bwd_kernel, subs, stages, width, tile),...  635 us
    pallas_call x1, Pallas kernels, fwd_call(): pl.pallas_call(functools.partial(fwd_kernel, subs, stages, width, tile),...  576 us
    pallas_call x3, Pallas kernels, grad_call(): pl.pallas_call(functools.partial(grad_kernel, last_stage, len(extras)), n...  167 us
    dot_general x1, matrix products, dot_tn(): lax.dot_general(lhs, rhs, (((0,), (0,)), ((), ())), preferred_element_typ...  54.5 us
  transfers between devices with their start and end apart: 1, of which 0 were waited for; matrix products, arithmetic and copies ran while one was open for 4% of the time, Pallas kernels for 6%

profile of v9, /device:TPU:0, one launch (start us, length us, event | category | flops | bytes accessed | tf_op | source)
XLA Modules:
  0.0 1443.8 jit_solution(3577363742080748619)
XLA Ops:
  0.6 1.4 reshape.69.bq
  2.0 576.4 %fwd_stage.1 = (bf16[24,256,1536]{2,1,0:T(8,128)(2,1)}, bf16[24,256,4608]{2,1,0:T(8,128)(2,1)}, bf16[24,256,768]{2,1,0:T(8,128)(2,1)}, bf16[24,256,1536]{2,1,0:T...) custom-call(bf16[24,256,1536]{2,1,0:T(8,128)(2,1)} %bitcast.35, ...), custom_call_target="tpu_custom_call" | custom-call | flops 231928233984 | bytes 320864256 | tf_op jit(solution)/shard_map/fwd_stage/pallas_call | solution.py:757
  578.4 635.2 %bwd_stage.1 = (bf16[24,256,1536]{2,1,0:T(8,128)(2,1)}, bf16[24,256,3072]{2,1,0:T(8,128)(2,1)}, bf16[24,256,1536]{2,1,0:T(8,128)(2,1)}, bf16[24,256,2304]{2,1,0:...) custom-call(bf16[24,256,1536]{2,1,0:T(8,128)(2,1)} %bitcast.36, ...), custom_call_target="tpu_custom_call" | custom-call | flops 231928233984 | bytes 320864256 | tf_op jit(solution)/shard_map/bwd_stage/pallas_call | solution.py:797
  1213.6 7.2 collective-permute-start
  1220.8 0.0 copy-start
  1220.8 54.5 %convolution_bitcast_fusion = f32[2304,1536]{1,0:T(8,128)} fusion(bf16[24,256,2304]{2,1,0:T(8,128)(2,1)} %get-tuple-element.63, bf16[24,256,1536]{2,1,0:T(8,128)(2,1)} %get-tuple-element.64), kind=kOutput, calls=%fused_computation | convolution fusion | flops 43486543872 | bytes 61341696 | tf_op jit(solution)/shard_map/dot_general | solution.py:48
  1275.3 0.0 copy-done
  1275.4 0.7 broadcast_in_dim_reshape.6
  1276.0 21.1 %weight_grad.5 = (f32[768,1536]{1,0:T(8,128)}, f32[1,1536]{1,0:T(1,128)}, f32[4,1536]{1,0:T(4,128)}, f32[1,3072]{1,0:T(1,128)}, f32[1,1536]{1,0:T(1,128)}) custom-call(s32[1]{0:T(128)} %bitcast.stage, bf16[6144,768]{1,0:T(8,128)(2,1)} %bitcast.54, bf16[6144,1536]{1,0:T(8,128)(2,1)} %bitcast.50, f32[1,1536]{1,0:T(1,128)} %get-tuple-element.68.refs_0_, ...), custom_call_target="tpu_custom_call" | custom-call | flops 14495514624 | bytes 33030144 | tf_op jit(solution)/shard_map/weight_grad/pallas_call | solution.py:861
  1297.1 72.4 %weight_grad.4 = (f32[1536,3072]{1,0:T(8,128)}, bf16[24,256,1536]{2,1,0:T(8,128)(2,1)}) custom-call(s32[1]{0:T(128)} %bitcast.stage, bf16[6144,1536]{1,0:T(8,128)(2,1)} %bitcast.46, bf16[6144,3072]{1,0:T(8,128)(2,1)} %bitcast.45, bf16[24,256,1536]{2,1,0:T(8,128)(2,1)} %get-tuple-element.57.refs_0_), custom_call_target="tpu_custom_call" | custom-call | flops 57982058496 | bytes 113246208 | tf_op jit(solution)/shard_map/weight_grad/pallas_call | solution.py:861
  1369.5 0.0 collective-permute-done.refs_3_
  1369.5 73.9 %weight_grad.3 = (f32[3072,1536]{1,0:T(8,128)}, bf16[24,256,1536]{2,1,0:T(8,128)(2,1)}) custom-call(s32[1]{0:T(128)} %bitcast.stage, bf16[6144,3072]{1,0:T(8,128)(2,1)} %bitcast.44, bf16[6144,1536]{1,0:T(8,128)(2,1)} %bitcast.47, bf16[24,256,1536]{2,1,0:T(8,128)(2,1)} %get-tuple-element.55.refs_0_, bf16[24,256,1536]{2,1,0:T(8,128)(2,1)} %get-tuple-element.47.mid_all.refs_1_, ...), custom_call_target="tpu_custom_call" | custom-call | flops 57982058496 | bytes 113246208 | tf_op jit(solution)/shard_map/weight_grad/pallas_call | solution.py:861
  (1 shorter events, 0.0 us)
Async XLA Ops:
  1213.6 155.9 %collective-permute-start = (bf16[24,256,1536]{2,1,0:T(8,128)(2,1)}, bf16[24,256,1536]{2,1,0:T(8,128)(2,1)}, u32[]{:S(2)}, u32[]{:S(2)}) collective-permute-start(bf16[24,256,1536]{2,1,0:T(8,128)(2,1)} %get-tuple-element.58.refs_2_), channel_id=1, source_target_pairs={{3,7},{7,3}} | collective-permute-start | bytes 56623112 | tf_op jit(solution)/shard_map/ppermute | solution.py:896
  1220.8 54.5 %copy-start = (f32[1,2304]{1,0:T(1,128)S(1)}, f32[1,2304]{1,0:T(1,128)}, u32[]{:S(2)}) copy-start(f32[1,2304]{1,0:T(1,128)} %get-tuple-element.65) | copy-start | bytes 27652
